TPU v7x, 1024 devices: a whole 8x8x8 slice. The times are simulated.
1024 devices in a mesh: exp: 64 (over z, x), head: 16 (over y, core).
Axes of the slice: x: 8, y: 8, z: 8, core: 2. Of those that a mesh axis runs over, the one named last changes fastest.
Arguments:
- normed_input: bfloat16 [64, 128, 4096], P('exp', None, 'head'), may hold values from -11 to 11
- norm_gain: float32 [4096], P('head'), may hold values from 0.5 to 1.5
- norm_scale: float32 [64, 128], P('exp'), may hold values from 0.4 to 4
- out_grad: bfloat16 [64, 128, 4096], P('exp', None, 'head'), may hold values from -6 to 6
- router_weight: bfloat16 [4096, 128], P('head'), may hold values from -0.125 to 0.125
- routed_experts: int32 [64, 128, 8], P('exp'), may hold values from 0 to 127, all different within a row; in each aligned block of 128 rows (0 to 127, 128 to 255, ..., all dimensions but the last counted through in order) at most 15 rows name the same one
- expert_grad: bfloat16 [128, 64, 15, 4096], P('exp', None, None, 'head'), may hold values from -10 to 10, as said below
- gate_grad: bfloat16 [128, 64, 15], P('exp'), may hold values from -48 to 48
- out_proj: bfloat16 [8192, 4096], P('head'), may hold values from -0.0625 to 0.0625
- query_states: bfloat16 [64, 128, 8192], P('exp', None, 'head'), may hold values from -5 to 5
- rotated_keys: bfloat16 [64, 128, 512], P('exp'), may hold values from -5 to 5
- value_tensor: bfloat16 [64, 128, 512], P('exp'), may hold values from -6 to 6
Outputs:
- grad_hidden: bfloat16 [64, 128, 4096], P('exp', None, 'head')
- grad_query: bfloat16 [64, 128, 8192], P('exp', 'head')
- key_gradient: bfloat16 [64, 128, 512], P('exp', 'head')
- value_gradient: bfloat16 [64, 128, 512], P('exp', 'head')
Inputs may be any that keep to these rules, and one draw needn't show every extreme that they name: `routed_experts`: each token names 8 different experts. Within one sequence, an aligned block of 128 rows, no expert is named by more than 15 tokens, a bound that some block reaches. `expert_grad`: slot c of expert e for sequence s holds the row of the c-th token of sequence s, in order of position, that names e; slots past that count hold unrelated values. `gate_grad`: same slot layout as expert_grad.
All inputs are finite; a program needn't handle non-finite values.
Results may differ from a plain program's by a relative error of at most 0.01225.
Values may be sent and summed in bfloat16 or wider, within the bound.
No kernel may reach another device: no remote copies, remote signals or barrier semaphores. Data moves between devices by JAX's collectives and lax.ppermute only.
A program may use at most 32 MiB of HBM per device.

v0:
```python
import math

import jax
import jax.numpy as jnp
from jax import lax
from jax.sharding import PartitionSpec as P

QUERY_HEADS = 64
KEY_VALUE_HEADS = 4
HEAD_WIDTH = 128


def in_one_piece(arrays, axis, split_dim, concat_dim, along):
    columns = [a.reshape(*a.shape[:along], -1) for a in arrays]
    both = jnp.concatenate(columns, axis=along)
    filled, at, done = (
        lax.all_to_all(both, axis, split_axis=split_dim, concat_axis=concat_dim, tiled=True),
        0,
        [],
    )
    for a, column in zip(arrays, columns):
        slab = filled[..., at : at + column.shape[along]]
        done.append(slab.reshape(*slab.shape[:along], *a.shape[along:]))
        at += column.shape[along]
    return tuple(done)


def sent_to_all(x, axis):
    copies = jnp.broadcast_to(x, (lax.axis_size(axis), *x.shape))
    return lax.all_to_all(copies, axis, split_axis=0, concat_axis=0, tiled=True)


def taken_together(x, axis):
    return sent_to_all(x, axis).sum(axis=0)


def packed_total(arrays, axis):
    ends = [0]
    for a in arrays:
        ends.append(ends[-1] + a.size)
    total = taken_together(jnp.concatenate([a.ravel() for a in arrays]), axis)
    return tuple((total[b:e].reshape(a.shape) for a, b, e in zip(arrays, ends, ends[1:])))


def laid_out(tiles, dim):
    lengths = list(tiles.shape[1:])
    lengths[dim] *= tiles.shape[0]
    return jnp.moveaxis(tiles, 0, dim).reshape(lengths)


def gathered_copies(x, axis, dim):
    tiles = sent_to_all(x, axis)
    return laid_out(tiles, dim)


def per_device(
    normed_input,
    norm_gain,
    norm_scale,
    out_grad,
    router_weight,
    routed_experts,
    expert_grad,
    gate_grad,
    out_proj,
    query_states,
    rotated_keys,
    value_tensor,
):
    highest = lax.Precision.HIGHEST
    hidden_part = normed_input[0].astype(jnp.float32)
    expert_ids = routed_experts[0]
    seq_len = hidden_part.shape[0]
    experts_all = router_weight.shape[1]
    capacity = expert_grad.shape[2]
    width_total = out_proj.shape[1]
    scaled = hidden_part * norm_gain
    normed_low = scaled.astype(jnp.bfloat16)
    member = expert_ids[:, :, None] == lax.iota(jnp.int32, experts_all)[None, None, :]
    member_f = member.astype(jnp.float32)
    local_logits = jnp.dot(normed_low, router_weight, preferred_element_type=jnp.float32)
    picked_part = jnp.einsum("le,lke->lk", local_logits, member_f, precision=highest)
    returned_rows, returned_gates = in_one_piece((expert_grad, gate_grad), "exp", 1, 0, 3)
    per_token = jnp.sum(member.astype(jnp.int32), axis=1, dtype=jnp.int32)
    before = jnp.cumsum(per_token, axis=0, dtype=jnp.int32) - per_token
    slot_index = jnp.sum(jnp.where(member, before[:, None, :], 0), axis=-1, dtype=jnp.int32)
    flat_index = expert_ids * capacity + slot_index
    slot_rows = jnp.take(returned_rows.reshape(experts_all * capacity, -1), flat_index, axis=0)
    slot_grads = jnp.take(returned_gates.reshape(-1), flat_index).astype(jnp.float32)
    rows_full = slot_rows.astype(jnp.float32)
    weight_full = router_weight.astype(jnp.float32)
    along_rows = jnp.einsum("lkd,ld->lk", rows_full, scaled, precision=highest)
    router_scaled = jnp.dot(scaled, weight_full, precision=highest)
    along_router = jnp.einsum("le,lke->lk", router_scaled, member_f, precision=highest)
    picked, along_rows, along_router = packed_total((picked_part, along_rows, along_router), "head")
    gate_weights = jax.nn.softmax(picked, axis=-1)
    gate_diff = gate_weights * (
        slot_grads - jnp.sum(gate_weights * slot_grads, axis=-1, keepdims=True)
    )
    diff_full = jnp.einsum("lk,lke->le", gate_diff, member_f, precision=highest)
    grad_normed = jnp.einsum("lk,lkd->ld", gate_weights, rows_full, precision=highest)
    grad_normed = grad_normed + jnp.dot(diff_full, weight_full.T, precision=highest)
    inner = jnp.sum(gate_weights * along_rows, axis=-1) + jnp.sum(gate_diff * along_router, axis=-1)
    grad_hidden = out_grad[0].astype(jnp.float32) + norm_scale[0][:, None] * (
        norm_gain * grad_normed - hidden_part * inner[:, None] / width_total
    )
    grad_hidden = grad_hidden.astype(jnp.bfloat16)
    context_grad = lax.dot_general(
        gathered_copies(grad_hidden, "head", 1),
        out_proj,
        (((1,), (1,)), ((), ())),
        preferred_element_type=jnp.float32,
    ).astype(jnp.bfloat16)
    resident_heads = out_proj.shape[0] // HEAD_WIDTH
    key_value_index = lax.axis_index("head") * resident_heads // (QUERY_HEADS // KEY_VALUE_HEADS)
    key_block = lax.dynamic_slice_in_dim(
        rotated_keys[0], key_value_index * HEAD_WIDTH, HEAD_WIDTH, 1
    )
    value_block = lax.dynamic_slice_in_dim(
        value_tensor[0], key_value_index * HEAD_WIDTH, HEAD_WIDTH, 1
    )
    queries = query_states[0].reshape(seq_len, resident_heads, HEAD_WIDTH)
    grads_ctx = context_grad.reshape(seq_len, resident_heads, HEAD_WIDTH)
    inv_sqrt = 1.0 / math.sqrt(HEAD_WIDTH)
    scores = (
        jnp.einsum("qhd,kd->hqk", queries, key_block, preferred_element_type=jnp.float32) * inv_sqrt
    )
    positions = lax.iota(jnp.int32, seq_len)
    causal = positions[:, None] >= positions[None, :]
    scores = jnp.where(causal[None], scores, -jnp.inf)
    attn_probs = jax.nn.softmax(scores, axis=-1)
    probs_low = attn_probs.astype(jnp.bfloat16)
    prob_grads = jnp.einsum(
        "qhd,kd->hqk", grads_ctx, value_block, preferred_element_type=jnp.float32
    )
    row_delta = jnp.sum(attn_probs * prob_grads, axis=-1, keepdims=True)
    score_grads = (attn_probs * (prob_grads - row_delta) * inv_sqrt).astype(jnp.bfloat16)
    grad_query = jnp.einsum(
        "hqk,kd->qhd", score_grads, key_block, preferred_element_type=jnp.float32
    )
    grad_query = grad_query.astype(jnp.bfloat16).reshape(seq_len, resident_heads * HEAD_WIDTH)
    partial_key_sum = jnp.einsum(
        "hqk,qhd->kd", score_grads, queries, preferred_element_type=jnp.float32
    ).astype(jnp.bfloat16)
    partial_value_sum = jnp.einsum(
        "hqk,qhd->kd", probs_low, grads_ctx, preferred_element_type=jnp.float32
    ).astype(jnp.bfloat16)
    query_tokens, received_keys, received_values = (
        lax.all_to_all(grad_query, "head", split_axis=0, concat_axis=1, tiled=True),
        lax.all_to_all(partial_key_sum, "head", split_axis=0, concat_axis=1, tiled=True),
        lax.all_to_all(partial_value_sum, "head", split_axis=0, concat_axis=1, tiled=True),
    )
    resident_tokens = received_keys.shape[0]
    replica_count = lax.axis_size("head") // KEY_VALUE_HEADS
    key_gradient = jnp.sum(
        received_keys.astype(jnp.float32).reshape(
            resident_tokens, KEY_VALUE_HEADS, replica_count, HEAD_WIDTH
        ),
        axis=2,
    )
    value_gradient = jnp.sum(
        received_values.astype(jnp.float32).reshape(
            resident_tokens, KEY_VALUE_HEADS, replica_count, HEAD_WIDTH
        ),
        axis=2,
    )
    key_gradient = key_gradient.astype(jnp.bfloat16).reshape(
        resident_tokens, KEY_VALUE_HEADS * HEAD_WIDTH
    )
    value_gradient = value_gradient.astype(jnp.bfloat16).reshape(
        resident_tokens, KEY_VALUE_HEADS * HEAD_WIDTH
    )
    return (grad_hidden[None], query_tokens[None], key_gradient[None], value_gradient[None])


def solution(mesh):
    placed = (
        P("exp", None, "head"),
        P("head"),
        P("exp", None),
        P("exp", None, "head"),
        P("head", None),
        P("exp", None, None),
        P("exp", None, None, "head"),
        P("exp", None, None),
        P("head", None),
        P("exp", None, "head"),
        P("exp", None, None),
        P("exp", None, None),
    )
    return jax.shard_map(
        per_device,
        mesh=mesh,
        in_specs=placed,
        out_specs=(
            P("exp", None, "head"),
            P("exp", "head", None),
            P("exp", "head", None),
            P("exp", "head", None),
        ),
        check_vma=False,
    )
```

profile of v0, /device:TPU:1, one launch (start us, length us, event | category | flops | bytes accessed | tf_op | source)
XLA Modules:
  0.0 175.3 jit_solution(8855955060754652506)
XLA Ops:
  0.6 1.6 copy.87
  2.3 1.8 %copy.86 = bf16[2,64,15,256]{3,2,0,1:T(8,128)(2,1)S(1)} copy(bf16[2,64,15,256]{3,1,2,0:T(8,128)(2,1)} %param.18) | data formatting | bytes 1966080 | tf_op args[6]
  4.1 1.5 pad_maximum_fusion
  5.6 23.2 %all-to-all-start = ((bf16[2,64,15,257]{3,2,0,1:T(8,128)(2,1)}), bf16[2,64,15,257]{3,2,0,1:T(8,128)(2,1)S(1)}, u32[]{:S(2)}, u32[]{:S(2)}) async-start(bf16[2,64,15,257]{3,2,0,1:T(8,128)(2,1)} %pad_maximum_fusion), calls=%async_computation | async-start | bytes 3145728 | tf_op jit(solution)/shard_map/all_to_all | solution.py:17
  30.2 2.4 %select_reduce_fusion = s32[128,8]{1,0:T(8,128)S(1)} fusion(s32[128,128]{1,0:T(8,128)S(1)} %sub.46, s32[128,8]{1,0:T(8,128)S(1)} %bitcast.149), kind=kLoop, calls=%fused_computation.33 | loop fusion | flops 392192 | bytes 73728 | tf_op jit(solution)/shard_map/reduce_sum | solution.py:86
  33.7 0.7 fusion.36
  34.3 33.5 %all-to-all-done = bf16[2,64,15,257]{3,2,0,1:T(8,128)(2,1)S(1)} async-done(((bf16[2,64,15,257]{3,2,0,1:T(8,128)(2,1)}), bf16[2,64,15,257]{3,2,0,1:T(8,128)(2,1)S(1)}, u32[]{:S(2)}, u32[]{:S(2)}) %all-to-all-start) | async-done | bytes 986912 | tf_op jit(solution)/shard_map/all_to_all | solution.py:17
  67.8 1.1 slice.57
  68.9 1.4 reshape.180
  70.3 3.9 %gather_fusion = bf16[1024,256]{1,0:T(8,128)(2,1)S(1)} fusion(bf16[1920,256]{1,0:T(8,128)(2,1)S(1)} %reshape.180, s32[1024]{0:T(1024)S(1)} %broadcast_clamp_fusion), kind=kCustom, calls=%fused_computation | custom fusion | bytes 1052672 | tf_op jit(solution)/shard_map/jit(_take)/gather | solution.py:88
  74.3 1.6 fusion.29
  76.0 0.8 broadcast_in_dim.70
  76.8 10.8 %all-to-all-start.1 = ((f32[16,1,3072]{2,1,0:T(1,128)}), f32[16,1,3072]{2,1,0:T(1,128)S(1)}, u32[]{:S(2)}, u32[]{:S(2)}) async-start(f32[16,1,3072]{2,1,0:T(1,128)} %broadcast_in_dim.70), calls=%async_computation.1 | async-start | bytes 393216 | tf_op jit(solution)/shard_map/all_to_all | solution.py:30
  88.1 6.8 %gather_fusion.1 = bf16[1024]{0:T(1024)(128)(2,1)S(1)} fusion(bf16[1920]{0:T(1024)(128)(2,1)S(1)} %reshape_reshape.3, s32[1024]{0:T(1024)S(1)} %broadcast_clamp_fusion), kind=kCustom, calls=%fused_computation.1 | custom fusion | bytes 8192 | tf_op jit(solution)/shard_map/jit(_take)/gather | solution.py:89
  95.1 2.7 %all-to-all-done.1 = f32[16,1,3072]{2,1,0:T(1,128)S(1)} async-done(((f32[16,1,3072]{2,1,0:T(1,128)}), f32[16,1,3072]{2,1,0:T(1,128)S(1)}, u32[]{:S(2)}, u32[]{:S(2)}) %all-to-all-start.1) | async-done | bytes 196640 | tf_op jit(solution)/shard_map/all_to_all | solution.py:30
  98.8 0.6 fusion.21
  99.5 0.7 fusion.28
  100.6 1.2 broadcast_in_dim.75
  101.8 4.6 %all-to-all-start.2 = ((bf16[16,128,256]{1,2,0:T(8,128)(2,1)}), bf16[16,128,256]{1,2,0:T(8,128)(2,1)S(1)}, u32[]{:S(2)}, u32[]{:S(2)}) async-start(bf16[16,128,256]{1,2,0:T(8,128)(2,1)} %broadcast_in_dim.75), calls=%async_computation.2 | async-start | bytes 2097152 | tf_op jit(solution)/shard_map/all_to_all | solution.py:30
  106.7 27.6 %all-to-all-done.2 = bf16[16,128,256]{1,2,0:T(8,128)(2,1)S(1)} async-done(((bf16[16,128,256]{1,2,0:T(8,128)(2,1)}), bf16[16,128,256]{1,2,0:T(8,128)(2,1)S(1)}, u32[]{:S(2)}, u32[]{:S(2)}) %all-to-all-start.2) | async-done | bytes 1048608 | tf_op jit(solution)/shard_map/all_to_all | solution.py:30
  134.3 3.7 %fusion.10 = bf16[16,4,8,128]{3,2,1,0:T(8,128)(2,1)S(1)} fusion(bf16[128,4096]{0,1:T(8,128)(2,1)S(1)} %bitcast.146, bf16[512,4096]{1,0:T(8,128)(2,1)} %param.20), kind=kOutput, calls=%fused_computation.17 | convolution fusion | flops 536936448 | bytes 5373952 | tf_op jit(solution)/shard_map/dot_general | solution.py:108
  138.0 0.9 convolution_bitcast_fusion
  139.0 0.8 fusion.20
  139.8 3.4 %all-to-all-start.4 = ((bf16[16,8,128]{2,1,0:T(8,128)(2,1)}), bf16[16,8,128]{2,1,0:T(8,128)(2,1)S(1)}, u32[]{:S(2)}, u32[]{:S(2)}) async-start(bf16[16,8,128]{2,1,0:T(8,128)(2,1)} %fusion.20), calls=%async_computation.4 | async-start | bytes 65536 | tf_op jit(solution)/shard_map/all_to_all | solution.py:150
  143.3 0.8 fusion.19
  144.0 6.6 %all-to-all-done.4 = bf16[16,8,128]{2,1,0:T(8,128)(2,1)S(1)} async-done(((bf16[16,8,128]{2,1,0:T(8,128)(2,1)}), bf16[16,8,128]{2,1,0:T(8,128)(2,1)S(1)}, u32[]{:S(2)}, u32[]{:S(2)}) %all-to-all-start.4) | async-done | bytes 32800 | tf_op jit(solution)/shard_map/all_to_all | solution.py:150
  150.6 3.7 %all-to-all-start.5 = ((bf16[16,8,128]{2,1,0:T(8,128)(2,1)}), bf16[16,8,128]{2,1,0:T(8,128)(2,1)S(1)}, u32[]{:S(2)}, u32[]{:S(2)}) async-start(bf16[16,8,128]{2,1,0:T(8,128)(2,1)} %fusion.19), calls=%async_computation.5 | async-start | bytes 65536 | tf_op jit(solution)/shard_map/all_to_all | solution.py:151
  154.7 0.7 all_to_all.58
  155.4 6.4 %all-to-all-done.5 = bf16[16,8,128]{2,1,0:T(8,128)(2,1)S(1)} async-done(((bf16[16,8,128]{2,1,0:T(8,128)(2,1)}), bf16[16,8,128]{2,1,0:T(8,128)(2,1)S(1)}, u32[]{:S(2)}, u32[]{:S(2)}) %all-to-all-start.5) | async-done | bytes 32800 | tf_op jit(solution)/shard_map/all_to_all | solution.py:151
  161.8 3.7 %all-to-all-start.3 = ((bf16[16,8,512]{2,1,0:T(8,128)(2,1)}), bf16[16,8,512]{2,1,0:T(8,128)(2,1)S(1)}, u32[]{:S(2)}, u32[]{:S(2)}) async-start(bf16[16,8,512]{2,1,0:T(8,128)(2,1)} %all_to_all.58), calls=%async_computation.3 | async-start | bytes 262144 | tf_op jit(solution)/shard_map/all_to_all | solution.py:149
  166.7 8.0 %all-to-all-done.3 = bf16[16,8,512]{2,1,0:T(8,128)(2,1)S(1)} async-done(((bf16[16,8,512]{2,1,0:T(8,128)(2,1)}), bf16[16,8,512]{2,1,0:T(8,128)(2,1)S(1)}, u32[]{:S(2)}, u32[]{:S(2)}) %all-to-all-start.3) | async-done | bytes 131104 | tf_op jit(solution)/shard_map/all_to_all | solution.py:149
  174.7 0.7 copy.145
  (56 shorter events, 6.5 us)
Async XLA Ops:
  0.6 105.8 %copy-start = (bf16[1,128,512]{2,1,0:T(8,128)(2,1)S(1)}, bf16[1,128,512]{2,1,0:T(8,128)(2,1)}, u32[]{:S(2)}) copy-start(bf16[1,128,512]{2,1,0:T(8,128)(2,1)} %param.22) | copy-start | bytes 393220
  4.1 24.7 %copy-start.1 = (bf16[1,128,256]{2,1,0:T(8,128)(2,1)S(1)}, bf16[1,128,256]{2,1,0:T(8,128)(2,1)}, u32[]{:S(2)}) copy-start(bf16[1,128,256]{2,1,0:T(8,128)(2,1)} %param.12) | copy-start | bytes 196612
  4.1 24.7 %copy-start.2 = (bf16[256,128]{1,0:T(8,128)(2,1)S(1)}, bf16[256,128]{1,0:T(8,128)(2,1)}, u32[]{:S(2)}) copy-start(bf16[256,128]{1,0:T(8,128)(2,1)} %param.16) | copy-start | bytes 196612
  4.1 24.7 %copy-start.6 = (f32[256]{0:T(256)S(1)}, f32[256]{0:T(256)}, u32[]{:S(2)}) copy-start(f32[256]{0:T(256)} %param.13) | copy-start | bytes 3076
  4.1 24.9 %copy-start.7 = (s32[1,128,8]{1,2,0:T(8,128)S(1)}, s32[1,128,8]{1,2,0:T(8,128)}, u32[]{:S(2)}) copy-start(s32[1,128,8]{1,2,0:T(8,128)} %param.17) | copy-start | bytes 12292
  5.6 62.2 %all-to-all-start = ((bf16[2,64,15,257]{3,2,0,1:T(8,128)(2,1)}), bf16[2,64,15,257]{3,2,0,1:T(8,128)(2,1)S(1)}, u32[]{:S(2)}, u32[]{:S(2)}) async-start(bf16[2,64,15,257]{3,2,0,1:T(8,128)(2,1)} %pad_maximum_fusion), calls=%async_computation | async-start | bytes 3145728 | tf_op jit(solution)/shard_map/all_to_all | solution.py:17
  76.8 21.0 %all-to-all-start.1 = ((f32[16,1,3072]{2,1,0:T(1,128)}), f32[16,1,3072]{2,1,0:T(1,128)S(1)}, u32[]{:S(2)}, u32[]{:S(2)}) async-start(f32[16,1,3072]{2,1,0:T(1,128)} %broadcast_in_dim.70), calls=%async_computation.1 | async-start | bytes 393216 | tf_op jit(solution)/shard_map/all_to_all | solution.py:30
  94.9 5.2 %copy-start.5 = (bf16[1,128,256]{2,1,0:T(8,128)(2,1)S(1)}, bf16[1,128,256]{2,1,0:T(8,128)(2,1)}, u32[]{:S(2)}) copy-start(bf16[1,128,256]{2,1,0:T(8,128)(2,1)} %param.15) | copy-start | bytes 196612
  95.0 5.2 %copy-start.8 = (f32[1,128]{1,0:T(1,128)S(1)}, f32[1,128]{1,0:T(1,128)}, u32[]{:S(2)}) copy-start(f32[1,128]{1,0:T(1,128)} %param.14) | copy-start | bytes 1540
  98.7 7.7 %copy-start.4 = (bf16[1,128,512]{2,1,0:T(8,128)(2,1)S(1)}, bf16[1,128,512]{2,1,0:T(8,128)(2,1)}, u32[]{:S(2)}) copy-start(bf16[1,128,512]{2,1,0:T(8,128)(2,1)} %param.21) | copy-start | bytes 393220
  100.4 37.6 %copy-start.3 = (bf16[128,256]{1,0:T(8,128)(2,1)}, bf16[128,256]{1,0:T(8,128)(2,1)S(1)}, u32[]{:S(2)}) copy-start(bf16[128,256]{1,0:T(8,128)(2,1)S(1)} %fusion.16) | copy-start | bytes 196612
  101.8 32.5 %all-to-all-start.2 = ((bf16[16,128,256]{1,2,0:T(8,128)(2,1)}), bf16[16,128,256]{1,2,0:T(8,128)(2,1)S(1)}, u32[]{:S(2)}, u32[]{:S(2)}) async-start(bf16[16,128,256]{1,2,0:T(8,128)(2,1)} %broadcast_in_dim.75), calls=%async_computation.2 | async-start | bytes 2097152 | tf_op jit(solution)/shard_map/all_to_all | solution.py:30
  139.8 10.8 %all-to-all-start.4 = ((bf16[16,8,128]{2,1,0:T(8,128)(2,1)}), bf16[16,8,128]{2,1,0:T(8,128)(2,1)S(1)}, u32[]{:S(2)}, u32[]{:S(2)}) async-start(bf16[16,8,128]{2,1,0:T(8,128)(2,1)} %fusion.20), calls=%async_computation.4 | async-start | bytes 65536 | tf_op jit(solution)/shard_map/all_to_all | solution.py:150
  150.6 11.2 %all-to-all-start.5 = ((bf16[16,8,128]{2,1,0:T(8,128)(2,1)}), bf16[16,8,128]{2,1,0:T(8,128)(2,1)S(1)}, u32[]{:S(2)}, u32[]{:S(2)}) async-start(bf16[16,8,128]{2,1,0:T(8,128)(2,1)} %fusion.19), calls=%async_computation.5 | async-start | bytes 65536 | tf_op jit(solution)/shard_map/all_to_all | solution.py:151
  161.8 12.9 %all-to-all-start.3 = ((bf16[16,8,512]{2,1,0:T(8,128)(2,1)}), bf16[16,8,512]{2,1,0:T(8,128)(2,1)S(1)}, u32[]{:S(2)}, u32[]{:S(2)}) async-start(bf16[16,8,512]{2,1,0:T(8,128)(2,1)} %all_to_all.58), calls=%async_computation.3 | async-start | bytes 262144 | tf_op jit(solution)/shard_map/all_to_all | solution.py:149
where the time goes:
time: 176 us; the launch traced here: 175 us
  waiting for transfers between devices  84.8 us (48%)
  starting transfers between devices  49.3 us (28%)
  local copies, waits for them, and re-layouts  21.7 us (12%)
  matrix products  11.5 us (7%)
  other arithmetic  7.01 us (4%)
    all_to_all x1, waiting for transfers between devices, in_one_piece(): lax.all_to_all(both, axis, split_axis=split_dim, concat_axis=concat_dim,...  33.5 us
    all_to_all x2, waiting for transfers between devices, sent_to_all(): return lax.all_to_all(copies, axis, split_axis=0, concat_axis=0, tiled=True)  30.3 us
    all_to_all x1, starting transfers between devices, in_one_piece(): lax.all_to_all(both, axis, split_axis=split_dim, concat_axis=concat_dim,...  23.2 us
    all_to_all x2, starting transfers between devices, sent_to_all(): return lax.all_to_all(copies, axis, split_axis=0, concat_axis=0, tiled=True)  15.3 us
    all_to_all x1, waiting for transfers between devices, per_device(): lax.all_to_all(grad_query, 'head', split_axis=0, concat_axis=1, tiled=True)  7.98 us
    gather x2, local copies, waits for them, and re-layouts, per_device(): jnp.take(returned_gates.reshape(-1), flat_index).astype(jnp.float32)  6.89 us
    all_to_all x1, waiting for transfers between devices, per_device(): lax.all_to_all(partial_key_sum, 'head', split_axis=0, concat_axis=1, tile...  6.61 us
    all_to_all x1, waiting for transfers between devices, per_device(): lax.all_to_all(partial_value_sum, 'head', split_axis=0, concat_axis=1, ti...  6.38 us
  transfers between devices with their start and end apart: 6, of which 6 were waited for; matrix products, arithmetic and copies ran while one was open for 9% of the time, Pallas kernels for 0%

commit v1 on v0

v1 whole, which is shorter than its diff:
```python
import math

import jax
import jax.numpy as jnp
from jax import lax
from jax.experimental import pallas as pl
from jax.experimental.pallas import tpu as pltpu
from jax.sharding import PartitionSpec as P


HEAD_WIDTH = 128
KEY_VALUE_HEADS = 4
TOPK = 8
F32 = jnp.float32
BF16 = jnp.bfloat16
TOKENS = 128
SLOTS = 16
ROWS = 144
TAIL = 136
GRANT = 24 * 2**20


def call(kernel, outs, *args):
    specs = [pl.BlockSpec(memory_space=pltpu.SMEM) if a.dtype == jnp.int32 and a.size == 1
             else pl.BlockSpec(memory_space=pltpu.VMEM) for a in args]
    one = isinstance(outs, jax.ShapeDtypeStruct)
    vm = pl.BlockSpec(memory_space=pltpu.VMEM)
    return pl.pallas_call(
        kernel,
        out_shape=outs,
        in_specs=specs,
        out_specs=vm if one else tuple(vm for _ in outs),
        compiler_params=pltpu.CompilerParams(vmem_limit_bytes=GRANT),
    )(*args)


def shape(s, d=F32):
    return jax.ShapeDtypeStruct(s, d)


def nn(a, b):
    return lax.dot_general(a, b, (((1,), (0,)), ((), ())), preferred_element_type=F32)


def nt(a, b):
    return lax.dot_general(a, b, (((1,), (1,)), ((), ())), preferred_element_type=F32)


def high_low(v):
    high = v.astype(BF16)
    return high, (v - high.astype(F32)).astype(BF16)


def three(v):
    a = v.astype(BF16)
    rest = v - a.astype(F32)
    b = rest.astype(BF16)
    return a, b, (rest - b.astype(F32)).astype(BF16)


def logits_kernel(x, gain, router, ids, sent):
    xv = x[...]
    scaled = xv.astype(F32) * gain[...]
    logits = nn(scaled.astype(BF16), router[...]).T
    experts = lax.broadcasted_iota(jnp.int32, logits.shape, 0)
    rows = []
    for k in range(TOPK):
        rows.append(jnp.sum(jnp.where(ids[k : k + 1, :] == experts, logits, 0.0), axis=0, keepdims=True))
    a, b, c = three(jnp.concatenate(rows, axis=0))
    sent[0:TOKENS, :] = xv
    sent[TOKENS : TOKENS + 8, 0:128] = a
    sent[TOKENS : TOKENS + 8, 128:256] = b
    sent[TOKENS + 8 : ROWS, 0:128] = c
    sent[TOKENS + 8 : ROWS, 128:256] = jnp.zeros_like(c)


def picks_kernel(own, total_out):
    total = jnp.zeros((8, 128), F32)
    for i in range(own.shape[0]):
        top = own[i, TOKENS : TOKENS + 8, :].astype(F32)
        low = own[i, TOKENS + 8 : ROWS, 0:128].astype(F32)
        total = total + ((top[:, 0:128] + top[:, 128:256]) + low)
    total_out[...] = total


def weights_kernel(own, other, ids, mix, dense, rank):
    total = own[...] + other[...]
    top = jnp.max(total, axis=0, keepdims=True)
    e = jnp.exp(total - top)
    gates = e / jnp.sum(e, axis=0, keepdims=True)
    n = dense.shape[0]
    experts = lax.broadcasted_iota(jnp.int32, (n, TOKENS), 0)
    weight = jnp.zeros((n, TOKENS), F32)
    member = jnp.zeros((n, TOKENS), F32)
    for k in range(TOPK):
        hit = ids[k : k + 1, :] == experts
        weight = jnp.where(hit, gates[k : k + 1, :], weight)
        member = jnp.where(hit, 1.0, member)
    t_from = lax.broadcasted_iota(jnp.int32, (TOKENS, TOKENS), 0)
    t_to = lax.broadcasted_iota(jnp.int32, (TOKENS, TOKENS), 1)
    earlier = jnp.where(t_from < t_to, 1.0, 0.0).astype(BF16)
    before = nn(member.astype(BF16), earlier)
    dense[...] = weight
    rank[...] = before
    step = 8
    for g in range(n // step):
        w3 = weight[g * step : (g + 1) * step, :][:, None, :]
        b3 = before[g * step : (g + 1) * step, :][:, None, :]
        slot = lax.broadcasted_iota(jnp.int32, (step, SLOTS, TOKENS), 1).astype(F32)
        block = jnp.where(jnp.broadcast_to(b3, slot.shape) == slot, jnp.broadcast_to(w3, slot.shape), 0.0)
        block = block.reshape(step * SLOTS, TOKENS).T
        mix[:, g * step * SLOTS : (g + 1) * step * SLOTS] = block.astype(BF16)


def rows_kernel(received, mix, dense, rank, router, x, gain, scale, out_grad, sent, full):
    n = dense.shape[0]
    rows = received[...]
    both = nn(mix[...], rows)
    e_of = lax.broadcasted_iota(jnp.int32, (n, n * SLOTS), 0)
    j_of = lax.broadcasted_iota(jnp.int32, (n, n * SLOTS), 1)
    pick = jnp.where(j_of == e_of * SLOTS + (SLOTS - 1), 1.0, 0.0).astype(BF16)
    table = nn(pick, received[:, 0:128])
    ranks = rank[...]
    slot_grads = jnp.zeros((n, TOKENS), F32)
    for c in range(SLOTS - 1):
        slot_grads = jnp.where(ranks == float(c), table[:, c : c + 1], slot_grads)
    weight = dense[...]
    mean = jnp.sum(weight * slot_grads, axis=0, keepdims=True)
    diff = (weight * (slot_grads - mean)).T
    d_high, d_low = high_low(diff)
    routed = nt(d_high, router[...]) + nt(d_low, router[...])
    grad = both + routed
    inner_terms = x[...].astype(F32) * gain[...] * grad
    i_high, i_mid, i_low = three(inner_terms)
    ones = jnp.ones((8, 256), BF16)
    inner = (nt(ones, i_high) + nt(ones, i_mid)) + nt(ones, i_low)
    s = jnp.broadcast_to(scale[...], (TOKENS, TOKENS)).T
    moved = out_grad[...].astype(F32) + jnp.concatenate([s, s], axis=1) * (gain[...] * grad)
    full[...] = moved
    low = moved.astype(BF16)
    a, b, c = three(inner)
    row = lax.broadcasted_iota(jnp.int32, (8, 256), 0)
    first = jnp.concatenate([a.astype(F32), b.astype(F32)], axis=1)
    second = jnp.concatenate([c.astype(F32), jnp.zeros((8, 128), F32)], axis=1)
    extra = jnp.where(row == 0, first, jnp.where(row == 1, second, 0.0)).astype(BF16)
    for i in range(sent.shape[0]):
        sent[i, 0:TOKENS, :] = low
        sent[i, TOKENS:TAIL, :] = extra


def contract(part, proj, core):
    total = None
    for i in range(part.shape[0]):
        at = pl.multiple_of(i * 512 + core * 256, 256)
        term = nt(part[i, 0:TOKENS, :], proj[:, pl.ds(at, 256)])
        total = term if total is None else total + term
    return total


def half_kernel(place, own, proj, out):
    out[...] = contract(own, proj, place[0] % 2)


def early_kernel(place, own, other, proj, queries, keys, hidden_ctx, probs):
    core = place[0] % 2
    hidden_ctx[...] = contract(own, proj, core) + contract(other, proj, 1 - core)
    inv_sqrt = 1.0 / math.sqrt(HEAD_WIDTH)
    kv = pl.multiple_of(place[0] // KEY_VALUE_HEADS * HEAD_WIDTH, HEAD_WIDTH)
    key = keys[:, pl.ds(kv, HEAD_WIDTH)]
    at_key = lax.broadcasted_iota(jnp.int32, (TOKENS, TOKENS), 0)
    at_query = lax.broadcasted_iota(jnp.int32, (TOKENS, TOKENS), 1)
    for h in range(probs.shape[0]):
        scores = nt(key, queries[:, h * 128 : (h + 1) * 128]) * inv_sqrt
        scores = jnp.where(at_key <= at_query, scores, -jnp.inf)
        e = jnp.exp(scores - jnp.max(scores, axis=0, keepdims=True))
        probs[h] = e / jnp.sum(e, axis=0, keepdims=True)


def attention_kernel(place, own, other, half, proj, queries, keys, values, hidden_ctx, probs, scale, width, sent, shift):
    core = place[0] % 2
    row = jnp.zeros((1, 128), F32)
    for part in (own, other):
        for i in range(part.shape[0]):
            tail = part[i, TOKENS:TAIL, :].astype(F32)
            row = row + ((tail[0:1, 0:128] + tail[0:1, 128:256]) + tail[1:2, 0:128])
    column = jnp.broadcast_to(row * scale[...] / width[0].astype(F32), (TOKENS, TOKENS)).T
    shift[...] = column
    inv_sqrt = 1.0 / math.sqrt(HEAD_WIDTH)
    kv = pl.multiple_of(place[0] // KEY_VALUE_HEADS * HEAD_WIDTH, HEAD_WIDTH)
    key = keys[:, pl.ds(kv, HEAD_WIDTH)]
    value = values[:, pl.ds(kv, HEAD_WIDTH)]
    ctx = half[...] + contract(other, proj, 1 - core)
    n = probs.shape[0]
    key_sum = jnp.zeros((TOKENS, HEAD_WIDTH), F32)
    value_sum = jnp.zeros((TOKENS, HEAD_WIDTH), F32)
    for h in range(n):
        cols = slice(h * 128, (h + 1) * 128)
        grads = (ctx[:, cols] - column * hidden_ctx[:, cols]).astype(BF16)
        p = probs[h]
        prob_grads = nt(value, grads)
        delta = jnp.sum(p * prob_grads, axis=0, keepdims=True)
        score_grads = p * (prob_grads - delta) * inv_sqrt
        low = score_grads.astype(BF16)
        sent[:, cols] = nn(score_grads.T.astype(BF16), key).astype(BF16)
        key_sum = key_sum + nn(low, queries[:, cols])
        value_sum = value_sum + nn(p.astype(BF16), grads)
    sent[:, n * 128 : n * 128 + 128] = key_sum.astype(BF16)
    sent[:, n * 128 + 128 : n * 128 + 256] = value_sum.astype(BF16)


def hidden_kernel(full, x, shift, out):
    s = shift[...]
    out[...] = (full[...] - x[...].astype(F32) * jnp.concatenate([s, s], axis=1)).astype(BF16)


def collect_kernel(received, query_out, key_out, value_out):
    n = received.shape[0]
    heads = received.shape[2] - 256
    for i in range(n):
        query_out[:, i * heads : (i + 1) * heads] = received[i, :, 0:heads]
    group = n // KEY_VALUE_HEADS
    for g in range(KEY_VALUE_HEADS):
        for out, at in ((key_out, heads), (value_out, heads + 128)):
            parts = [received[g * group + r, :, at : at + 128].astype(F32) for r in range(group)]
            total = parts[0]
            for part in parts[1:]:
                total = total + part
            out[:, g * 128 : (g + 1) * 128] = total.astype(BF16)


def per_device(
    normed_input,
    norm_gain,
    norm_scale,
    out_grad,
    router_weight,
    routed_experts,
    expert_grad,
    gate_grad,
    out_proj,
    query_states,
    rotated_keys,
    value_tensor,
):
    held, sequences, capacity, columns = expert_grad.shape
    n_head = lax.axis_size("head")
    n_experts = router_weight.shape[1]
    cores = [[2 * i + c for i in range(n_head // 2)] for c in range(2)]
    swap = [(i, i ^ 1) for i in range(n_head)]
    place = lax.axis_index("head").reshape(1)
    x, ids = normed_input[0], routed_experts[0].T
    gain = norm_gain.reshape(1, columns)
    width = jnp.full((1,), out_proj.shape[1], jnp.int32)

    local = out_proj.shape[0]
    gates = jnp.pad(gate_grad.transpose(1, 0, 2)[:, :, None, :], ((0, 0), (0, 0), (0, 0), (0, columns - capacity)))
    packed = jnp.concatenate([expert_grad.transpose(1, 0, 2, 3), gates], axis=2)
    packed = packed.reshape(sequences, held * SLOTS, columns)
    received = lax.all_to_all(packed, "exp", split_axis=0, concat_axis=0, tiled=True)
    received = received.reshape(n_experts * SLOTS, columns)
    early = call(logits_kernel, shape((ROWS, columns), BF16), x, gain, router_weight, ids)
    early_own = lax.all_gather(early, "head", axis_index_groups=cores)
    picks = call(picks_kernel, shape((8, 128)), early_own)
    picks_other = lax.ppermute(picks, "head", swap)
    mix, dense, rank = call(
        weights_kernel,
        (shape((TOKENS, n_experts * SLOTS), BF16), shape((n_experts, TOKENS)), shape((n_experts, TOKENS))),
        picks, picks_other, ids,
    )
    late, full = call(
        rows_kernel,
        (shape((n_head // 2, TAIL, columns), BF16), shape((TOKENS, columns))),
        received, mix, dense, rank, router_weight, x, gain, norm_scale, out_grad[0],
    )
    late_own = lax.all_to_all(late, "head", split_axis=0, concat_axis=0, tiled=True, axis_index_groups=cores)
    early_other = lax.ppermute(early_own, "head", swap)
    hidden_ctx, probs = call(
        early_kernel,
        (shape((TOKENS, local)), shape((local // HEAD_WIDTH, TOKENS, TOKENS))),
        place, early_own, early_other, out_proj, query_states[0], rotated_keys[0],
    )
    late_other = lax.ppermute(late_own, "head", swap)
    half = call(half_kernel, shape((TOKENS, local)), place, late_own, out_proj)
    grads, shift = call(
        attention_kernel,
        (shape((TOKENS, local + 256), BF16), shape((TOKENS, TOKENS))),
        place, late_own, late_other, half, out_proj, query_states[0], rotated_keys[0], value_tensor[0],
        hidden_ctx, probs, norm_scale, width,
    )
    grad_hidden = call(hidden_kernel, shape((TOKENS, columns), BF16), full, x, shift)
    tokens = TOKENS // n_head
    returned = lax.all_to_all(
        grads.reshape(n_head, tokens, local + 256), "head", split_axis=0, concat_axis=0, tiled=True
    )
    query_out, key_out, value_out = call(
        collect_kernel,
        (shape((tokens, n_head * local), BF16), shape((tokens, 512), BF16), shape((tokens, 512), BF16)),
        returned,
    )
    return (grad_hidden[None], query_out[None], key_out[None], value_out[None])


def solution(mesh):
    placed = (
        P("exp", None, "head"),
        P("head"),
        P("exp", None),
        P("exp", None, "head"),
        P("head", None),
        P("exp", None, None),
        P("exp", None, None, "head"),
        P("exp", None, None),
        P("head", None),
        P("exp", None, "head"),
        P("exp", None, None),
        P("exp", None, None),
    )
    return jax.shard_map(
        per_device,
        mesh=mesh,
        in_specs=placed,
        out_specs=(
            P("exp", None, "head"),
            P("exp", "head", None),
            P("exp", "head", None),
            P("exp", "head", None),
        ),
        check_vma=False,
    )
```

time: 176 us -> 111 us (0.63)
  waiting for transfers between devices: 84.8 us -> 26.3 us
  blocking collectives: 0 us -> 23.7 us
  local copies, waits for them, and re-layouts: 21.7 us -> 5.21 us
  matrix products: 11.5 us -> 0 us
  Pallas kernels: 0 us -> 9.39 us
  other arithmetic: 7.01 us -> 1.3 us
  starting transfers between devices: 49.3 us -> 43.9 us
    all_to_all x6 -> x3, waiting for transfers between devices: 84.8 us -> 25.5 us  [the longest x1 16 us: per_device(): lax.all_to_all(late, 'head', split_axis=0, concat_axis=0, tiled=True, axi...]
    all_gather x0 -> x1, blocking collectives: none -> 23.7 us  [per_device(): early_own = lax.all_gather(early, 'head', axis_index_groups=cores)]
    all_to_all x6 -> x3, starting transfers between devices: 49.3 us -> 31.6 us  [the longest x1 23.3 us: per_device(): lax.all_to_all(packed, 'exp', split_axis=0, concat_axis=0, tiled=True)]
    ppermute x0 -> x3, starting transfers between devices: none -> 12.3 us  [the longest x1 7.19 us: per_device(): picks_other = lax.ppermute(picks, 'head', swap)]
    dot_general x13 -> x0, matrix products: 11.2 us -> none  [the longest x1 3.7 us: per_device(): lax.dot_general(gathered_copies(grad_hidden, 'head', 1), out_proj, (((1,)...]
    gather x3 -> x0, local copies, waits for them, and re-layouts: 10.8 us -> none  [the longest x2 6.89 us: per_device(): jnp.take(returned_gates.reshape(-1), flat_index).astype(jnp.float32)]
    pallas_call x0 -> x9, Pallas kernels: none -> 9.39 us  [call(): pl.pallas_call(kernel, out_shape=outs, in_specs=specs, out_specs=vm if on...]
    reduce_sum x8 -> x0, other arithmetic: 4.51 us -> none  [the longest x1 2.39 us: per_device(): jnp.sum(jnp.where(member, before[:, None, :], 0), axis=-1, dtype=jnp.int32)]
  transfers between devices with their start and end apart: 6 -> 6, of which waited for: 6 -> 3; matrix products, arithmetic and copies ran while one was open for 9% -> 0% of each run, Pallas kernels for 0% -> 3%
where the time goes in v1:
time: 111 us
  starting transfers between devices  43.9 us (40%)
  waiting for transfers between devices  26.3 us (24%)
  blocking collectives  23.7 us (21%)
  Pallas kernels  9.39 us (8%)
  local copies, waits for them, and re-layouts  5.21 us (5%)
  other arithmetic  1.3 us (1%)
    all_gather x1, blocking collectives, per_device(): early_own = lax.all_gather(early, 'head', axis_index_groups=cores)  23.7 us
    all_to_all x1, starting transfers between devices, per_device(): lax.all_to_all(packed, 'exp', split_axis=0, concat_axis=0, tiled=True)  23.3 us
    all_to_all x1, waiting for transfers between devices, per_device(): lax.all_to_all(late, 'head', split_axis=0, concat_axis=0, tiled=True, axi...  16 us
    all_to_all x1, waiting for transfers between devices, per_device(): lax.all_to_all(grads.reshape(n_head, tokens, local + 256), 'head', split_...  9.51 us
    pallas_call x9, Pallas kernels, call(): pl.pallas_call(kernel, out_shape=outs, in_specs=specs, out_specs=vm if on...  9.39 us
    ppermute x1, starting transfers between devices, per_device(): picks_other = lax.ppermute(picks, 'head', swap)  7.19 us
    all_to_all x1, starting transfers between devices, per_device(): lax.all_to_all(late, 'head', split_axis=0, concat_axis=0, tiled=True, axi...  4.95 us
    unnamed x23, local copies, waits for them, and re-layouts  3.64 us
  transfers between devices with their start and end apart: 6, of which 3 were waited for; matrix products, arithmetic and copies ran while one was open for 0% of the time, Pallas kernels for 3%

profile of v1, /device:TPU:1, one launch (start us, length us, event | category | flops | bytes accessed | tf_op | source)
XLA Modules:
  0.0 110.7 jit_solution(15280711620310602073)
XLA Ops:
  0.6 0.8 copy.18
  1.4 1.3 %fusion.1 = bf16[64,2,16,256]{3,0,2,1:T(8,128)(2,1)S(1)} fusion(bf16[64,2,1,15]{3,0,2,1:T(8,128)(2,1)S(1)} %copy.18, bf16[64,2,15,256]{3,0,2,1:T(8,128)(2,1)} %bitcast.40), kind=kLoop, calls=%fused_computation.2 | loop fusion | flops 3145728 | bytes 2035456 | tf_op jit(solution)/shard_map/concatenate | solution.py:257
  2.7 0.0 copy-start.2
  2.8 0.0 copy-start.5
  2.8 0.0 copy-start.8
  2.8 0.0 copy-start.9
  2.8 1.6 %copy.17 = bf16[64,32,256]{2,1,0:T(8,128)(2,1)} copy(bf16[64,32,256]{2,0,1:T(8,128)(2,1)S(1)} %bitcast.39) | data formatting | bytes 2097152 | tf_op jit(solution)/shard_map/reshape | solution.py:258
  4.4 23.3 %all-to-all-start = ((bf16[64,32,256]{2,1,0:T(8,128)(2,1)}), bf16[64,32,256]{2,1,0:T(8,128)(2,1)S(1)}, u32[]{:S(2)}, u32[]{:S(2)}) async-start(bf16[64,32,256]{2,1,0:T(8,128)(2,1)} %copy.17), calls=%async_computation | async-start | bytes 2097152 | tf_op jit(solution)/shard_map/all_to_all | solution.py:259
  27.7 0.3 shard_map.147
  28.0 0.0 copy-start.3
  28.0 0.0 copy-start.4
  28.0 23.7 %all-gather = bf16[1152,256]{1,0:T(8,128)(2,1)S(1)} all-gather(bf16[144,256]{1,0:T(8,128)(2,1)S(1)} %shard_map.147), channel_id=2, replica_groups={{0,2,4,6,8,10,12,14},{1,3,5,7,9,11,13,15},{16,18,20,22,24,26,28,30},{17..., dimensions={0}, use_global_device_ids=true | all-gather | bytes 663552 | tf_op jit(solution)/shard_map/all_gather | solution.py:262
  51.8 7.2 %collective-permute-start = (f32[8,128]{1,0:T(8,128)S(1)}, f32[8,128]{1,0:T(8,128)S(1)}, u32[]{:S(2)}, u32[]{:S(2)}) collective-permute-start(f32[8,128]{1,0:T(8,128)S(1)} %shard_map.148.own), channel_id=1, source_target_pairs={{0,1},{1,0},{2,3},{3,2},{4,5},{5,4},{6,7},{7,6},{8,9},{9,8},{10,11... | collective-permute-start | bytes 12296 | tf_op jit(solution)/shard_map/ppermute | solution.py:264
  59.0 0.8 collective-permute-done.other
  59.8 0.4 shard_map.149
  60.2 0.0 all-to-all-done
  60.2 2.4 %shard_map.150 = (bf16[8,136,256]{2,1,0:T(8,128)(2,1)}, f32[128,256]{1,0:T(8,128)S(1)}) custom-call(bf16[2048,256]{1,0:T(8,128)(2,1)S(1)} %bitcast.25, bf16[128,2048]{1,0:T(8,128)(2,1)S(1)} %get-tuple-element.16.mix, f32[128,128]{1,0:T(8,128)S(1)} %get-tuple-element.17.dense, f32[128,128]{1,0:T(8,128)S(1)} %get-tuple-element.18.rank, ...), custom_call_target="tpu_custom_call" | custom-call | tf_op jit(solution)/shard_map/pallas_call | solution.py:28
  62.6 4.9 %all-to-all-start.1 = ((bf16[8,136,256]{2,1,0:T(8,128)(2,1)}), bf16[8,136,256]{2,1,0:T(8,128)(2,1)S(1)}, u32[]{:S(2)}, u32[]{:S(2)}) async-start(bf16[8,136,256]{2,1,0:T(8,128)(2,1)} %get-tuple-element.20), calls=%async_computation.1 | async-start | bytes 1114112 | tf_op jit(solution)/shard_map/all_to_all | solution.py:275
  67.5 2.7 %collective-permute-start.2 = (bf16[8,144,256]{2,1,0:T(8,128)(2,1)S(1)}, bf16[8,144,256]{2,1,0:T(8,128)(2,1)S(1)}, u32[]{:S(2)}, u32[]{:S(2)}) collective-permute-start(bf16[8,144,256]{2,1,0:T(8,128)(2,1)S(1)} %bitcast.23), channel_id=1, source_target_pairs={{0,1},{1,0},{2,3},{3,2},{4,5},{5,4},{6,7},{7,6},{8,9},{9,8},{10,11... | collective-permute-start | bytes 1769480 | tf_op jit(solution)/shard_map/ppermute | solution.py:276
  70.2 16.0 %all-to-all-done.1.own = bf16[8,136,256]{2,1,0:T(8,128)(2,1)S(1)} async-done(((bf16[8,136,256]{2,1,0:T(8,128)(2,1)}), bf16[8,136,256]{2,1,0:T(8,128)(2,1)S(1)}, u32[]{:S(2)}, u32[]{:S(2)}) %all-to-all-start.1) | async-done | bytes 557088 | tf_op jit(solution)/shard_map/all_to_all | solution.py:275
  86.2 2.4 %collective-permute-start.1 = (bf16[8,136,256]{2,1,0:T(8,128)(2,1)S(1)}, bf16[8,136,256]{2,1,0:T(8,128)(2,1)S(1)}, u32[]{:S(2)}, u32[]{:S(2)}) collective-permute-start(bf16[8,136,256]{2,1,0:T(8,128)(2,1)S(1)} %all-to-all-done.1.own), channel_id=1, source_target_pairs={{0,1},{1,0},{2,3},{3,2},{4,5},{5,4},{6,7},{7,6},{8,9},{9,8},{10,11... | collective-permute-start | bytes 1671176 | tf_op jit(solution)/shard_map/ppermute | solution.py:282
  88.6 0.0 copy-start
  88.6 2.2 %copy-done = bf16[512,4096]{1,0:T(8,128)(2,1)S(1)} copy-done((bf16[512,4096]{1,0:T(8,128)(2,1)S(1)}, bf16[512,4096]{1,0:T(8,128)(2,1)}, u32[]{:S(2)}) %copy-start) | copy-done | bytes 4194328
  90.8 1.6 %shard_map.152 = (f32[128,512]{1,0:T(8,128)S(1)}, f32[4,128,128]{2,1,0:T(8,128)S(1)}) custom-call(s32[1]{0:T(128)} %bitcast.11.place, bf16[8,144,256]{2,1,0:T(8,128)(2,1)S(1)} %bitcast.24, bf16[8,144,256]{2,1,0:T(8,128)(2,1)S(1)} %collective-permute-done.2.other, bf16[512,4096]{1,0:T(8,128)(2,1)S(1)} %copy-done, bf16[128,512]{1,0:T(8,128)(2,1)S(1)} %bitcast.29, ...), custom_call_target="tpu_custom_call" | custom-call | tf_op jit(solution)/shard_map/pallas_call | solution.py:28
  92.5 0.5 copy-done.1
  93.0 0.8 shard_map.151.half
  93.8 0.1 copy-done.6
  93.9 2.5 %shard_map.153 = (bf16[128,768]{1,0:T(8,128)(2,1)}, f32[128,128]{1,0:T(8,128)S(1)}) custom-call(s32[1]{0:T(128)} %bitcast.11.place, bf16[8,136,256]{2,1,0:T(8,128)(2,1)S(1)} %all-to-all-done.1.own, bf16[8,136,256]{2,1,0:T(8,128)(2,1)S(1)} %collective-permute-done.1.other, f32[128,512]{1,0:T(8,128)S(1)} %shard_map.151.half, bf16[512,4096]{1,0:T(8,128)(2,1)S(1)} %copy-done.1, ...), custom_call_target="tpu_custom_call" | custom-call | tf_op jit(solution)/shard_map/pallas_call | solution.py:28
  96.4 3.4 %all-to-all-start.2 = ((bf16[16,8,768]{2,1,0:T(8,128)(2,1)}), bf16[16,8,768]{2,1,0:T(8,128)(2,1)S(1)}, u32[]{:S(2)}, u32[]{:S(2)}) async-start(bf16[16,8,768]{2,1,0:T(8,128)(2,1)} %bitcast.16), calls=%async_computation.2 | async-start | bytes 393216 | tf_op jit(solution)/shard_map/all_to_all | solution.py:292
  99.9 0.7 shard_map.154
  100.5 9.5 %all-to-all-done.2.received = bf16[16,8,768]{2,1,0:T(8,128)(2,1)S(1)} async-done(((bf16[16,8,768]{2,1,0:T(8,128)(2,1)}), bf16[16,8,768]{2,1,0:T(8,128)(2,1)S(1)}, u32[]{:S(2)}, u32[]{:S(2)}) %all-to-all-start.2) | async-done | bytes 196640 | tf_op jit(solution)/shard_map/all_to_all | solution.py:292
  110.0 0.7 shard_map.155
  (15 shorter events, 0.0 us)
Async XLA Ops:
  2.7 24.9 %copy-start.2 = (bf16[1,128,256]{2,1,0:T(8,128)(2,1)S(1)}, bf16[1,128,256]{2,1,0:T(8,128)(2,1)}, u32[]{:S(2)}) copy-start(bf16[1,128,256]{2,1,0:T(8,128)(2,1)} %param.12) | copy-start | bytes 196612
  2.8 24.9 %copy-start.5 = (bf16[256,128]{1,0:T(8,128)(2,1)S(1)}, bf16[256,128]{1,0:T(8,128)(2,1)}, u32[]{:S(2)}) copy-start(bf16[256,128]{1,0:T(8,128)(2,1)} %router.3) | copy-start | bytes 196612
  2.8 24.9 %copy-start.8 = (s32[1,128,8]{1,2,0:T(8,128)S(1)}, s32[1,128,8]{1,2,0:T(8,128)}, u32[]{:S(2)}) copy-start(s32[1,128,8]{1,2,0:T(8,128)} %param.17) | copy-start | bytes 12292
  2.8 24.9 %copy-start.9 = (f32[256]{0:T(256)S(1)}, f32[256]{0:T(256)}, u32[]{:S(2)}) copy-start(f32[256]{0:T(256)} %param.13) | copy-start | bytes 3076
  4.4 55.8 %copy-start.7 = (bf16[1,128,256]{2,1,0:T(8,128)(2,1)S(1)}, bf16[1,128,256]{2,1,0:T(8,128)(2,1)}, u32[]{:S(2)}) copy-start(bf16[1,128,256]{2,1,0:T(8,128)(2,1)} %param.15) | copy-start | bytes 196612
  4.4 55.8 %copy-start.10 = (f32[1,128]{1,0:T(1,128)S(1)}, f32[1,128]{1,0:T(1,128)}, u32[]{:S(2)}) copy-start(f32[1,128]{1,0:T(1,128)} %scale.3) | copy-start | bytes 1540
  4.4 55.8 %all-to-all-start = ((bf16[64,32,256]{2,1,0:T(8,128)(2,1)}), bf16[64,32,256]{2,1,0:T(8,128)(2,1)S(1)}, u32[]{:S(2)}, u32[]{:S(2)}) async-start(bf16[64,32,256]{2,1,0:T(8,128)(2,1)} %copy.17), calls=%async_computation | async-start | bytes 2097152 | tf_op jit(solution)/shard_map/all_to_all | solution.py:259
  28.0 60.6 %copy-start.3 = (bf16[1,128,512]{2,1,0:T(8,128)(2,1)S(1)}, bf16[1,128,512]{2,1,0:T(8,128)(2,1)}, u32[]{:S(2)}) copy-start(bf16[1,128,512]{2,1,0:T(8,128)(2,1)} %param.21) | copy-start | bytes 393220
  28.0 60.6 %copy-start.4 = (bf16[1,128,512]{2,1,0:T(8,128)(2,1)S(1)}, bf16[1,128,512]{2,1,0:T(8,128)(2,1)}, u32[]{:S(2)}) copy-start(bf16[1,128,512]{2,1,0:T(8,128)(2,1)} %param.22) | copy-start | bytes 393220
  51.8 8.0 %collective-permute-start = (f32[8,128]{1,0:T(8,128)S(1)}, f32[8,128]{1,0:T(8,128)S(1)}, u32[]{:S(2)}, u32[]{:S(2)}) collective-permute-start(f32[8,128]{1,0:T(8,128)S(1)} %shard_map.148.own), channel_id=1, source_target_pairs={{0,1},{1,0},{2,3},{3,2},{4,5},{5,4},{6,7},{7,6},{8,9},{9,8},{10,11... | collective-permute-start | bytes 12296 | tf_op jit(solution)/shard_map/ppermute | solution.py:264
  62.6 23.6 %all-to-all-start.1 = ((bf16[8,136,256]{2,1,0:T(8,128)(2,1)}), bf16[8,136,256]{2,1,0:T(8,128)(2,1)S(1)}, u32[]{:S(2)}, u32[]{:S(2)}) async-start(bf16[8,136,256]{2,1,0:T(8,128)(2,1)} %get-tuple-element.20), calls=%async_computation.1 | async-start | bytes 1114112 | tf_op jit(solution)/shard_map/all_to_all | solution.py:275
  67.5 21.1 %collective-permute-start.2 = (bf16[8,144,256]{2,1,0:T(8,128)(2,1)S(1)}, bf16[8,144,256]{2,1,0:T(8,128)(2,1)S(1)}, u32[]{:S(2)}, u32[]{:S(2)}) collective-permute-start(bf16[8,144,256]{2,1,0:T(8,128)(2,1)S(1)} %bitcast.23), channel_id=1, source_target_pairs={{0,1},{1,0},{2,3},{3,2},{4,5},{5,4},{6,7},{7,6},{8,9},{9,8},{10,11... | collective-permute-start | bytes 1769480 | tf_op jit(solution)/shard_map/ppermute | solution.py:276
  86.2 7.6 %collective-permute-start.1 = (bf16[8,136,256]{2,1,0:T(8,128)(2,1)S(1)}, bf16[8,136,256]{2,1,0:T(8,128)(2,1)S(1)}, u32[]{:S(2)}, u32[]{:S(2)}) collective-permute-start(bf16[8,136,256]{2,1,0:T(8,128)(2,1)S(1)} %all-to-all-done.1.own), channel_id=1, source_target_pairs={{0,1},{1,0},{2,3},{3,2},{4,5},{5,4},{6,7},{7,6},{8,9},{9,8},{10,11... | collective-permute-start | bytes 1671176 | tf_op jit(solution)/shard_map/ppermute | solution.py:282
  88.6 2.2 %copy-start = (bf16[512,4096]{1,0:T(8,128)(2,1)S(1)}, bf16[512,4096]{1,0:T(8,128)(2,1)}, u32[]{:S(2)}) copy-start(bf16[512,4096]{1,0:T(8,128)(2,1)} %proj.5) | copy-start | bytes 12582916
  90.8 2.2 %copy-start.1 = (bf16[512,4096]{1,0:T(8,128)(2,1)S(1)}, bf16[512,4096]{1,0:T(8,128)(2,1)}, u32[]{:S(2)}) copy-start(bf16[512,4096]{1,0:T(8,128)(2,1)} %proj.5) | copy-start | bytes 12582916
  93.0 0.9 copy-start.6
  96.4 13.6 %all-to-all-start.2 = ((bf16[16,8,768]{2,1,0:T(8,128)(2,1)}), bf16[16,8,768]{2,1,0:T(8,128)(2,1)S(1)}, u32[]{:S(2)}, u32[]{:S(2)}) async-start(bf16[16,8,768]{2,1,0:T(8,128)(2,1)} %bitcast.16), calls=%async_computation.2 | async-start | bytes 393216 | tf_op jit(solution)/shard_map/all_to_all | solution.py:292

commit v2 on v1

v2 whole, which is shorter than its diff:
```python
import math

import jax
import jax.numpy as jnp
from jax import lax
from jax.experimental import pallas as pl
from jax.experimental.pallas import tpu as pltpu
from jax.sharding import PartitionSpec as P


HEAD_WIDTH = 128
KEY_VALUE_HEADS = 4
TOPK = 8
F32 = jnp.float32
BF16 = jnp.bfloat16
TOKENS = 128
SLOTS = 16
MAIN = 112
LEFT = TOKENS - MAIN
ROWS = MAIN + 8
GRANT = 24 * 2**20


def call(kernel, outs, *args, far=(), far_out=False, scratch=()):
    specs = [
        pl.BlockSpec(
            memory_space=pltpu.SMEM if a.dtype == jnp.int32 and a.size == 1 else pltpu.HBM if i in far else pltpu.VMEM
        )
        for i, a in enumerate(args)
    ]
    args = [pltpu.with_memory_space_constraint(a, pltpu.HBM) if i in far else a for i, a in enumerate(args)]
    one = isinstance(outs, jax.ShapeDtypeStruct)
    vm, hbm = pl.BlockSpec(memory_space=pltpu.VMEM), pl.BlockSpec(memory_space=pltpu.HBM)
    return pl.pallas_call(
        kernel,
        out_shape=outs,
        in_specs=specs,
        out_specs=vm if one else tuple(hbm if far_out else vm for _ in outs),
        scratch_shapes=scratch,
        compiler_params=pltpu.CompilerParams(vmem_limit_bytes=GRANT),
    )(*args)


def shape(s, d=F32):
    return jax.ShapeDtypeStruct(s, d)


def nn(a, b):
    return lax.dot_general(a, b, (((1,), (0,)), ((), ())), preferred_element_type=F32)


def nt(a, b):
    return lax.dot_general(a, b, (((1,), (1,)), ((), ())), preferred_element_type=F32)


def high_low(v):
    high = v.astype(BF16)
    return high, (v - high.astype(F32)).astype(BF16)


def three(v):
    a = v.astype(BF16)
    rest = v - a.astype(F32)
    b = rest.astype(BF16)
    return a, b, (rest - b.astype(F32)).astype(BF16)


def pack_kernel(rows, gates, out, table):
    held, capacity, chunk, columns = rows.shape

    @pl.when(pl.program_id(0) == 0)
    def _():
        flat = gates[...].astype(F32)
        n = flat.shape[2]
        for e in range(held):
            wide = jnp.concatenate([flat[:, e, :], jnp.zeros((capacity, 128 - n), F32)], axis=1)
            table[e] = jnp.concatenate([wide, jnp.zeros((128 - capacity, 128), F32)], axis=0).T[0:n]

    at = pl.multiple_of(pl.program_id(0) * chunk, chunk)
    for e in range(held):
        for lane in range(0, columns, 128):
            last = table[e, pl.ds(at, chunk), :] if lane == 0 else jnp.zeros((chunk, 128), F32)
            block = jnp.concatenate([rows[e, :, :, lane : lane + 128].astype(F32), last[None]], axis=0)
            out[:, e * SLOTS : (e + 1) * SLOTS, lane : lane + 128] = jnp.swapaxes(block, 0, 1).astype(BF16)


def pack(expert_grad, gate_grad):
    held, n, capacity, columns = expert_grad.shape
    chunk = min(n, 16)
    run = pl.pallas_call(
        pack_kernel,
        grid=(n // chunk,),
        in_specs=[
            pl.BlockSpec((held, capacity, chunk, columns), lambda i: (0, 0, i, 0)),
            pl.BlockSpec((capacity, held, n), lambda i: (0, 0, 0)),
        ],
        out_specs=pl.BlockSpec((chunk, held * SLOTS, columns), lambda i: (i, 0, 0)),
        out_shape=shape((n, held * SLOTS, columns), BF16),
        scratch_shapes=[pltpu.VMEM((held, n, 128), F32)],
        name="pack",
        compiler_params=pltpu.CompilerParams(vmem_limit_bytes=GRANT),
    )
    stay = lambda a: pltpu.with_memory_space_constraint(a, pltpu.HBM)
    return run(stay(expert_grad.transpose(0, 2, 1, 3)), stay(gate_grad.transpose(2, 0, 1)))


def logits_kernel(x, gain, router, ids, sent):
    xv = x[...]
    scaled = xv.astype(F32) * gain[...]
    logits = nn(scaled.astype(BF16), router[...]).T
    experts = lax.broadcasted_iota(jnp.int32, logits.shape, 0)
    rows = []
    for k in range(TOPK):
        rows.append(jnp.sum(jnp.where(ids[k : k + 1, :] == experts, logits, 0.0), axis=0, keepdims=True))
    a, b = high_low(jnp.concatenate(rows, axis=0))
    sent[0:MAIN, :] = xv[0:MAIN]
    sent[MAIN:ROWS, 0:128] = a
    sent[MAIN:ROWS, 128:256] = b


def spread(gates, ids):
    n = gates.shape[1]
    experts = lax.broadcasted_iota(jnp.int32, (n, TOKENS), 0)
    weight = jnp.zeros((n, TOKENS), F32)
    member = jnp.zeros((n, TOKENS), F32)
    for k in range(TOPK):
        hit = ids[k : k + 1, :] == experts
        weight = jnp.where(hit, gates[k : k + 1, :], weight)
        member = jnp.where(hit, 1.0, member)
    t_from = lax.broadcasted_iota(jnp.int32, (TOKENS, TOKENS), 0)
    t_to = lax.broadcasted_iota(jnp.int32, (TOKENS, TOKENS), 1)
    earlier = jnp.where(t_from < t_to, 1.0, 0.0).astype(BF16)
    return weight, nn(member.astype(BF16), earlier)


def weights_kernel(gathered, ids, mix, gates_out):
    total = jnp.zeros((8, 128), F32)
    for i in range(gathered.shape[0]):
        both = gathered[i, MAIN:ROWS, :].astype(F32)
        total = total + (both[:, 0:128] + both[:, 128:256])
    top = jnp.max(total, axis=0, keepdims=True)
    e = jnp.exp(total - top)
    gates = e / jnp.sum(e, axis=0, keepdims=True)
    gates_out[...] = gates
    weight, before = spread(gates, ids)
    step = 8
    for g in range(weight.shape[0] // step):
        w3 = weight[g * step : (g + 1) * step, :][:, None, :]
        b3 = before[g * step : (g + 1) * step, :][:, None, :]
        slot = lax.broadcasted_iota(jnp.int32, (step, SLOTS, TOKENS), 1).astype(F32)
        block = jnp.where(jnp.broadcast_to(b3, slot.shape) == slot, jnp.broadcast_to(w3, slot.shape), 0.0)
        block = block.reshape(step * SLOTS, TOKENS).T
        mix[:, g * step * SLOTS : (g + 1) * step * SLOTS] = block.astype(BF16)


def rows_kernel(received, mix, gates, ids, router, x, gain, scale, out_grad, sent_out, rest_out, full_out, sent, rest, full, done):
    weight, ranks = spread(gates[...], ids)
    n = weight.shape[0]
    rows = received[...]
    both = nn(mix[...], rows)
    e_of = lax.broadcasted_iota(jnp.int32, (n, n * SLOTS), 0)
    j_of = lax.broadcasted_iota(jnp.int32, (n, n * SLOTS), 1)
    pick = jnp.where(j_of == e_of * SLOTS + (SLOTS - 1), 1.0, 0.0).astype(BF16)
    table = nn(pick, received[:, 0:128])
    slot_grads = jnp.zeros((n, TOKENS), F32)
    for c in range(SLOTS - 1):
        slot_grads = jnp.where(ranks == float(c), table[:, c : c + 1], slot_grads)
    mean = jnp.sum(weight * slot_grads, axis=0, keepdims=True)
    diff = (weight * (slot_grads - mean)).T
    d_high, d_low = high_low(diff)
    routed = nt(d_high, router[...]) + nt(d_low, router[...])
    grad = both + routed
    s = jnp.broadcast_to(scale[...], (TOKENS, TOKENS)).T
    moved = out_grad[...].astype(F32) + jnp.concatenate([s, s], axis=1) * (gain[...] * grad)
    low = moved.astype(BF16)
    full[...] = moved
    sent[0:MAIN, :] = low[0:MAIN]
    rest[0:LEFT, :] = low[MAIN:TOKENS]
    rest[LEFT : 2 * LEFT, :] = x[MAIN:TOKENS, :]
    n_head = rest_out.shape[0]
    copies = [pltpu.make_async_copy(rest, rest_out.at[i], done.at[i]) for i in range(n_head)]
    copies.append(pltpu.make_async_copy(full, full_out, done.at[n_head]))
    copies.append(pltpu.make_async_copy(sent.at[0:MAIN], sent_out.at[0:MAIN], done.at[n_head + 1]))
    for copy in copies:
        copy.start()
    inner_terms = x[...].astype(F32) * gain[...] * grad
    i_high, i_mid, i_low = three(inner_terms)
    ones = jnp.ones((8, 256), BF16)
    inner = (nt(ones, i_high) + nt(ones, i_mid)) + nt(ones, i_low)
    a, b, c = three(inner)
    row = lax.broadcasted_iota(jnp.int32, (8, 256), 0)
    first = jnp.concatenate([a.astype(F32), b.astype(F32)], axis=1)
    second = jnp.concatenate([c.astype(F32), jnp.zeros((8, 128), F32)], axis=1)
    extra = jnp.where(row == 0, first, jnp.where(row == 1, second, 0.0)).astype(BF16)
    sent[MAIN:ROWS, :] = extra
    copies.append(pltpu.make_async_copy(sent.at[MAIN:ROWS], sent_out.at[MAIN:ROWS], done.at[n_head + 2]))
    copies[-1].start()
    for copy in copies:
        copy.wait()


def contract(rows_of, n, copies, held):
    total = None
    for i in range(n):
        copies[i].wait()
        term = nt(rows_of(i), held[i])
        total = term if total is None else total + term
    return total


def pieces(proj, held, done):
    n = held.shape[0]
    copies = [pltpu.make_async_copy(proj.at[:, i * 256 : (i + 1) * 256], held.at[i], done.at[i]) for i in range(n)]
    for copy in copies:
        copy.start()
    return copies


def early_kernel(place, gathered, proj, queries, keys, hidden_ctx, probs, held, done):
    copies = pieces(proj, held, done)
    hidden_ctx[...] = contract(lambda i: gathered[i, 0:MAIN, :], gathered.shape[0], copies, held)
    inv_sqrt = 1.0 / math.sqrt(HEAD_WIDTH)
    kv = pl.multiple_of(place[0] // KEY_VALUE_HEADS * HEAD_WIDTH, HEAD_WIDTH)
    key = keys[:, pl.ds(kv, HEAD_WIDTH)]
    at_key = lax.broadcasted_iota(jnp.int32, (TOKENS, TOKENS), 0)
    at_query = lax.broadcasted_iota(jnp.int32, (TOKENS, TOKENS), 1)
    for h in range(probs.shape[0]):
        scores = nt(key, queries[:, h * 128 : (h + 1) * 128]) * inv_sqrt
        scores = jnp.where(at_key <= at_query, scores, -jnp.inf)
        e = jnp.exp(scores - jnp.max(scores, axis=0, keepdims=True))
        probs[h] = e / jnp.sum(e, axis=0, keepdims=True)


def attention_kernel(place, gathered, rest, proj, queries, keys, values, hidden_ctx, probs, scale, width, sent, shift, held, done, value_held):
    copies = pieces(proj, held, done)
    kv = pl.multiple_of(place[0] // KEY_VALUE_HEADS * HEAD_WIDTH, HEAD_WIDTH)
    fetch = pltpu.make_async_copy(values.at[:, pl.ds(kv, HEAD_WIDTH)], value_held, done.at[held.shape[0]])
    fetch.start()
    row = jnp.zeros((1, 128), F32)
    for i in range(gathered.shape[0]):
        tail = gathered[i, MAIN:ROWS, :].astype(F32)
        row = row + ((tail[0:1, 0:128] + tail[0:1, 128:256]) + tail[1:2, 0:128])
    column = jnp.broadcast_to(row * scale[...] / width[0].astype(F32), (TOKENS, TOKENS)).T
    shift[...] = column
    inv_sqrt = 1.0 / math.sqrt(HEAD_WIDTH)
    key = keys[:, pl.ds(kv, HEAD_WIDTH)]
    stacked = contract(
        lambda i: jnp.concatenate([gathered[i, 0:MAIN, :], rest[i]], axis=0), gathered.shape[0], copies, held
    )
    ctx = stacked[0:TOKENS]
    hidden = jnp.concatenate([hidden_ctx[...], stacked[TOKENS:]], axis=0)
    fetch.wait()
    value = value_held[...]
    n = probs.shape[0]
    key_sum = jnp.zeros((TOKENS, HEAD_WIDTH), F32)
    value_sum = jnp.zeros((TOKENS, HEAD_WIDTH), F32)
    for h in range(n):
        cols = slice(h * 128, (h + 1) * 128)
        grads = (ctx[:, cols] - column * hidden[:, cols]).astype(BF16)
        p = probs[h]
        prob_grads = nt(value, grads)
        delta = jnp.sum(p * prob_grads, axis=0, keepdims=True)
        score_grads = p * (prob_grads - delta) * inv_sqrt
        low = score_grads.astype(BF16)
        sent[:, cols] = nn(score_grads.T.astype(BF16), key).astype(BF16)
        key_sum = key_sum + nn(low, queries[:, cols])
        value_sum = value_sum + nn(p.astype(BF16), grads)
    sent[:, n * 128 : n * 128 + 128] = key_sum.astype(BF16)
    sent[:, n * 128 + 128 : n * 128 + 256] = value_sum.astype(BF16)


def hidden_kernel(full, x, shift, out):
    s = shift[...]
    out[...] = (full[...] - x[...].astype(F32) * jnp.concatenate([s, s], axis=1)).astype(BF16)


def collect_kernel(received, query_out, key_out, value_out):
    n = received.shape[0]
    heads = received.shape[2] - 256
    for i in range(n):
        query_out[:, i * heads : (i + 1) * heads] = received[i, :, 0:heads]
    group = n // KEY_VALUE_HEADS
    for g in range(KEY_VALUE_HEADS):
        for out, at in ((key_out, heads), (value_out, heads + 128)):
            parts = [received[g * group + r, :, at : at + 128].astype(F32) for r in range(group)]
            total = parts[0]
            for part in parts[1:]:
                total = total + part
            out[:, g * 128 : (g + 1) * 128] = total.astype(BF16)


def per_device(
    normed_input,
    norm_gain,
    norm_scale,
    out_grad,
    router_weight,
    routed_experts,
    expert_grad,
    gate_grad,
    out_proj,
    query_states,
    rotated_keys,
    value_tensor,
):
    _, _, _, columns = expert_grad.shape
    n_head = lax.axis_size("head")
    n_experts = router_weight.shape[1]
    place = lax.axis_index("head").reshape(1)
    x, ids = normed_input[0], routed_experts[0].T
    gain = norm_gain.reshape(1, columns)
    width = jnp.full((1,), out_proj.shape[1], jnp.int32)

    local = out_proj.shape[0]
    held_pieces = (pltpu.VMEM((n_head, local, columns), BF16), pltpu.SemaphoreType.DMA((n_head + 1,)))
    packed = pack(expert_grad, gate_grad)
    received = lax.all_to_all(packed, "exp", split_axis=0, concat_axis=0, tiled=True)
    received = received.reshape(n_experts * SLOTS, columns)
    early = call(logits_kernel, shape((ROWS, columns), BF16), x, gain, router_weight, ids)
    early = lax.all_gather(early, "head")
    mix, gate_weights = call(
        weights_kernel, (shape((TOKENS, n_experts * SLOTS), BF16), shape((TOPK, TOKENS))),
        early, ids,
    )
    hidden_ctx, probs = call(
        early_kernel,
        (shape((MAIN, local)), shape((local // HEAD_WIDTH, TOKENS, TOKENS))),
        place, early, out_proj, query_states[0], rotated_keys[0],
        far=(2,), scratch=held_pieces,
    )
    late, rest, full = call(
        rows_kernel,
        (pltpu.HBM((ROWS, columns), BF16), pltpu.HBM((n_head, 2 * LEFT, columns), BF16), pltpu.HBM((TOKENS, columns), F32)),
        received, mix, gate_weights, ids, router_weight, x, gain, norm_scale, out_grad[0],
        far_out=True,
        scratch=(
            pltpu.VMEM((ROWS, columns), BF16), pltpu.VMEM((2 * LEFT, columns), BF16),
            pltpu.VMEM((TOKENS, columns), F32), pltpu.SemaphoreType.DMA((n_head + 3,)),
        ),
    )
    rest = lax.all_to_all(rest, "head", split_axis=0, concat_axis=0, tiled=True)
    late = lax.all_gather(late, "head")
    grads, shift = call(
        attention_kernel,
        (shape((TOKENS, local + 256), BF16), shape((TOKENS, TOKENS))),
        place, late, rest, out_proj, query_states[0], rotated_keys[0], value_tensor[0],
        hidden_ctx, probs, norm_scale, width,
        far=(3, 6), scratch=held_pieces + (pltpu.VMEM((TOKENS, HEAD_WIDTH), BF16),),
    )
    grad_hidden = call(hidden_kernel, shape((TOKENS, columns), BF16), full, x, shift)
    tokens = TOKENS // n_head
    returned = lax.all_to_all(
        grads.reshape(n_head, tokens, local + 256), "head", split_axis=0, concat_axis=0, tiled=True
    )
    query_out, key_out, value_out = call(
        collect_kernel,
        (shape((tokens, n_head * local), BF16), shape((tokens, 512), BF16), shape((tokens, 512), BF16)),
        returned,
    )
    return (grad_hidden[None], query_out[None], key_out[None], value_out[None])


def solution(mesh):
    placed = (
        P("exp", None, "head"),
        P("head"),
        P("exp", None),
        P("exp", None, "head"),
        P("head", None),
        P("exp", None, None),
        P("exp", None, None, "head"),
        P("exp", None, None),
        P("head", None),
        P("exp", None, "head"),
        P("exp", None, None),
        P("exp", None, None),
    )
    return jax.shard_map(
        per_device,
        mesh=mesh,
        in_specs=placed,
        out_specs=(
            P("exp", None, "head"),
            P("exp", "head", None),
            P("exp", "head", None),
            P("exp", "head", None),
        ),
        check_vma=False,
    )
```

time: 111 us -> 114 us (1.027)
  blocking collectives: 23.7 us -> 42 us
  waiting for transfers between devices: 26.3 us -> 11.4 us
  Pallas kernels: 9.39 us -> 16.3 us
  starting transfers between devices: 43.9 us -> 40.1 us
  local copies, waits for them, and re-layouts: 5.21 us -> 3.09 us
  other arithmetic: 1.3 us -> 0 us
    all_gather x1 -> x2, blocking collectives: 23.7 us -> 42 us  [the longest x1 21.9 us: per_device(): early = lax.all_gather(early, 'head')]
    all_to_all x1, waiting for transfers between devices: 16 us -> 0.01 us  [per_device(): rest = lax.all_to_all(rest, 'head', split_axis=0, concat_axis=0, tiled=True)]
    ppermute x3 -> x0, starting transfers between devices: 12.3 us -> none  [the longest x1 7.19 us: per_device(): picks_other = lax.ppermute(picks, 'head', swap)]
    all_to_all x1, starting transfers between devices: 4.95 us -> 10.9 us  [per_device(): rest = lax.all_to_all(rest, 'head', split_axis=0, concat_axis=0, tiled=True)]
    pallas_call x0 -> x1, Pallas kernels: none -> 3.87 us  [pack(): run(stay(expert_grad.transpose(0, 2, 1, 3)), stay(gate_grad.transpose(2,...]
    pallas_call x9 -> x7, Pallas kernels: 9.39 us -> 12.5 us  [call(): pl.pallas_call(kernel, out_shape=outs, in_specs=specs, out_specs=vm if on...]
    all_to_all x1, starting transfers between devices: 3.42 us -> 5.99 us  [per_device(): lax.all_to_all(grads.reshape(n_head, tokens, local + 256), 'head', split_...]
    all_to_all x1, waiting for transfers between devices: 0.01 us -> 1.85 us  [per_device(): lax.all_to_all(packed, 'exp', split_axis=0, concat_axis=0, tiled=True)]
  transfers between devices with their start and end apart: 6 -> 3, of which waited for: 3 -> 2; matrix products, arithmetic and copies ran while one was open for 0% -> 0% of each run, Pallas kernels for 3% -> 4%
where the time goes in v2:
time: 114 us
  blocking collectives  42 us (37%)
  starting transfers between devices  40.1 us (35%)
  Pallas kernels  16.3 us (14%)
  waiting for transfers between devices  11.4 us (10%)
  local copies, waits for them, and re-layouts  3.09 us (3%)
    all_to_all x1, starting transfers between devices, per_device(): lax.all_to_all(packed, 'exp', split_axis=0, concat_axis=0, tiled=True)  23.1 us
    all_gather x1, blocking collectives, per_device(): early = lax.all_gather(early, 'head')  21.9 us
    all_gather x1, blocking collectives, per_device(): late = lax.all_gather(late, 'head')  20.1 us
    pallas_call x7, Pallas kernels, call(): pl.pallas_call(kernel, out_shape=outs, in_specs=specs, out_specs=vm if on...  12.5 us
    all_to_all x1, starting transfers between devices, per_device(): rest = lax.all_to_all(rest, 'head', split_axis=0, concat_axis=0, tiled=True)  10.9 us
    all_to_all x1, waiting for transfers between devices, per_device(): lax.all_to_all(grads.reshape(n_head, tokens, local + 256), 'head', split_...  9.54 us
    all_to_all x1, starting transfers between devices, per_device(): lax.all_to_all(grads.reshape(n_head, tokens, local + 256), 'head', split_...  5.99 us
    pallas_call x1, Pallas kernels, pack(): run(stay(expert_grad.transpose(0, 2, 1, 3)), stay(gate_grad.transpose(2,...  3.87 us
  transfers between devices with their start and end apart: 3, of which 2 were waited for; matrix products, arithmetic and copies ran while one was open for 0% of the time, Pallas kernels for 4%

profile of v2, /device:TPU:1, one launch (start us, length us, event | category | flops | bytes accessed | tf_op | source)
XLA Modules:
  0.0 113.7 jit_solution(2651123700953982561)
XLA Ops:
  0.6 0.0 copy-start.1
  0.6 0.0 copy-start.11
  0.7 0.0 copy-start.5
  0.7 0.0 copy-start.9
  0.7 0.0 copy-start.12
  0.7 0.0 copy-start.7
  0.7 0.0 copy-start.2
  0.7 0.0 copy-start.3
  0.7 3.9 %pack.1 = bf16[64,32,256]{2,1,0:T(8,128)(2,1)} custom-call(bf16[2,15,64,256]{3,2,1,0:T(8,128)(2,1)} %bitcast.37, bf16[15,2,64]{2,1,0:T(2,128)(2,1)} %bitcast.40), custom_call_target="tpu_custom_call" | custom-call | tf_op jit(solution)/shard_map/pack/pallas_call | solution.py:104
  4.6 23.1 %all-to-all-start = ((bf16[64,32,256]{2,1,0:T(8,128)(2,1)}), bf16[64,32,256]{2,1,0:T(8,128)(2,1)S(1)}, u32[]{:S(2)}, u32[]{:S(2)}) async-start(bf16[64,32,256]{2,1,0:T(8,128)(2,1)} %pack.1), calls=%async_computation | async-start | bytes 2097152 | tf_op jit(solution)/shard_map/all_to_all | solution.py:317
  27.7 0.0 copy-start
  27.8 0.8 copy-done
  28.6 0.8 copy-done.4
  29.4 0.7 copy-done.8
  30.1 0.7 copy-done.10
  30.8 0.3 shard_map.147
  31.1 21.9 %all-gather = bf16[1920,256]{1,0:T(8,128)(2,1)S(1)} all-gather(bf16[120,256]{1,0:T(8,128)(2,1)S(1)} %shard_map.147), channel_id=2, replica_groups=mesh['exp'=64,'head'=16] {'head'}, dimensions={0}, use_global_device_ids=true | all-gather | bytes 1044480 | tf_op jit(solution)/shard_map/all_gather | solution.py:320
  53.0 0.4 shard_map.148
  53.4 1.9 %all-to-all-done = bf16[64,32,256]{2,1,0:T(8,128)(2,1)S(1)} async-done(((bf16[64,32,256]{2,1,0:T(8,128)(2,1)}), bf16[64,32,256]{2,1,0:T(8,128)(2,1)S(1)}, u32[]{:S(2)}, u32[]{:S(2)}) %all-to-all-start) | async-done | bytes 1048608 | tf_op jit(solution)/shard_map/all_to_all | solution.py:317
  55.2 0.0 copy-done.1
  55.3 2.4 %shard_map.149 = (bf16[120,256]{1,0:T(8,128)(2,1)}, bf16[16,32,256]{2,1,0:T(8,128)(2,1)}, f32[128,256]{1,0:T(8,128)}) custom-call(bf16[2048,256]{1,0:T(8,128)(2,1)S(1)} %bitcast.22, bf16[128,2048]{1,0:T(8,128)(2,1)S(1)} %get-tuple-element.16.mix, f32[8,128]{1,0:T(8,128)S(1)} %get-tuple-element.17.gates, s32[8,128]{1,0:T(8,128)S(1)} %bitcast.34, ...), custom_call_target="tpu_custom_call" | custom-call | tf_op jit(solution)/shard_map/pallas_call | solution.py:34
  57.7 0.0 copy-start.13
  57.7 10.9 %all-to-all-start.1 = ((bf16[16,32,256]{2,1,0:T(8,128)(2,1)}), bf16[16,32,256]{2,1,0:T(8,128)(2,1)S(1)}, u32[]{:S(2)}, u32[]{:S(2)}) async-start(bf16[16,32,256]{2,1,0:T(8,128)(2,1)} %get-tuple-element.20), calls=%async_computation.1 | async-start | bytes 524288 | tf_op jit(solution)/shard_map/all_to_all | solution.py:341
  68.7 3.1 %shard_map.150 = (f32[112,512]{1,0:T(8,128)S(1)}, f32[4,128,128]{2,1,0:T(8,128)S(1)}) custom-call(s32[1]{0:T(128)} %bitcast.9.place, bf16[16,120,256]{2,1,0:T(8,128)(2,1)S(1)} %bitcast.21, bf16[512,4096]{1,0:T(8,128)(2,1)} %proj.3, bf16[128,512]{1,0:T(8,128)(2,1)S(1)} %bitcast.27, bf16[128,512]{1,0:T(8,128)(2,1)S(1)} %bitcast.29), custom_call_target="tpu_custom_call" | custom-call | tf_op jit(solution)/shard_map/pallas_call | solution.py:34
  71.8 0.0 copy-start.6
  71.8 20.1 %all-gather.1 = bf16[1920,256]{1,0:T(8,128)(2,1)S(1)} all-gather(bf16[120,256]{1,0:T(8,128)(2,1)S(1)} %copy-done.13), channel_id=3, replica_groups=mesh['exp'=64,'head'=16] {'head'}, dimensions={0}, use_global_device_ids=true | all-gather | bytes 1044480 | tf_op jit(solution)/shard_map/all_gather | solution.py:342
  92.0 0.0 all-to-all-done.1.rest
  92.0 4.9 %shard_map.151 = (bf16[128,768]{1,0:T(8,128)(2,1)}, f32[128,128]{1,0:T(8,128)S(1)}) custom-call(s32[1]{0:T(128)} %bitcast.9.place, bf16[16,120,256]{2,1,0:T(8,128)(2,1)S(1)} %bitcast.23, bf16[16,32,256]{2,1,0:T(8,128)(2,1)S(1)} %all-to-all-done.1.rest, bf16[512,4096]{1,0:T(8,128)(2,1)} %proj.3, bf16[128,512]{1,0:T(8,128)(2,1)S(1)} %bitcast.28, ...), custom_call_target="tpu_custom_call" | custom-call | tf_op jit(solution)/shard_map/pallas_call | solution.py:34
  96.9 6.0 %all-to-all-start.2 = ((bf16[16,8,768]{2,1,0:T(8,128)(2,1)}), bf16[16,8,768]{2,1,0:T(8,128)(2,1)S(1)}, u32[]{:S(2)}, u32[]{:S(2)}) async-start(bf16[16,8,768]{2,1,0:T(8,128)(2,1)} %bitcast.15), calls=%async_computation.2 | async-start | bytes 393216 | tf_op jit(solution)/shard_map/all_to_all | solution.py:352
  102.9 0.7 shard_map.152
  103.5 9.5 %all-to-all-done.2.received = bf16[16,8,768]{2,1,0:T(8,128)(2,1)S(1)} async-done(((bf16[16,8,768]{2,1,0:T(8,128)(2,1)}), bf16[16,8,768]{2,1,0:T(8,128)(2,1)S(1)}, u32[]{:S(2)}, u32[]{:S(2)}) %all-to-all-start.2) | async-done | bytes 196640 | tf_op jit(solution)/shard_map/all_to_all | solution.py:352
  113.1 0.7 shard_map.153
  (12 shorter events, 0.0 us)
Async XLA Ops:
  0.6 54.6 %copy-start.1 = (bf16[1,128,256]{2,1,0:T(8,128)(2,1)S(1)}, bf16[1,128,256]{2,1,0:T(8,128)(2,1)}, u32[]{:S(2)}) copy-start(bf16[1,128,256]{2,1,0:T(8,128)(2,1)} %param.12) | copy-start | bytes 196612
  0.6 54.6 %copy-start.11 = (f32[256]{0:T(256)S(1)}, f32[256]{0:T(256)}, u32[]{:S(2)}) copy-start(f32[256]{0:T(256)} %param.13) | copy-start | bytes 3076
  0.7 54.6 %copy-start.5 = (bf16[256,128]{1,0:T(8,128)(2,1)S(1)}, bf16[256,128]{1,0:T(8,128)(2,1)}, u32[]{:S(2)}) copy-start(bf16[256,128]{1,0:T(8,128)(2,1)} %router.3) | copy-start | bytes 196612
  0.7 52.3 %copy-start.9 = (s32[1,128,8]{1,2,0:T(8,128)S(1)}, s32[1,128,8]{1,2,0:T(8,128)}, u32[]{:S(2)}) copy-start(s32[1,128,8]{1,2,0:T(8,128)} %param.17) | copy-start | bytes 12292
  0.7 54.6 %copy-start.12 = (f32[1,128]{1,0:T(1,128)S(1)}, f32[1,128]{1,0:T(1,128)}, u32[]{:S(2)}) copy-start(f32[1,128]{1,0:T(1,128)} %scale.3) | copy-start | bytes 1540
  0.7 54.6 %copy-start.7 = (bf16[1,128,256]{2,1,0:T(8,128)(2,1)S(1)}, bf16[1,128,256]{2,1,0:T(8,128)(2,1)}, u32[]{:S(2)}) copy-start(bf16[1,128,256]{2,1,0:T(8,128)(2,1)} %param.15) | copy-start | bytes 196612
  0.7 67.9 %copy-start.2 = (bf16[1,128,512]{2,1,0:T(8,128)(2,1)S(1)}, bf16[1,128,512]{2,1,0:T(8,128)(2,1)}, u32[]{:S(2)}) copy-start(bf16[1,128,512]{2,1,0:T(8,128)(2,1)} %param.21) | copy-start | bytes 393220
  0.7 67.9 %copy-start.3 = (bf16[1,128,512]{2,1,0:T(8,128)(2,1)S(1)}, bf16[1,128,512]{2,1,0:T(8,128)(2,1)}, u32[]{:S(2)}) copy-start(bf16[1,128,512]{2,1,0:T(8,128)(2,1)} %param.22) | copy-start | bytes 393220
  4.6 50.6 %all-to-all-start = ((bf16[64,32,256]{2,1,0:T(8,128)(2,1)}), bf16[64,32,256]{2,1,0:T(8,128)(2,1)S(1)}, u32[]{:S(2)}, u32[]{:S(2)}) async-start(bf16[64,32,256]{2,1,0:T(8,128)(2,1)} %pack.1), calls=%async_computation | async-start | bytes 2097152 | tf_op jit(solution)/shard_map/all_to_all | solution.py:317
  27.7 0.8 copy-start
  28.6 0.8 copy-start.4
  29.4 0.7 copy-start.8
  30.1 0.7 copy-start.10
  57.7 14.1 %copy-start.13 = (bf16[120,256]{1,0:T(8,128)(2,1)S(1)}, bf16[120,256]{1,0:T(8,128)(2,1)}, u32[]{:S(2)}) copy-start(bf16[120,256]{1,0:T(8,128)(2,1)} %get-tuple-element.19) | copy-start | bytes 184324
  57.7 34.3 %all-to-all-start.1 = ((bf16[16,32,256]{2,1,0:T(8,128)(2,1)}), bf16[16,32,256]{2,1,0:T(8,128)(2,1)S(1)}, u32[]{:S(2)}, u32[]{:S(2)}) async-start(bf16[16,32,256]{2,1,0:T(8,128)(2,1)} %get-tuple-element.20), calls=%async_computation.1 | async-start | bytes 524288 | tf_op jit(solution)/shard_map/all_to_all | solution.py:341
  71.8 31.1 %copy-start.6 = (f32[128,256]{1,0:T(8,128)S(1)}, f32[128,256]{1,0:T(8,128)}, u32[]{:S(2)}) copy-start(f32[128,256]{1,0:T(8,128)} %get-tuple-element.18.full) | copy-start | bytes 393220
  96.9 16.2 %all-to-all-start.2 = ((bf16[16,8,768]{2,1,0:T(8,128)(2,1)}), bf16[16,8,768]{2,1,0:T(8,128)(2,1)S(1)}, u32[]{:S(2)}, u32[]{:S(2)}) async-start(bf16[16,8,768]{2,1,0:T(8,128)(2,1)} %bitcast.15), calls=%async_computation.2 | async-start | bytes 393216 | tf_op jit(solution)/shard_map/all_to_all | solution.py:352

commit v3 on v1

--- a/solution.py
+++ b/solution.py
@@ -15,21 +15,27 @@
 BF16 = jnp.bfloat16
 TOKENS = 128
 SLOTS = 16
-ROWS = 144
+ROWS = 136
 TAIL = 136
 GRANT = 24 * 2**20
 
 
-def call(kernel, outs, *args):
-    specs = [pl.BlockSpec(memory_space=pltpu.SMEM) if a.dtype == jnp.int32 and a.size == 1
-             else pl.BlockSpec(memory_space=pltpu.VMEM) for a in args]
+def call(kernel, outs, *args, far=(), far_out=(), scratch=()):
+    specs = [
+        pl.BlockSpec(
+            memory_space=pltpu.SMEM if a.dtype == jnp.int32 and a.size == 1 else pltpu.HBM if i in far else pltpu.VMEM
+        )
+        for i, a in enumerate(args)
+    ]
+    args = [pltpu.with_memory_space_constraint(a, pltpu.HBM) if i in far else a for i, a in enumerate(args)]
     one = isinstance(outs, jax.ShapeDtypeStruct)
-    vm = pl.BlockSpec(memory_space=pltpu.VMEM)
+    vm, hbm = pl.BlockSpec(memory_space=pltpu.VMEM), pl.BlockSpec(memory_space=pltpu.HBM)
     return pl.pallas_call(
         kernel,
         out_shape=outs,
         in_specs=specs,
-        out_specs=vm if one else tuple(vm for _ in outs),
+        out_specs=vm if one else tuple(hbm if i in far_out else vm for i in range(len(outs))),
+        scratch_shapes=scratch,
         compiler_params=pltpu.CompilerParams(vmem_limit_bytes=GRANT),
     )(*args)
 
@@ -66,20 +72,17 @@
     rows = []
     for k in range(TOPK):
         rows.append(jnp.sum(jnp.where(ids[k : k + 1, :] == experts, logits, 0.0), axis=0, keepdims=True))
-    a, b, c = three(jnp.concatenate(rows, axis=0))
+    a, b = high_low(jnp.concatenate(rows, axis=0))
     sent[0:TOKENS, :] = xv
-    sent[TOKENS : TOKENS + 8, 0:128] = a
-    sent[TOKENS : TOKENS + 8, 128:256] = b
-    sent[TOKENS + 8 : ROWS, 0:128] = c
-    sent[TOKENS + 8 : ROWS, 128:256] = jnp.zeros_like(c)
+    sent[TOKENS:ROWS, 0:128] = a
+    sent[TOKENS:ROWS, 128:256] = b
 
 
 def picks_kernel(own, total_out):
     total = jnp.zeros((8, 128), F32)
     for i in range(own.shape[0]):
-        top = own[i, TOKENS : TOKENS + 8, :].astype(F32)
-        low = own[i, TOKENS + 8 : ROWS, 0:128].astype(F32)
-        total = total + ((top[:, 0:128] + top[:, 128:256]) + low)
+        both = own[i, TOKENS:ROWS, :].astype(F32)
+        total = total + (both[:, 0:128] + both[:, 128:256])
     total_out[...] = total
 
 
@@ -112,7 +115,7 @@
         mix[:, g * step * SLOTS : (g + 1) * step * SLOTS] = block.astype(BF16)
 
 
-def rows_kernel(received, mix, dense, rank, router, x, gain, scale, out_grad, sent, full):
+def rows_kernel(received, mix, dense, rank, router, x, gain, scale, out_grad, sent_out, full, sent, done):
     n = dense.shape[0]
     rows = received[...]
     both = nn(mix[...], rows)
@@ -130,22 +133,31 @@
     d_high, d_low = high_low(diff)
     routed = nt(d_high, router[...]) + nt(d_low, router[...])
     grad = both + routed
+    s = jnp.broadcast_to(scale[...], (TOKENS, TOKENS)).T
+    moved = out_grad[...].astype(F32) + jnp.concatenate([s, s], axis=1) * (gain[...] * grad)
+    full[...] = moved
+    sent[0:TOKENS, :] = moved.astype(BF16)
+    copies = [
+        pltpu.make_async_copy(sent.at[0:TOKENS], sent_out.at[i, 0:TOKENS], done.at[i]) for i in range(sent_out.shape[0])
+    ]
+    for copy in copies:
+        copy.start()
     inner_terms = x[...].astype(F32) * gain[...] * grad
     i_high, i_mid, i_low = three(inner_terms)
     ones = jnp.ones((8, 256), BF16)
     inner = (nt(ones, i_high) + nt(ones, i_mid)) + nt(ones, i_low)
-    s = jnp.broadcast_to(scale[...], (TOKENS, TOKENS)).T
-    moved = out_grad[...].astype(F32) + jnp.concatenate([s, s], axis=1) * (gain[...] * grad)
-    full[...] = moved
-    low = moved.astype(BF16)
     a, b, c = three(inner)
     row = lax.broadcasted_iota(jnp.int32, (8, 256), 0)
     first = jnp.concatenate([a.astype(F32), b.astype(F32)], axis=1)
     second = jnp.concatenate([c.astype(F32), jnp.zeros((8, 128), F32)], axis=1)
     extra = jnp.where(row == 0, first, jnp.where(row == 1, second, 0.0)).astype(BF16)
-    for i in range(sent.shape[0]):
-        sent[i, 0:TOKENS, :] = low
-        sent[i, TOKENS:TAIL, :] = extra
+    sent[TOKENS:TAIL, :] = extra
+    for i in range(sent_out.shape[0]):
+        at = pltpu.make_async_copy(sent.at[TOKENS:TAIL], sent_out.at[i, TOKENS:TAIL], done.at[len(copies)])
+        at.start()
+        copies.append(at)
+    for copy in copies:
+        copy.wait()
 
 
 def contract(part, proj, core):
@@ -157,8 +169,18 @@
     return total
 
 
-def half_kernel(place, own, proj, out):
-    out[...] = contract(own, proj, place[0] % 2)
+def half_kernel(place, own, proj, out, held, done):
+    bands = 2
+    size = held.shape[0] // bands
+    copies = [
+        pltpu.make_async_copy(proj.at[b * size : (b + 1) * size], held.at[b * size : (b + 1) * size], done.at[b])
+        for b in range(bands)
+    ]
+    for copy in copies:
+        copy.start()
+    for b in range(bands):
+        copies[b].wait()
+        out[:, b * size : (b + 1) * size] = contract(own, held.at[b * size : (b + 1) * size], place[0] % 2)
 
 
 def early_kernel(place, own, other, proj, queries, keys, hidden_ctx, probs):
@@ -169,11 +191,11 @@
     key = keys[:, pl.ds(kv, HEAD_WIDTH)]
     at_key = lax.broadcasted_iota(jnp.int32, (TOKENS, TOKENS), 0)
     at_query = lax.broadcasted_iota(jnp.int32, (TOKENS, TOKENS), 1)
-    for h in range(probs.shape[0]):
+    for h in range(probs.shape[1] // TOKENS):
         scores = nt(key, queries[:, h * 128 : (h + 1) * 128]) * inv_sqrt
         scores = jnp.where(at_key <= at_query, scores, -jnp.inf)
         e = jnp.exp(scores - jnp.max(scores, axis=0, keepdims=True))
-        probs[h] = e / jnp.sum(e, axis=0, keepdims=True)
+        probs[:, h * TOKENS : (h + 1) * TOKENS] = e / jnp.sum(e, axis=0, keepdims=True)
 
 
 def attention_kernel(place, own, other, half, proj, queries, keys, values, hidden_ctx, probs, scale, width, sent, shift):
@@ -190,22 +212,19 @@
     key = keys[:, pl.ds(kv, HEAD_WIDTH)]
     value = values[:, pl.ds(kv, HEAD_WIDTH)]
     ctx = half[...] + contract(other, proj, 1 - core)
-    n = probs.shape[0]
-    key_sum = jnp.zeros((TOKENS, HEAD_WIDTH), F32)
-    value_sum = jnp.zeros((TOKENS, HEAD_WIDTH), F32)
+    n = hidden_ctx.shape[1] // HEAD_WIDTH
+    stack = lambda v: jnp.concatenate([v[:, h * 128 : (h + 1) * 128] for h in range(n)], axis=0)
+    wide = jnp.concatenate([column] * n, axis=1)
+    grads = stack((ctx - wide * hidden_ctx[...]).astype(BF16))
+    p = probs[...]
+    prob_grads = nt(value, grads)
+    delta = jnp.sum(p * prob_grads, axis=0, keepdims=True)
+    score_grads = p * (prob_grads - delta) * inv_sqrt
+    query_grads = nn(score_grads.T.astype(BF16), key).astype(BF16)
     for h in range(n):
-        cols = slice(h * 128, (h + 1) * 128)
-        grads = (ctx[:, cols] - column * hidden_ctx[:, cols]).astype(BF16)
-        p = probs[h]
-        prob_grads = nt(value, grads)
-        delta = jnp.sum(p * prob_grads, axis=0, keepdims=True)
-        score_grads = p * (prob_grads - delta) * inv_sqrt
-        low = score_grads.astype(BF16)
-        sent[:, cols] = nn(score_grads.T.astype(BF16), key).astype(BF16)
-        key_sum = key_sum + nn(low, queries[:, cols])
-        value_sum = value_sum + nn(p.astype(BF16), grads)
-    sent[:, n * 128 : n * 128 + 128] = key_sum.astype(BF16)
-    sent[:, n * 128 + 128 : n * 128 + 256] = value_sum.astype(BF16)
+        sent[:, h * 128 : (h + 1) * 128] = query_grads[h * 128 : (h + 1) * 128]
+    sent[:, n * 128 : n * 128 + 128] = nn(score_grads.astype(BF16), stack(queries[...])).astype(BF16)
+    sent[:, n * 128 + 128 : n * 128 + 256] = nn(p.astype(BF16), grads).astype(BF16)
 
 
 def hidden_kernel(full, x, shift, out):
@@ -269,22 +288,26 @@
     )
     late, full = call(
         rows_kernel,
-        (shape((n_head // 2, TAIL, columns), BF16), shape((TOKENS, columns))),
+        (pltpu.HBM((n_head // 2, TAIL, columns), BF16), shape((TOKENS, columns))),
         received, mix, dense, rank, router_weight, x, gain, norm_scale, out_grad[0],
+        far_out=(0,), scratch=(pltpu.VMEM((TAIL, columns), BF16), pltpu.SemaphoreType.DMA((n_head,))),
     )
     late_own = lax.all_to_all(late, "head", split_axis=0, concat_axis=0, tiled=True, axis_index_groups=cores)
     early_other = lax.ppermute(early_own, "head", swap)
     hidden_ctx, probs = call(
         early_kernel,
-        (shape((TOKENS, local)), shape((local // HEAD_WIDTH, TOKENS, TOKENS))),
+        (shape((TOKENS, local)), shape((TOKENS, local // HEAD_WIDTH * TOKENS))),
         place, early_own, early_other, out_proj, query_states[0], rotated_keys[0],
     )
     late_other = lax.ppermute(late_own, "head", swap)
-    half = call(half_kernel, shape((TOKENS, local)), place, late_own, out_proj)
+    half, held = call(
+        half_kernel, (shape((TOKENS, local)), shape(out_proj.shape, BF16)), place, late_own, out_proj,
+        far=(2,), scratch=(pltpu.SemaphoreType.DMA((2,)),),
+    )
     grads, shift = call(
         attention_kernel,
         (shape((TOKENS, local + 256), BF16), shape((TOKENS, TOKENS))),
-        place, late_own, late_other, half, out_proj, query_states[0], rotated_keys[0], value_tensor[0],
+        place, late_own, late_other, half, held, query_states[0], rotated_keys[0], value_tensor[0],
         hidden_ctx, probs, norm_scale, width,
     )
     grad_hidden = call(hidden_kernel, shape((TOKENS, columns), BF16), full, x, shift)

time: 111 us -> 112 us (level)
  Pallas kernels: 9.39 us -> 11.1 us
    pallas_call x9, Pallas kernels: 9.39 us -> 11.1 us  [call(): pl.pallas_call(kernel, out_shape=outs, in_specs=specs, out_specs=vm if on...]
    unnamed x23 -> x21, local copies, waits for them, and re-layouts: 3.64 us -> 3.05 us
  transfers between devices with their start and end apart: 6 -> 6, of which waited for: 3 -> 3; matrix products, arithmetic and copies ran while one was open for 0% -> 0% of each run, Pallas kernels for 3% -> 5%
where the time goes in v3:
time: 112 us
  starting transfers between devices  44 us (39%)
  waiting for transfers between devices  26.2 us (23%)
  blocking collectives  23.6 us (21%)
  Pallas kernels  11.1 us (10%)
  local copies, waits for them, and re-layouts  4.62 us (4%)
  other arithmetic  1.29 us (1%)
    all_gather x1, blocking collectives, per_device(): early_own = lax.all_gather(early, 'head', axis_index_groups=cores)  23.6 us
    all_to_all x1, starting transfers between devices, per_device(): lax.all_to_all(packed, 'exp', split_axis=0, concat_axis=0, tiled=True)  23.3 us
    all_to_all x1, waiting for transfers between devices, per_device(): lax.all_to_all(late, 'head', split_axis=0, concat_axis=0, tiled=True, axi...  15.9 us
    pallas_call x9, Pallas kernels, call(): pl.pallas_call(kernel, out_shape=outs, in_specs=specs, out_specs=vm if on...  11.1 us
    all_to_all x1, waiting for transfers between devices, per_device(): lax.all_to_all(grads.reshape(n_head, tokens, local + 256), 'head', split_...  9.51 us
    ppermute x1, starting transfers between devices, per_device(): picks_other = lax.ppermute(picks, 'head', swap)  7.21 us
    all_to_all x1, starting transfers between devices, per_device(): lax.all_to_all(late, 'head', split_axis=0, concat_axis=0, tiled=True, axi...  4.97 us
    all_to_all x1, starting transfers between devices, per_device(): lax.all_to_all(grads.reshape(n_head, tokens, local + 256), 'head', split_...  3.42 us
  transfers between devices with their start and end apart: 6, of which 3 were waited for; matrix products, arithmetic and copies ran while one was open for 0% of the time, Pallas kernels for 5%

profile of v3, /device:TPU:1, one launch (start us, length us, event | category | flops | bytes accessed | tf_op | source)
XLA Modules:
  0.0 111.7 jit_solution(7178447320392920026)
XLA Ops:
  0.6 0.8 copy.18
  1.4 1.3 %fusion.1 = bf16[64,2,16,256]{3,0,2,1:T(8,128)(2,1)S(1)} fusion(bf16[64,2,1,15]{3,0,2,1:T(8,128)(2,1)S(1)} %copy.18, bf16[64,2,15,256]{3,0,2,1:T(8,128)(2,1)} %bitcast.40), kind=kLoop, calls=%fused_computation.2 | loop fusion | flops 3145728 | bytes 2035456 | tf_op jit(solution)/shard_map/concatenate | solution.py:276
  2.7 0.0 copy-start.1
  2.8 0.0 copy-start.4
  2.8 0.0 copy-start.7
  2.8 0.0 copy-start.8
  2.8 1.6 %copy.17 = bf16[64,32,256]{2,1,0:T(8,128)(2,1)} copy(bf16[64,32,256]{2,0,1:T(8,128)(2,1)S(1)} %bitcast.39) | data formatting | bytes 2097152 | tf_op jit(solution)/shard_map/reshape | solution.py:277
  4.4 23.3 %all-to-all-start = ((bf16[64,32,256]{2,1,0:T(8,128)(2,1)}), bf16[64,32,256]{2,1,0:T(8,128)(2,1)S(1)}, u32[]{:S(2)}, u32[]{:S(2)}) async-start(bf16[64,32,256]{2,1,0:T(8,128)(2,1)} %copy.17), calls=%async_computation | async-start | bytes 2097152 | tf_op jit(solution)/shard_map/all_to_all | solution.py:278
  27.7 0.3 shard_map.147
  28.0 0.0 copy-start.2
  28.0 0.0 copy-start.3
  28.0 23.6 %all-gather = bf16[1088,256]{1,0:T(8,128)(2,1)S(1)} all-gather(bf16[136,256]{1,0:T(8,128)(2,1)S(1)} %shard_map.147), channel_id=2, replica_groups={{0,2,4,6,8,10,12,14},{1,3,5,7,9,11,13,15},{16,18,20,22,24,26,28,30},{17..., dimensions={0}, use_global_device_ids=true | all-gather | bytes 626688 | tf_op jit(solution)/shard_map/all_gather | solution.py:281
  51.6 7.2 %collective-permute-start = (f32[8,128]{1,0:T(8,128)S(1)}, f32[8,128]{1,0:T(8,128)S(1)}, u32[]{:S(2)}, u32[]{:S(2)}) collective-permute-start(f32[8,128]{1,0:T(8,128)S(1)} %shard_map.148.own), channel_id=1, source_target_pairs={{0,1},{1,0},{2,3},{3,2},{4,5},{5,4},{6,7},{7,6},{8,9},{9,8},{10,11... | collective-permute-start | bytes 12296 | tf_op jit(solution)/shard_map/ppermute | solution.py:283
  58.9 0.8 collective-permute-done.other
  59.7 0.4 shard_map.149
  60.1 0.0 all-to-all-done
  60.1 2.3 %shard_map.150 = (bf16[8,136,256]{2,1,0:T(8,128)(2,1)}, f32[128,256]{1,0:T(8,128)S(1)}) custom-call(bf16[2048,256]{1,0:T(8,128)(2,1)S(1)} %bitcast.25, bf16[128,2048]{1,0:T(8,128)(2,1)S(1)} %get-tuple-element.18.mix, f32[128,128]{1,0:T(8,128)S(1)} %get-tuple-element.19.dense, f32[128,128]{1,0:T(8,128)S(1)} %get-tuple-element.20.rank, ...), custom_call_target="tpu_custom_call" | custom-call | tf_op jit(solution)/shard_map/pallas_call | solution.py:33
  62.4 5.0 %all-to-all-start.1 = ((bf16[8,136,256]{2,1,0:T(8,128)(2,1)}), bf16[8,136,256]{2,1,0:T(8,128)(2,1)S(1)}, u32[]{:S(2)}, u32[]{:S(2)}) async-start(bf16[8,136,256]{2,1,0:T(8,128)(2,1)} %get-tuple-element.22), calls=%async_computation.1 | async-start | bytes 1114112 | tf_op jit(solution)/shard_map/all_to_all | solution.py:295
  67.4 2.8 %collective-permute-start.2 = (bf16[8,136,256]{2,1,0:T(8,128)(2,1)S(1)}, bf16[8,136,256]{2,1,0:T(8,128)(2,1)S(1)}, u32[]{:S(2)}, u32[]{:S(2)}) collective-permute-start(bf16[8,136,256]{2,1,0:T(8,128)(2,1)S(1)} %bitcast.23), channel_id=1, source_target_pairs={{0,1},{1,0},{2,3},{3,2},{4,5},{5,4},{6,7},{7,6},{8,9},{9,8},{10,11... | collective-permute-start | bytes 1671176 | tf_op jit(solution)/shard_map/ppermute | solution.py:296
  70.2 15.9 %all-to-all-done.1.own = bf16[8,136,256]{2,1,0:T(8,128)(2,1)S(1)} async-done(((bf16[8,136,256]{2,1,0:T(8,128)(2,1)}), bf16[8,136,256]{2,1,0:T(8,128)(2,1)S(1)}, u32[]{:S(2)}, u32[]{:S(2)}) %all-to-all-start.1) | async-done | bytes 557088 | tf_op jit(solution)/shard_map/all_to_all | solution.py:295
  86.1 2.4 %collective-permute-start.1 = (bf16[8,136,256]{2,1,0:T(8,128)(2,1)S(1)}, bf16[8,136,256]{2,1,0:T(8,128)(2,1)S(1)}, u32[]{:S(2)}, u32[]{:S(2)}) collective-permute-start(bf16[8,136,256]{2,1,0:T(8,128)(2,1)S(1)} %all-to-all-done.1.own), channel_id=1, source_target_pairs={{0,1},{1,0},{2,3},{3,2},{4,5},{5,4},{6,7},{7,6},{8,9},{9,8},{10,11... | collective-permute-start | bytes 1671176 | tf_op jit(solution)/shard_map/ppermute | solution.py:302
  88.5 0.0 copy-start
  88.5 2.2 %copy-done = bf16[512,4096]{1,0:T(8,128)(2,1)S(1)} copy-done((bf16[512,4096]{1,0:T(8,128)(2,1)S(1)}, bf16[512,4096]{1,0:T(8,128)(2,1)}, u32[]{:S(2)}) %copy-start) | copy-done | bytes 4194328
  90.7 1.6 %shard_map.152 = (f32[128,512]{1,0:T(8,128)S(1)}, f32[128,512]{1,0:T(8,128)S(1)}) custom-call(s32[1]{0:T(128)} %bitcast.11.place, bf16[8,136,256]{2,1,0:T(8,128)(2,1)S(1)} %bitcast.24, bf16[8,136,256]{2,1,0:T(8,128)(2,1)S(1)} %collective-permute-done.2.other, bf16[512,4096]{1,0:T(8,128)(2,1)S(1)} %copy-done, bf16[128,512]{1,0:T(8,128)(2,1)S(1)} %bitcast.29, ...), custom_call_target="tpu_custom_call" | custom-call | tf_op jit(solution)/shard_map/pallas_call | solution.py:33
  92.4 0.0 copy-start.5
  92.4 3.1 %shard_map.151 = (f32[128,512]{1,0:T(8,128)S(1)}, bf16[512,4096]{1,0:T(8,128)(2,1)S(1)}) custom-call(s32[1]{0:T(128)} %bitcast.11.place, bf16[8,136,256]{2,1,0:T(8,128)(2,1)S(1)} %all-to-all-done.1.own, bf16[512,4096]{1,0:T(8,128)(2,1)} %proj.3), custom_call_target="tpu_custom_call" | custom-call | tf_op jit(solution)/shard_map/pallas_call | solution.py:33
  95.4 0.0 collective-permute-done.1.other
  95.5 2.0 %shard_map.153 = (bf16[128,768]{1,0:T(8,128)(2,1)}, f32[128,128]{1,0:T(8,128)S(1)}) custom-call(s32[1]{0:T(128)} %bitcast.11.place, bf16[8,136,256]{2,1,0:T(8,128)(2,1)S(1)} %all-to-all-done.1.own, bf16[8,136,256]{2,1,0:T(8,128)(2,1)S(1)} %collective-permute-done.1.other, f32[128,512]{1,0:T(8,128)S(1)} %get-tuple-element.23.half, ...), custom_call_target="tpu_custom_call" | custom-call | tf_op jit(solution)/shard_map/pallas_call | solution.py:33
  97.5 3.4 %all-to-all-start.2 = ((bf16[16,8,768]{2,1,0:T(8,128)(2,1)}), bf16[16,8,768]{2,1,0:T(8,128)(2,1)S(1)}, u32[]{:S(2)}, u32[]{:S(2)}) async-start(bf16[16,8,768]{2,1,0:T(8,128)(2,1)} %bitcast.16), calls=%async_computation.2 | async-start | bytes 393216 | tf_op jit(solution)/shard_map/all_to_all | solution.py:315
  100.9 0.7 shard_map.154
  101.6 9.5 %all-to-all-done.2.received = bf16[16,8,768]{2,1,0:T(8,128)(2,1)S(1)} async-done(((bf16[16,8,768]{2,1,0:T(8,128)(2,1)}), bf16[16,8,768]{2,1,0:T(8,128)(2,1)S(1)}, u32[]{:S(2)}, u32[]{:S(2)}) %all-to-all-start.2) | async-done | bytes 196640 | tf_op jit(solution)/shard_map/all_to_all | solution.py:315
  111.1 0.7 shard_map.155
  (13 shorter events, 0.0 us)
Async XLA Ops:
  2.7 24.9 %copy-start.1 = (bf16[1,128,256]{2,1,0:T(8,128)(2,1)S(1)}, bf16[1,128,256]{2,1,0:T(8,128)(2,1)}, u32[]{:S(2)}) copy-start(bf16[1,128,256]{2,1,0:T(8,128)(2,1)} %param.12) | copy-start | bytes 196612
  2.8 24.9 %copy-start.4 = (bf16[256,128]{1,0:T(8,128)(2,1)S(1)}, bf16[256,128]{1,0:T(8,128)(2,1)}, u32[]{:S(2)}) copy-start(bf16[256,128]{1,0:T(8,128)(2,1)} %router.3) | copy-start | bytes 196612
  2.8 24.9 %copy-start.7 = (s32[1,128,8]{1,2,0:T(8,128)S(1)}, s32[1,128,8]{1,2,0:T(8,128)}, u32[]{:S(2)}) copy-start(s32[1,128,8]{1,2,0:T(8,128)} %param.17) | copy-start | bytes 12292
  2.8 24.9 %copy-start.8 = (f32[256]{0:T(256)S(1)}, f32[256]{0:T(256)}, u32[]{:S(2)}) copy-start(f32[256]{0:T(256)} %param.13) | copy-start | bytes 3076
  4.4 55.7 %copy-start.6 = (bf16[1,128,256]{2,1,0:T(8,128)(2,1)S(1)}, bf16[1,128,256]{2,1,0:T(8,128)(2,1)}, u32[]{:S(2)}) copy-start(bf16[1,128,256]{2,1,0:T(8,128)(2,1)} %param.15) | copy-start | bytes 196612
  4.4 55.7 %copy-start.9 = (f32[1,128]{1,0:T(1,128)S(1)}, f32[1,128]{1,0:T(1,128)}, u32[]{:S(2)}) copy-start(f32[1,128]{1,0:T(1,128)} %scale.3) | copy-start | bytes 1540
  4.4 55.7 %all-to-all-start = ((bf16[64,32,256]{2,1,0:T(8,128)(2,1)}), bf16[64,32,256]{2,1,0:T(8,128)(2,1)S(1)}, u32[]{:S(2)}, u32[]{:S(2)}) async-start(bf16[64,32,256]{2,1,0:T(8,128)(2,1)} %copy.17), calls=%async_computation | async-start | bytes 2097152 | tf_op jit(solution)/shard_map/all_to_all | solution.py:278
  28.0 60.5 %copy-start.2 = (bf16[1,128,512]{2,1,0:T(8,128)(2,1)S(1)}, bf16[1,128,512]{2,1,0:T(8,128)(2,1)}, u32[]{:S(2)}) copy-start(bf16[1,128,512]{2,1,0:T(8,128)(2,1)} %param.21) | copy-start | bytes 393220
  28.0 60.5 %copy-start.3 = (bf16[1,128,512]{2,1,0:T(8,128)(2,1)S(1)}, bf16[1,128,512]{2,1,0:T(8,128)(2,1)}, u32[]{:S(2)}) copy-start(bf16[1,128,512]{2,1,0:T(8,128)(2,1)} %param.22) | copy-start | bytes 393220
  51.6 8.0 %collective-permute-start = (f32[8,128]{1,0:T(8,128)S(1)}, f32[8,128]{1,0:T(8,128)S(1)}, u32[]{:S(2)}, u32[]{:S(2)}) collective-permute-start(f32[8,128]{1,0:T(8,128)S(1)} %shard_map.148.own), channel_id=1, source_target_pairs={{0,1},{1,0},{2,3},{3,2},{4,5},{5,4},{6,7},{7,6},{8,9},{9,8},{10,11... | collective-permute-start | bytes 12296 | tf_op jit(solution)/shard_map/ppermute | solution.py:283
  62.4 23.6 %all-to-all-start.1 = ((bf16[8,136,256]{2,1,0:T(8,128)(2,1)}), bf16[8,136,256]{2,1,0:T(8,128)(2,1)S(1)}, u32[]{:S(2)}, u32[]{:S(2)}) async-start(bf16[8,136,256]{2,1,0:T(8,128)(2,1)} %get-tuple-element.22), calls=%async_computation.1 | async-start | bytes 1114112 | tf_op jit(solution)/shard_map/all_to_all | solution.py:295
  67.4 21.1 %collective-permute-start.2 = (bf16[8,136,256]{2,1,0:T(8,128)(2,1)S(1)}, bf16[8,136,256]{2,1,0:T(8,128)(2,1)S(1)}, u32[]{:S(2)}, u32[]{:S(2)}) collective-permute-start(bf16[8,136,256]{2,1,0:T(8,128)(2,1)S(1)} %bitcast.23), channel_id=1, source_target_pairs={{0,1},{1,0},{2,3},{3,2},{4,5},{5,4},{6,7},{7,6},{8,9},{9,8},{10,11... | collective-permute-start | bytes 1671176 | tf_op jit(solution)/shard_map/ppermute | solution.py:296
  86.1 9.4 %collective-permute-start.1 = (bf16[8,136,256]{2,1,0:T(8,128)(2,1)S(1)}, bf16[8,136,256]{2,1,0:T(8,128)(2,1)S(1)}, u32[]{:S(2)}, u32[]{:S(2)}) collective-permute-start(bf16[8,136,256]{2,1,0:T(8,128)(2,1)S(1)} %all-to-all-done.1.own), channel_id=1, source_target_pairs={{0,1},{1,0},{2,3},{3,2},{4,5},{5,4},{6,7},{7,6},{8,9},{9,8},{10,11... | collective-permute-start | bytes 1671176 | tf_op jit(solution)/shard_map/ppermute | solution.py:302
  88.5 2.2 %copy-start = (bf16[512,4096]{1,0:T(8,128)(2,1)S(1)}, bf16[512,4096]{1,0:T(8,128)(2,1)}, u32[]{:S(2)}) copy-start(bf16[512,4096]{1,0:T(8,128)(2,1)} %proj.3) | copy-start | bytes 12582916
  92.4 3.1 %copy-start.5 = (bf16[1,128,512]{2,1,0:T(8,128)(2,1)S(1)}, bf16[1,128,512]{2,1,0:T(8,128)(2,1)}, u32[]{:S(2)}) copy-start(bf16[1,128,512]{2,1,0:T(8,128)(2,1)} %param.23) | copy-start | bytes 393220
  97.5 13.6 %all-to-all-start.2 = ((bf16[16,8,768]{2,1,0:T(8,128)(2,1)}), bf16[16,8,768]{2,1,0:T(8,128)(2,1)S(1)}, u32[]{:S(2)}, u32[]{:S(2)}) async-start(bf16[16,8,768]{2,1,0:T(8,128)(2,1)} %bitcast.16), calls=%async_computation.2 | async-start | bytes 393216 | tf_op jit(solution)/shard_map/all_to_all | solution.py:315

commit v4 on v3

--- a/solution.py
+++ b/solution.py
@@ -15,7 +15,9 @@
 BF16 = jnp.bfloat16
 TOKENS = 128
 SLOTS = 16
-ROWS = 136
+MAIN = 112
+LEFT = TOKENS - MAIN
+ROWS = MAIN + 8
 TAIL = 136
 GRANT = 24 * 2**20
 
@@ -73,25 +75,13 @@
     for k in range(TOPK):
         rows.append(jnp.sum(jnp.where(ids[k : k + 1, :] == experts, logits, 0.0), axis=0, keepdims=True))
     a, b = high_low(jnp.concatenate(rows, axis=0))
-    sent[0:TOKENS, :] = xv
-    sent[TOKENS:ROWS, 0:128] = a
-    sent[TOKENS:ROWS, 128:256] = b
-
-
-def picks_kernel(own, total_out):
-    total = jnp.zeros((8, 128), F32)
-    for i in range(own.shape[0]):
-        both = own[i, TOKENS:ROWS, :].astype(F32)
-        total = total + (both[:, 0:128] + both[:, 128:256])
-    total_out[...] = total
-
-
-def weights_kernel(own, other, ids, mix, dense, rank):
-    total = own[...] + other[...]
-    top = jnp.max(total, axis=0, keepdims=True)
-    e = jnp.exp(total - top)
-    gates = e / jnp.sum(e, axis=0, keepdims=True)
-    n = dense.shape[0]
+    sent[0:MAIN, :] = xv[0:MAIN]
+    sent[MAIN:ROWS, 0:128] = a
+    sent[MAIN:ROWS, 128:256] = b
+
+
+def spread(gates, ids):
+    n = gates.shape[1]
     experts = lax.broadcasted_iota(jnp.int32, (n, TOKENS), 0)
     weight = jnp.zeros((n, TOKENS), F32)
     member = jnp.zeros((n, TOKENS), F32)
@@ -102,11 +92,21 @@
     t_from = lax.broadcasted_iota(jnp.int32, (TOKENS, TOKENS), 0)
     t_to = lax.broadcasted_iota(jnp.int32, (TOKENS, TOKENS), 1)
     earlier = jnp.where(t_from < t_to, 1.0, 0.0).astype(BF16)
-    before = nn(member.astype(BF16), earlier)
-    dense[...] = weight
-    rank[...] = before
+    return weight, nn(member.astype(BF16), earlier)
+
+
+def weights_kernel(gathered, ids, mix, gates_out):
+    total = jnp.zeros((8, 128), F32)
+    for i in range(gathered.shape[0]):
+        both = gathered[i, MAIN:ROWS, :].astype(F32)
+        total = total + (both[:, 0:128] + both[:, 128:256])
+    top = jnp.max(total, axis=0, keepdims=True)
+    e = jnp.exp(total - top)
+    gates = e / jnp.sum(e, axis=0, keepdims=True)
+    gates_out[...] = gates
+    weight, before = spread(gates, ids)
     step = 8
-    for g in range(n // step):
+    for g in range(weight.shape[0] // step):
         w3 = weight[g * step : (g + 1) * step, :][:, None, :]
         b3 = before[g * step : (g + 1) * step, :][:, None, :]
         slot = lax.broadcasted_iota(jnp.int32, (step, SLOTS, TOKENS), 1).astype(F32)
@@ -115,19 +115,18 @@
         mix[:, g * step * SLOTS : (g + 1) * step * SLOTS] = block.astype(BF16)
 
 
-def rows_kernel(received, mix, dense, rank, router, x, gain, scale, out_grad, sent_out, full, sent, done):
-    n = dense.shape[0]
+def rows_kernel(received, mix, gates, ids, router, x, gain, scale, out_grad, sent_out, full_out, sent, full, done):
+    weight, ranks = spread(gates[...], ids)
+    n = weight.shape[0]
     rows = received[...]
     both = nn(mix[...], rows)
     e_of = lax.broadcasted_iota(jnp.int32, (n, n * SLOTS), 0)
     j_of = lax.broadcasted_iota(jnp.int32, (n, n * SLOTS), 1)
     pick = jnp.where(j_of == e_of * SLOTS + (SLOTS - 1), 1.0, 0.0).astype(BF16)
     table = nn(pick, received[:, 0:128])
-    ranks = rank[...]
     slot_grads = jnp.zeros((n, TOKENS), F32)
     for c in range(SLOTS - 1):
         slot_grads = jnp.where(ranks == float(c), table[:, c : c + 1], slot_grads)
-    weight = dense[...]
     mean = jnp.sum(weight * slot_grads, axis=0, keepdims=True)
     diff = (weight * (slot_grads - mean)).T
     d_high, d_low = high_low(diff)
@@ -140,6 +139,7 @@
     copies = [
         pltpu.make_async_copy(sent.at[0:TOKENS], sent_out.at[i, 0:TOKENS], done.at[i]) for i in range(sent_out.shape[0])
     ]
+    copies.append(pltpu.make_async_copy(full, full_out, done.at[len(copies)]))
     for copy in copies:
         copy.start()
     inner_terms = x[...].astype(F32) * gain[...] * grad
@@ -160,17 +160,23 @@
         copy.wait()
 
 
-def contract(part, proj, core):
+def contract(rows_of, blocks, proj):
     total = None
-    for i in range(part.shape[0]):
-        at = pl.multiple_of(i * 512 + core * 256, 256)
-        term = nt(part[i, 0:TOKENS, :], proj[:, pl.ds(at, 256)])
+    for i, at in blocks:
+        term = nt(rows_of(i), proj[:, pl.ds(at, 256)])
         total = term if total is None else total + term
     return total
 
 
-def half_kernel(place, own, proj, out, held, done):
-    bands = 2
+def stacked(part, left, proj, core):
+    blocks = [(i, pl.multiple_of(i * 512 + core * 256, 256)) for i in range(part.shape[0])]
+    return contract(
+        lambda i: jnp.concatenate([part[i, 0:TOKENS, :], left[2 * i + core]], axis=0), blocks, proj
+    )
+
+
+def half_kernel(place, own, left, proj, out, held, done):
+    bands = done.shape[0]
     size = held.shape[0] // bands
     copies = [
         pltpu.make_async_copy(proj.at[b * size : (b + 1) * size], held.at[b * size : (b + 1) * size], done.at[b])
@@ -180,12 +186,12 @@
         copy.start()
     for b in range(bands):
         copies[b].wait()
-        out[:, b * size : (b + 1) * size] = contract(own, held.at[b * size : (b + 1) * size], place[0] % 2)
-
-
-def early_kernel(place, own, other, proj, queries, keys, hidden_ctx, probs):
-    core = place[0] % 2
-    hidden_ctx[...] = contract(own, proj, core) + contract(other, proj, 1 - core)
+        out[:, b * size : (b + 1) * size] = stacked(own, left, held.at[b * size : (b + 1) * size], place[0] % 2)
+
+
+def early_kernel(place, gathered, proj, queries, keys, hidden_ctx, probs):
+    blocks = [(i, i * 256) for i in range(gathered.shape[0])]
+    hidden_ctx[...] = contract(lambda i: gathered[i, 0:MAIN, :], blocks, proj)
     inv_sqrt = 1.0 / math.sqrt(HEAD_WIDTH)
     kv = pl.multiple_of(place[0] // KEY_VALUE_HEADS * HEAD_WIDTH, HEAD_WIDTH)
     key = keys[:, pl.ds(kv, HEAD_WIDTH)]
@@ -198,7 +204,7 @@
         probs[:, h * TOKENS : (h + 1) * TOKENS] = e / jnp.sum(e, axis=0, keepdims=True)
 
 
-def attention_kernel(place, own, other, half, proj, queries, keys, values, hidden_ctx, probs, scale, width, sent, shift):
+def attention_kernel(place, own, other, left, half, proj, queries, keys, values, hidden_ctx, probs, scale, width, sent, shift):
     core = place[0] % 2
     row = jnp.zeros((1, 128), F32)
     for part in (own, other):
@@ -211,11 +217,13 @@
     kv = pl.multiple_of(place[0] // KEY_VALUE_HEADS * HEAD_WIDTH, HEAD_WIDTH)
     key = keys[:, pl.ds(kv, HEAD_WIDTH)]
     value = values[:, pl.ds(kv, HEAD_WIDTH)]
-    ctx = half[...] + contract(other, proj, 1 - core)
+    both = half[...] + stacked(other, left, proj, 1 - core)
+    ctx = both[0:TOKENS]
+    hidden = jnp.concatenate([hidden_ctx[...], both[TOKENS:]], axis=0)
     n = hidden_ctx.shape[1] // HEAD_WIDTH
     stack = lambda v: jnp.concatenate([v[:, h * 128 : (h + 1) * 128] for h in range(n)], axis=0)
     wide = jnp.concatenate([column] * n, axis=1)
-    grads = stack((ctx - wide * hidden_ctx[...]).astype(BF16))
+    grads = stack((ctx - wide * hidden).astype(BF16))
     p = probs[...]
     prob_grads = nt(value, grads)
     delta = jnp.sum(p * prob_grads, axis=0, keepdims=True)
@@ -278,36 +286,37 @@
     received = lax.all_to_all(packed, "exp", split_axis=0, concat_axis=0, tiled=True)
     received = received.reshape(n_experts * SLOTS, columns)
     early = call(logits_kernel, shape((ROWS, columns), BF16), x, gain, router_weight, ids)
-    early_own = lax.all_gather(early, "head", axis_index_groups=cores)
-    picks = call(picks_kernel, shape((8, 128)), early_own)
-    picks_other = lax.ppermute(picks, "head", swap)
-    mix, dense, rank = call(
-        weights_kernel,
-        (shape((TOKENS, n_experts * SLOTS), BF16), shape((n_experts, TOKENS)), shape((n_experts, TOKENS))),
-        picks, picks_other, ids,
+    early = lax.all_gather(early, "head")
+    mix, gate_weights = call(
+        weights_kernel, (shape((TOKENS, n_experts * SLOTS), BF16), shape((TOPK, TOKENS))), early, ids,
+    )
+    hidden_ctx, probs = call(
+        early_kernel,
+        (shape((MAIN, local)), shape((TOKENS, local // HEAD_WIDTH * TOKENS))),
+        place, early, out_proj, query_states[0], rotated_keys[0],
     )
     late, full = call(
         rows_kernel,
-        (pltpu.HBM((n_head // 2, TAIL, columns), BF16), shape((TOKENS, columns))),
-        received, mix, dense, rank, router_weight, x, gain, norm_scale, out_grad[0],
-        far_out=(0,), scratch=(pltpu.VMEM((TAIL, columns), BF16), pltpu.SemaphoreType.DMA((n_head,))),
+        (pltpu.HBM((n_head // 2, TAIL, columns), BF16), pltpu.HBM((TOKENS, columns), F32)),
+        received, mix, gate_weights, ids, router_weight, x, gain, norm_scale, out_grad[0],
+        far_out=(0, 1),
+        scratch=(
+            pltpu.VMEM((TAIL, columns), BF16), pltpu.VMEM((TOKENS, columns), F32),
+            pltpu.SemaphoreType.DMA((n_head + 1,)),
+        ),
     )
     late_own = lax.all_to_all(late, "head", split_axis=0, concat_axis=0, tiled=True, axis_index_groups=cores)
-    early_other = lax.ppermute(early_own, "head", swap)
-    hidden_ctx, probs = call(
-        early_kernel,
-        (shape((TOKENS, local)), shape((TOKENS, local // HEAD_WIDTH * TOKENS))),
-        place, early_own, early_other, out_proj, query_states[0], rotated_keys[0],
-    )
+    left = lax.all_gather(x[MAIN:TOKENS], "head")
     late_other = lax.ppermute(late_own, "head", swap)
     half, held = call(
-        half_kernel, (shape((TOKENS, local)), shape(out_proj.shape, BF16)), place, late_own, out_proj,
-        far=(2,), scratch=(pltpu.SemaphoreType.DMA((2,)),),
+        half_kernel, (shape((TOKENS + LEFT, local)), shape(out_proj.shape, BF16)),
+        place, late_own, left, out_proj,
+        far=(3,), scratch=(pltpu.SemaphoreType.DMA((4,)),),
     )
     grads, shift = call(
         attention_kernel,
         (shape((TOKENS, local + 256), BF16), shape((TOKENS, TOKENS))),
-        place, late_own, late_other, half, held, query_states[0], rotated_keys[0], value_tensor[0],
+        place, late_own, late_other, left, half, held, query_states[0], rotated_keys[0], value_tensor[0],
         hidden_ctx, probs, norm_scale, width,
     )
     grad_hidden = call(hidden_kernel, shape((TOKENS, columns), BF16), full, x, shift)

time: 112 us -> 125 us (1.12)
  blocking collectives: 23.6 us -> 57.7 us
  waiting for transfers between devices: 26.2 us -> 14.4 us
  starting transfers between devices: 44 us -> 34.7 us
    all_to_all x0 -> x1, blocking collectives: none -> 20.9 us  [per_device(): lax.all_to_all(late, 'head', split_axis=0, concat_axis=0, tiled=True, axi...]
    all_to_all x1 -> x0, waiting for transfers between devices: 15.9 us -> none  [per_device(): lax.all_to_all(late, 'head', split_axis=0, concat_axis=0, tiled=True, axi...]
    all_gather x1 -> x2, blocking collectives: 23.6 us -> 36.8 us  [the longest x1 21.9 us: per_device(): early = lax.all_gather(early, 'head')]
    ppermute x2 -> x0, starting transfers between devices: 9.98 us -> none  [the longest x1 7.21 us: per_device(): picks_other = lax.ppermute(picks, 'head', swap)]
    ppermute x1, starting transfers between devices: 2.39 us -> 7.39 us  [per_device(): late_other = lax.ppermute(late_own, 'head', swap)]
    all_to_all x1 -> x0, starting transfers between devices: 4.97 us -> none  [per_device(): lax.all_to_all(late, 'head', split_axis=0, concat_axis=0, tiled=True, axi...]
    all_to_all x1, waiting for transfers between devices: 0.01 us -> 4.86 us  [per_device(): lax.all_to_all(packed, 'exp', split_axis=0, concat_axis=0, tiled=True)]
    pallas_call x9 -> x8, Pallas kernels: 11.1 us -> 11.1 us  [call(): pl.pallas_call(kernel, out_shape=outs, in_specs=specs, out_specs=vm if on...]
  transfers between devices with their start and end apart: 6 -> 3, of which waited for: 3 -> 2; matrix products, arithmetic and copies ran while one was open for 0% -> 0% of each run, Pallas kernels for 5% -> 5%
where the time goes in v4:
time: 125 us
  blocking collectives  57.7 us (46%)
  starting transfers between devices  34.7 us (28%)
  waiting for transfers between devices  14.4 us (12%)
  Pallas kernels  11.1 us (9%)
  local copies, waits for them, and re-layouts  4.62 us (4%)
  other arithmetic  1.3 us (1%)
    all_to_all x1, starting transfers between devices, per_device(): lax.all_to_all(packed, 'exp', split_axis=0, concat_axis=0, tiled=True)  23.3 us
    all_gather x1, blocking collectives, per_device(): early = lax.all_gather(early, 'head')  21.9 us
    all_to_all x1, blocking collectives, per_device(): lax.all_to_all(late, 'head', split_axis=0, concat_axis=0, tiled=True, axi...  20.9 us
    all_gather x1, blocking collectives, per_device(): left = lax.all_gather(x[MAIN:TOKENS], 'head')  14.9 us
    pallas_call x8, Pallas kernels, call(): pl.pallas_call(kernel, out_shape=outs, in_specs=specs, out_specs=vm if on...  11.1 us
    all_to_all x1, waiting for transfers between devices, per_device(): lax.all_to_all(grads.reshape(n_head, tokens, local + 256), 'head', split_...  9.54 us
    ppermute x1, starting transfers between devices, per_device(): late_other = lax.ppermute(late_own, 'head', swap)  7.39 us
    all_to_all x1, waiting for transfers between devices, per_device(): lax.all_to_all(packed, 'exp', split_axis=0, concat_axis=0, tiled=True)  4.86 us
  transfers between devices with their start and end apart: 3, of which 2 were waited for; matrix products, arithmetic and copies ran while one was open for 0% of the time, Pallas kernels for 5%

profile of v4, /device:TPU:1, one launch (start us, length us, event | category | flops | bytes accessed | tf_op | source)
XLA Modules:
  0.0 124.7 jit_solution(3263557352791770565)
XLA Ops:
  0.6 0.8 copy.20
  1.4 1.3 %fusion.1 = bf16[64,2,16,256]{3,0,2,1:T(8,128)(2,1)S(1)} fusion(bf16[64,2,1,15]{3,0,2,1:T(8,128)(2,1)S(1)} %copy.20, bf16[64,2,15,256]{3,0,2,1:T(8,128)(2,1)} %bitcast.40), kind=kLoop, calls=%fused_computation.2 | loop fusion | flops 3145728 | bytes 2035456 | tf_op jit(solution)/shard_map/concatenate | solution.py:284
  2.7 0.0 copy-start.1
  2.8 0.0 copy-start.4
  2.8 0.0 copy-start.8
  2.8 0.0 copy-start.9
  2.8 1.6 %copy.19 = bf16[64,32,256]{2,1,0:T(8,128)(2,1)} copy(bf16[64,32,256]{2,0,1:T(8,128)(2,1)S(1)} %bitcast.39) | data formatting | bytes 2097152 | tf_op jit(solution)/shard_map/reshape | solution.py:285
  4.4 23.3 %all-to-all-start = ((bf16[64,32,256]{2,1,0:T(8,128)(2,1)}), bf16[64,32,256]{2,1,0:T(8,128)(2,1)S(1)}, u32[]{:S(2)}, u32[]{:S(2)}) async-start(bf16[64,32,256]{2,1,0:T(8,128)(2,1)} %copy.19), calls=%async_computation | async-start | bytes 2097152 | tf_op jit(solution)/shard_map/all_to_all | solution.py:286
  27.7 0.0 copy-done.1
  27.7 0.0 copy-done.4
  27.7 0.0 copy-done.8
  27.7 0.0 copy-done.9
  27.7 0.3 shard_map.147
  28.0 21.9 %all-gather = bf16[1920,256]{1,0:T(8,128)(2,1)S(1)} all-gather(bf16[120,256]{1,0:T(8,128)(2,1)S(1)} %shard_map.147), channel_id=2, replica_groups=mesh['exp'=64,'head'=16] {'head'}, dimensions={0}, use_global_device_ids=true | all-gather | bytes 1044480 | tf_op jit(solution)/shard_map/all_gather | solution.py:289
  49.9 0.4 shard_map.148
  50.3 4.9 %all-to-all-done = bf16[64,32,256]{2,1,0:T(8,128)(2,1)S(1)} async-done(((bf16[64,32,256]{2,1,0:T(8,128)(2,1)}), bf16[64,32,256]{2,1,0:T(8,128)(2,1)S(1)}, u32[]{:S(2)}, u32[]{:S(2)}) %all-to-all-start) | async-done | bytes 1048608 | tf_op jit(solution)/shard_map/all_to_all | solution.py:286
  55.1 0.0 copy-done.7
  55.1 2.4 %shard_map.149 = (bf16[8,136,256]{2,1,0:T(8,128)(2,1)}, f32[128,256]{1,0:T(8,128)}) custom-call(bf16[2048,256]{1,0:T(8,128)(2,1)S(1)} %bitcast.24, bf16[128,2048]{1,0:T(8,128)(2,1)S(1)} %get-tuple-element.17.mix, f32[8,128]{1,0:T(8,128)S(1)} %get-tuple-element.18.gates, s32[8,128]{1,0:T(8,128)S(1)} %bitcast.36, bf16[256,128]{1,0:T(8,128)(2,1)S(1)} %copy-done.4, ...), custom_call_target="tpu_custom_call" | custom-call | tf_op jit(solution)/shard_map/pallas_call | solution.py:35
  57.6 20.9 %all_to_all.15.own = bf16[8,136,256]{2,1,0:T(8,128)(2,1)S(1)} all-to-all(bf16[8,136,256]{2,1,0:T(8,128)(2,1)} %get-tuple-element.20), channel_id=1, replica_groups={{0,2,4,6,8,10,12,14},{1,3,5,7,9,11,13,15},{16,18,20,22,24,26,28,30},{17..., dimensions={0} | all-to-all | bytes 1114112 | tf_op jit(solution)/shard_map/all_to_all | solution.py:308
  78.5 7.4 %collective-permute-start = (bf16[8,136,256]{2,1,0:T(8,128)(2,1)S(1)}, bf16[8,136,256]{2,1,0:T(8,128)(2,1)S(1)}, u32[]{:S(2)}, u32[]{:S(2)}) collective-permute-start(bf16[8,136,256]{2,1,0:T(8,128)(2,1)S(1)} %all_to_all.15.own), channel_id=1, source_target_pairs={{0,1},{1,0},{2,3},{3,2},{4,5},{5,4},{6,7},{7,6},{8,9},{9,8},{10,11... | collective-permute-start | bytes 1671176 | tf_op jit(solution)/shard_map/ppermute | solution.py:310
  86.0 0.0 copy-start
  86.0 2.2 %copy-done = bf16[512,4096]{1,0:T(8,128)(2,1)S(1)} copy-done((bf16[512,4096]{1,0:T(8,128)(2,1)S(1)}, bf16[512,4096]{1,0:T(8,128)(2,1)}, u32[]{:S(2)}) %copy-start) | copy-done | bytes 4194328
  88.2 1.6 %shard_map.151 = (f32[112,512]{1,0:T(8,128)S(1)}, f32[128,512]{1,0:T(8,128)S(1)}) custom-call(s32[1]{0:T(128)} %bitcast.11.place, bf16[16,120,256]{2,1,0:T(8,128)(2,1)S(1)} %bitcast.23, bf16[512,4096]{1,0:T(8,128)(2,1)S(1)} %copy-done, bf16[128,512]{1,0:T(8,128)(2,1)S(1)} %bitcast.28, bf16[128,512]{1,0:T(8,128)(2,1)S(1)} %bitcast.30), custom_call_target="tpu_custom_call" | custom-call | tf_op jit(solution)/shard_map/pallas_call | solution.py:35
  89.8 14.9 %all_gather.12.left = bf16[16,16,256]{2,1,0:T(8,128)(2,1)S(1)} all-gather(bf16[1,16,256]{2,1,0:T(8,128)(2,1)S(1)} %slice.4), channel_id=1, replica_groups=mesh['exp'=64,'head'=16] {'head'}, dimensions={0}, use_global_device_ids=true | all-gather | bytes 139264 | tf_op jit(solution)/shard_map/all_gather | solution.py:309
  104.6 3.1 %shard_map.150 = (f32[144,512]{1,0:T(8,128)S(1)}, bf16[512,4096]{1,0:T(8,128)(2,1)S(1)}) custom-call(s32[1]{0:T(128)} %bitcast.11.place, bf16[8,136,256]{2,1,0:T(8,128)(2,1)S(1)} %all_to_all.15.own, bf16[16,16,256]{2,1,0:T(8,128)(2,1)S(1)} %all_gather.12.left, bf16[512,4096]{1,0:T(8,128)(2,1)} %proj.3), custom_call_target="tpu_custom_call" | custom-call | tf_op jit(solution)/shard_map/pallas_call | solution.py:35
  107.8 0.0 collective-permute-done.other
  107.8 0.0 copy-start.6
  107.8 2.0 %shard_map.152 = (bf16[128,768]{1,0:T(8,128)(2,1)}, f32[128,128]{1,0:T(8,128)S(1)}) custom-call(s32[1]{0:T(128)} %bitcast.11.place, bf16[8,136,256]{2,1,0:T(8,128)(2,1)S(1)} %all_to_all.15.own, bf16[8,136,256]{2,1,0:T(8,128)(2,1)S(1)} %collective-permute-done.other, bf16[16,16,256]{2,1,0:T(8,128)(2,1)S(1)} %all_gather.12.left, ...), custom_call_target="tpu_custom_call" | custom-call | tf_op jit(solution)/shard_map/pallas_call | solution.py:35
  109.8 4.0 %all-to-all-start.2 = ((bf16[16,8,768]{2,1,0:T(8,128)(2,1)}), bf16[16,8,768]{2,1,0:T(8,128)(2,1)S(1)}, u32[]{:S(2)}, u32[]{:S(2)}) async-start(bf16[16,8,768]{2,1,0:T(8,128)(2,1)} %bitcast.16), calls=%async_computation.2 | async-start | bytes 393216 | tf_op jit(solution)/shard_map/all_to_all | solution.py:324
  113.8 0.7 shard_map.153
  114.5 9.5 %all-to-all-done.2.received = bf16[16,8,768]{2,1,0:T(8,128)(2,1)S(1)} async-done(((bf16[16,8,768]{2,1,0:T(8,128)(2,1)}), bf16[16,8,768]{2,1,0:T(8,128)(2,1)S(1)}, u32[]{:S(2)}, u32[]{:S(2)}) %all-to-all-start.2) | async-done | bytes 196640 | tf_op jit(solution)/shard_map/all_to_all | solution.py:324
  124.0 0.7 shard_map.154
  (11 shorter events, 0.0 us)
Async XLA Ops:
  2.7 24.9 %copy-start.1 = (bf16[1,128,256]{2,1,0:T(8,128)(2,1)S(1)}, bf16[1,128,256]{2,1,0:T(8,128)(2,1)}, u32[]{:S(2)}) copy-start(bf16[1,128,256]{2,1,0:T(8,128)(2,1)} %param.12) | copy-start | bytes 196612
  2.8 24.9 %copy-start.4 = (bf16[256,128]{1,0:T(8,128)(2,1)S(1)}, bf16[256,128]{1,0:T(8,128)(2,1)}, u32[]{:S(2)}) copy-start(bf16[256,128]{1,0:T(8,128)(2,1)} %router.3) | copy-start | bytes 196612
  2.8 24.9 %copy-start.8 = (s32[1,128,8]{1,2,0:T(8,128)S(1)}, s32[1,128,8]{1,2,0:T(8,128)}, u32[]{:S(2)}) copy-start(s32[1,128,8]{1,2,0:T(8,128)} %param.17) | copy-start | bytes 12292
  2.8 24.9 %copy-start.9 = (f32[256]{0:T(256)S(1)}, f32[256]{0:T(256)}, u32[]{:S(2)}) copy-start(f32[256]{0:T(256)} %param.13) | copy-start | bytes 3076
  4.4 50.8 %copy-start.7 = (bf16[1,128,256]{2,1,0:T(8,128)(2,1)S(1)}, bf16[1,128,256]{2,1,0:T(8,128)(2,1)}, u32[]{:S(2)}) copy-start(bf16[1,128,256]{2,1,0:T(8,128)(2,1)} %param.15) | copy-start | bytes 196612
  4.4 50.8 %copy-start.10 = (f32[1,128]{1,0:T(1,128)S(1)}, f32[1,128]{1,0:T(1,128)}, u32[]{:S(2)}) copy-start(f32[1,128]{1,0:T(1,128)} %scale.3) | copy-start | bytes 1540
  4.4 50.8 %all-to-all-start = ((bf16[64,32,256]{2,1,0:T(8,128)(2,1)}), bf16[64,32,256]{2,1,0:T(8,128)(2,1)S(1)}, u32[]{:S(2)}, u32[]{:S(2)}) async-start(bf16[64,32,256]{2,1,0:T(8,128)(2,1)} %copy.19), calls=%async_computation | async-start | bytes 2097152 | tf_op jit(solution)/shard_map/all_to_all | solution.py:286
  49.9 36.1 %copy-start.2 = (bf16[1,128,512]{2,1,0:T(8,128)(2,1)S(1)}, bf16[1,128,512]{2,1,0:T(8,128)(2,1)}, u32[]{:S(2)}) copy-start(bf16[1,128,512]{2,1,0:T(8,128)(2,1)} %param.21) | copy-start | bytes 393220
  49.9 36.1 %copy-start.3 = (bf16[1,128,512]{2,1,0:T(8,128)(2,1)S(1)}, bf16[1,128,512]{2,1,0:T(8,128)(2,1)}, u32[]{:S(2)}) copy-start(bf16[1,128,512]{2,1,0:T(8,128)(2,1)} %param.22) | copy-start | bytes 393220
  78.5 29.2 %collective-permute-start = (bf16[8,136,256]{2,1,0:T(8,128)(2,1)S(1)}, bf16[8,136,256]{2,1,0:T(8,128)(2,1)S(1)}, u32[]{:S(2)}, u32[]{:S(2)}) collective-permute-start(bf16[8,136,256]{2,1,0:T(8,128)(2,1)S(1)} %all_to_all.15.own), channel_id=1, source_target_pairs={{0,1},{1,0},{2,3},{3,2},{4,5},{5,4},{6,7},{7,6},{8,9},{9,8},{10,11... | collective-permute-start | bytes 1671176 | tf_op jit(solution)/shard_map/ppermute | solution.py:310
  86.0 2.2 %copy-start = (bf16[512,4096]{1,0:T(8,128)(2,1)S(1)}, bf16[512,4096]{1,0:T(8,128)(2,1)}, u32[]{:S(2)}) copy-start(bf16[512,4096]{1,0:T(8,128)(2,1)} %proj.3) | copy-start | bytes 12582916
  104.6 3.1 %copy-start.5 = (bf16[1,128,512]{2,1,0:T(8,128)(2,1)S(1)}, bf16[1,128,512]{2,1,0:T(8,128)(2,1)}, u32[]{:S(2)}) copy-start(bf16[1,128,512]{2,1,0:T(8,128)(2,1)} %param.23) | copy-start | bytes 393220
  107.8 6.1 %copy-start.6 = (f32[128,256]{1,0:T(8,128)S(1)}, f32[128,256]{1,0:T(8,128)}, u32[]{:S(2)}) copy-start(f32[128,256]{1,0:T(8,128)} %get-tuple-element.19.full) | copy-start | bytes 393220
  109.8 14.2 %all-to-all-start.2 = ((bf16[16,8,768]{2,1,0:T(8,128)(2,1)}), bf16[16,8,768]{2,1,0:T(8,128)(2,1)S(1)}, u32[]{:S(2)}, u32[]{:S(2)}) async-start(bf16[16,8,768]{2,1,0:T(8,128)(2,1)} %bitcast.16), calls=%async_computation.2 | async-start | bytes 393216 | tf_op jit(solution)/shard_map/all_to_all | solution.py:324

commit v5 on v4

--- a/solution.py
+++ b/solution.py
@@ -15,10 +15,11 @@
 BF16 = jnp.bfloat16
 TOKENS = 128
 SLOTS = 16
-MAIN = 112
+MAIN = 120
 LEFT = TOKENS - MAIN
-ROWS = MAIN + 8
-TAIL = 136
+ROWS = MAIN + TOPK - 1
+TAIL = 144
+STACK = TOKENS + LEFT
 GRANT = 24 * 2**20
 
 
@@ -74,10 +75,10 @@
     rows = []
     for k in range(TOPK):
         rows.append(jnp.sum(jnp.where(ids[k : k + 1, :] == experts, logits, 0.0), axis=0, keepdims=True))
-    a, b = high_low(jnp.concatenate(rows, axis=0))
-    sent[0:MAIN, :] = xv[0:MAIN]
-    sent[MAIN:ROWS, 0:128] = a
-    sent[MAIN:ROWS, 128:256] = b
+    a, b = high_low(jnp.concatenate([row - rows[0] for row in rows[1:]], axis=0))
+    sent[0, 0:MAIN, :] = xv[0:MAIN]
+    sent[0, MAIN:ROWS, 0:128] = a
+    sent[0, MAIN:ROWS, 128:256] = b
 
 
 def spread(gates, ids):
@@ -96,10 +97,11 @@
 
 
 def weights_kernel(gathered, ids, mix, gates_out):
-    total = jnp.zeros((8, 128), F32)
+    total = jnp.zeros((TOPK - 1, 128), F32)
     for i in range(gathered.shape[0]):
         both = gathered[i, MAIN:ROWS, :].astype(F32)
         total = total + (both[:, 0:128] + both[:, 128:256])
+    total = jnp.concatenate([jnp.zeros((1, 128), F32), total], axis=0)
     top = jnp.max(total, axis=0, keepdims=True)
     e = jnp.exp(total - top)
     gates = e / jnp.sum(e, axis=0, keepdims=True)
@@ -136,8 +138,9 @@
     moved = out_grad[...].astype(F32) + jnp.concatenate([s, s], axis=1) * (gain[...] * grad)
     full[...] = moved
     sent[0:TOKENS, :] = moved.astype(BF16)
+    sent[TOKENS:STACK, :] = x[MAIN:TOKENS, :]
     copies = [
-        pltpu.make_async_copy(sent.at[0:TOKENS], sent_out.at[i, 0:TOKENS], done.at[i]) for i in range(sent_out.shape[0])
+        pltpu.make_async_copy(sent.at[0:STACK], sent_out.at[i, 0:STACK], done.at[i]) for i in range(sent_out.shape[0])
     ]
     copies.append(pltpu.make_async_copy(full, full_out, done.at[len(copies)]))
     for copy in copies:
@@ -151,9 +154,9 @@
     first = jnp.concatenate([a.astype(F32), b.astype(F32)], axis=1)
     second = jnp.concatenate([c.astype(F32), jnp.zeros((8, 128), F32)], axis=1)
     extra = jnp.where(row == 0, first, jnp.where(row == 1, second, 0.0)).astype(BF16)
-    sent[TOKENS:TAIL, :] = extra
+    sent[STACK:TAIL, :] = extra
     for i in range(sent_out.shape[0]):
-        at = pltpu.make_async_copy(sent.at[TOKENS:TAIL], sent_out.at[i, TOKENS:TAIL], done.at[len(copies)])
+        at = pltpu.make_async_copy(sent.at[STACK:TAIL], sent_out.at[i, STACK:TAIL], done.at[len(copies)])
         at.start()
         copies.append(at)
     for copy in copies:
@@ -168,25 +171,24 @@
     return total
 
 
-def stacked(part, left, proj, core):
+def stacked(part, proj, core):
     blocks = [(i, pl.multiple_of(i * 512 + core * 256, 256)) for i in range(part.shape[0])]
-    return contract(
-        lambda i: jnp.concatenate([part[i, 0:TOKENS, :], left[2 * i + core]], axis=0), blocks, proj
-    )
-
-
-def half_kernel(place, own, left, proj, out, held, done):
-    bands = done.shape[0]
-    size = held.shape[0] // bands
+    return contract(lambda i: part[i, 0:STACK, :], blocks, proj)
+
+
+def half_kernel(place, own, proj, out, held, done):
+    pieces, bands = done.shape[0], 2
+    size, wide = held.shape[0] // pieces, held.shape[0] // bands
     copies = [
         pltpu.make_async_copy(proj.at[b * size : (b + 1) * size], held.at[b * size : (b + 1) * size], done.at[b])
-        for b in range(bands)
+        for b in range(pieces)
     ]
     for copy in copies:
         copy.start()
     for b in range(bands):
-        copies[b].wait()
-        out[:, b * size : (b + 1) * size] = stacked(own, left, held.at[b * size : (b + 1) * size], place[0] % 2)
+        for copy in copies[b * pieces // bands : (b + 1) * pieces // bands]:
+            copy.wait()
+        out[:, b * wide : (b + 1) * wide] = stacked(own, held.at[b * wide : (b + 1) * wide], place[0] % 2)
 
 
 def early_kernel(place, gathered, proj, queries, keys, hidden_ctx, probs):
@@ -204,12 +206,12 @@
         probs[:, h * TOKENS : (h + 1) * TOKENS] = e / jnp.sum(e, axis=0, keepdims=True)
 
 
-def attention_kernel(place, own, other, left, half, proj, queries, keys, values, hidden_ctx, probs, scale, width, sent, shift):
+def attention_kernel(place, own, other, half, proj, queries, keys, values, hidden_ctx, probs, scale, width, sent, shift):
     core = place[0] % 2
     row = jnp.zeros((1, 128), F32)
     for part in (own, other):
         for i in range(part.shape[0]):
-            tail = part[i, TOKENS:TAIL, :].astype(F32)
+            tail = part[i, STACK:TAIL, :].astype(F32)
             row = row + ((tail[0:1, 0:128] + tail[0:1, 128:256]) + tail[1:2, 0:128])
     column = jnp.broadcast_to(row * scale[...] / width[0].astype(F32), (TOKENS, TOKENS)).T
     shift[...] = column
@@ -217,7 +219,7 @@
     kv = pl.multiple_of(place[0] // KEY_VALUE_HEADS * HEAD_WIDTH, HEAD_WIDTH)
     key = keys[:, pl.ds(kv, HEAD_WIDTH)]
     value = values[:, pl.ds(kv, HEAD_WIDTH)]
-    both = half[...] + stacked(other, left, proj, 1 - core)
+    both = half[...] + stacked(other, proj, 1 - core)
     ctx = both[0:TOKENS]
     hidden = jnp.concatenate([hidden_ctx[...], both[TOKENS:]], axis=0)
     n = hidden_ctx.shape[1] // HEAD_WIDTH
@@ -285,8 +287,8 @@
     packed = packed.reshape(sequences, held * SLOTS, columns)
     received = lax.all_to_all(packed, "exp", split_axis=0, concat_axis=0, tiled=True)
     received = received.reshape(n_experts * SLOTS, columns)
-    early = call(logits_kernel, shape((ROWS, columns), BF16), x, gain, router_weight, ids)
-    early = lax.all_gather(early, "head")
+    early = call(logits_kernel, shape((1, ROWS, columns), BF16), x, gain, router_weight, ids)
+    early = lax.all_gather(early, "head", tiled=True)
     mix, gate_weights = call(
         weights_kernel, (shape((TOKENS, n_experts * SLOTS), BF16), shape((TOPK, TOKENS))), early, ids,
     )
@@ -306,17 +308,15 @@
         ),
     )
     late_own = lax.all_to_all(late, "head", split_axis=0, concat_axis=0, tiled=True, axis_index_groups=cores)
-    left = lax.all_gather(x[MAIN:TOKENS], "head")
     late_other = lax.ppermute(late_own, "head", swap)
     half, held = call(
-        half_kernel, (shape((TOKENS + LEFT, local)), shape(out_proj.shape, BF16)),
-        place, late_own, left, out_proj,
-        far=(3,), scratch=(pltpu.SemaphoreType.DMA((4,)),),
+        half_kernel, (shape((STACK, local)), shape(out_proj.shape, BF16)), place, late_own, out_proj,
+        far=(2,), scratch=(pltpu.SemaphoreType.DMA((16,)),),
     )
     grads, shift = call(
         attention_kernel,
         (shape((TOKENS, local + 256), BF16), shape((TOKENS, TOKENS))),
-        place, late_own, late_other, left, half, held, query_states[0], rotated_keys[0], value_tensor[0],
+        place, late_own, late_other, half, held, query_states[0], rotated_keys[0], value_tensor[0],
         hidden_ctx, probs, norm_scale, width,
     )
     grad_hidden = call(hidden_kernel, shape((TOKENS, columns), BF16), full, x, shift)

time: 125 us -> 110 us (0.88)
  blocking collectives: 57.7 us -> 43.7 us
    all_gather x2 -> x1, blocking collectives: 36.8 us -> 22.1 us  [per_device(): early = lax.all_gather(early, 'head', tiled=True)]
  transfers between devices with their start and end apart: 3 -> 3, of which waited for: 2 -> 2; matrix products, arithmetic and copies ran while one was open for 0% -> 0% of each run, Pallas kernels for 5% -> 6%
where the time goes in v5:
time: 110 us
  blocking collectives  43.7 us (40%)
  starting transfers between devices  34.1 us (31%)
  waiting for transfers between devices  14.2 us (13%)
  Pallas kernels  11.2 us (10%)
  local copies, waits for them, and re-layouts  4.62 us (4%)
  other arithmetic  1.29 us (1%)
    all_to_all x1, starting transfers between devices, per_device(): lax.all_to_all(packed, 'exp', split_axis=0, concat_axis=0, tiled=True)  23.3 us
    all_gather x1, blocking collectives, per_device(): early = lax.all_gather(early, 'head', tiled=True)  22.1 us
    all_to_all x1, blocking collectives, per_device(): lax.all_to_all(late, 'head', split_axis=0, concat_axis=0, tiled=True, axi...  21.6 us
    pallas_call x8, Pallas kernels, call(): pl.pallas_call(kernel, out_shape=outs, in_specs=specs, out_specs=vm if on...  11.2 us
    all_to_all x1, waiting for transfers between devices, per_device(): lax.all_to_all(grads.reshape(n_head, tokens, local + 256), 'head', split_...  9.5 us
    ppermute x1, starting transfers between devices, per_device(): late_other = lax.ppermute(late_own, 'head', swap)  7.42 us
    all_to_all x1, waiting for transfers between devices, per_device(): lax.all_to_all(packed, 'exp', split_axis=0, concat_axis=0, tiled=True)  4.68 us
    all_to_all x1, starting transfers between devices, per_device(): lax.all_to_all(grads.reshape(n_head, tokens, local + 256), 'head', split_...  3.42 us
  transfers between devices with their start and end apart: 3, of which 2 were waited for; matrix products, arithmetic and copies ran while one was open for 0% of the time, Pallas kernels for 6%

profile of v5, /device:TPU:1, one launch (start us, length us, event | category | flops | bytes accessed | tf_op | source)
XLA Modules:
  0.0 109.9 jit_solution(8304760214681755177)
XLA Ops:
  0.6 0.8 copy.20
  1.4 1.3 %fusion.1 = bf16[64,2,16,256]{3,0,2,1:T(8,128)(2,1)S(1)} fusion(bf16[64,2,1,15]{3,0,2,1:T(8,128)(2,1)S(1)} %copy.20, bf16[64,2,15,256]{3,0,2,1:T(8,128)(2,1)} %bitcast.37), kind=kLoop, calls=%fused_computation.2 | loop fusion | flops 3145728 | bytes 2035456 | tf_op jit(solution)/shard_map/concatenate | solution.py:286
  2.7 0.0 copy-start.1
  2.8 0.0 copy-start.4
  2.8 0.0 copy-start.8
  2.8 0.0 copy-start.9
  2.8 1.6 %copy.19 = bf16[64,32,256]{2,1,0:T(8,128)(2,1)} copy(bf16[64,32,256]{2,0,1:T(8,128)(2,1)S(1)} %bitcast.36) | data formatting | bytes 2097152 | tf_op jit(solution)/shard_map/reshape | solution.py:287
  4.4 23.3 %all-to-all-start = ((bf16[64,32,256]{2,1,0:T(8,128)(2,1)}), bf16[64,32,256]{2,1,0:T(8,128)(2,1)S(1)}, u32[]{:S(2)}, u32[]{:S(2)}) async-start(bf16[64,32,256]{2,1,0:T(8,128)(2,1)} %copy.19), calls=%async_computation | async-start | bytes 2097152 | tf_op jit(solution)/shard_map/all_to_all | solution.py:288
  27.7 0.0 copy-done.1
  27.7 0.0 copy-done.4
  27.7 0.0 copy-done.8
  27.7 0.0 copy-done.9
  27.7 0.3 shard_map.147
  28.0 22.1 %all_gather.3.gathered = bf16[16,127,256]{2,1,0:T(8,128)(2,1)S(1)} all-gather(bf16[1,127,256]{2,1,0:T(8,128)(2,1)S(1)} %shard_map.147), channel_id=1, replica_groups=mesh['exp'=64,'head'=16] {'head'}, dimensions={0}, use_global_device_ids=true | all-gather | bytes 1105408 | tf_op jit(solution)/shard_map/all_gather | solution.py:291
  50.0 0.4 shard_map.148
  50.5 4.7 %all-to-all-done = bf16[64,32,256]{2,1,0:T(8,128)(2,1)S(1)} async-done(((bf16[64,32,256]{2,1,0:T(8,128)(2,1)}), bf16[64,32,256]{2,1,0:T(8,128)(2,1)S(1)}, u32[]{:S(2)}, u32[]{:S(2)}) %all-to-all-start) | async-done | bytes 1048608 | tf_op jit(solution)/shard_map/all_to_all | solution.py:288
  55.1 0.0 copy-done.7
  55.1 2.5 %shard_map.149 = (bf16[8,144,256]{2,1,0:T(8,128)(2,1)}, f32[128,256]{1,0:T(8,128)}) custom-call(bf16[2048,256]{1,0:T(8,128)(2,1)S(1)} %bitcast.21, bf16[128,2048]{1,0:T(8,128)(2,1)S(1)} %get-tuple-element.17.mix, f32[8,128]{1,0:T(8,128)S(1)} %get-tuple-element.18.gates, s32[8,128]{1,0:T(8,128)S(1)} %bitcast.33, bf16[256,128]{1,0:T(8,128)(2,1)S(1)} %copy-done.4, ...), custom_call_target="tpu_custom_call" | custom-call | tf_op jit(solution)/shard_map/pallas_call | solution.py:36
  57.6 21.6 %all_to_all.15.own = bf16[8,144,256]{2,1,0:T(8,128)(2,1)S(1)} all-to-all(bf16[8,144,256]{2,1,0:T(8,128)(2,1)} %get-tuple-element.20), channel_id=1, replica_groups={{0,2,4,6,8,10,12,14},{1,3,5,7,9,11,13,15},{16,18,20,22,24,26,28,30},{17..., dimensions={0} | all-to-all | bytes 1179648 | tf_op jit(solution)/shard_map/all_to_all | solution.py:310
  79.2 7.4 %collective-permute-start = (bf16[8,144,256]{2,1,0:T(8,128)(2,1)S(1)}, bf16[8,144,256]{2,1,0:T(8,128)(2,1)S(1)}, u32[]{:S(2)}, u32[]{:S(2)}) collective-permute-start(bf16[8,144,256]{2,1,0:T(8,128)(2,1)S(1)} %all_to_all.15.own), channel_id=1, source_target_pairs={{0,1},{1,0},{2,3},{3,2},{4,5},{5,4},{6,7},{7,6},{8,9},{9,8},{10,11... | collective-permute-start | bytes 1769480 | tf_op jit(solution)/shard_map/ppermute | solution.py:311
  86.7 0.0 copy-start
  86.7 2.2 %copy-done = bf16[512,4096]{1,0:T(8,128)(2,1)S(1)} copy-done((bf16[512,4096]{1,0:T(8,128)(2,1)S(1)}, bf16[512,4096]{1,0:T(8,128)(2,1)}, u32[]{:S(2)}) %copy-start) | copy-done | bytes 4194328
  88.9 1.6 %shard_map.151 = (f32[120,512]{1,0:T(8,128)S(1)}, f32[128,512]{1,0:T(8,128)S(1)}) custom-call(s32[1]{0:T(128)} %bitcast.10.place, bf16[16,127,256]{2,1,0:T(8,128)(2,1)S(1)} %all_gather.3.gathered, bf16[512,4096]{1,0:T(8,128)(2,1)S(1)} %copy-done, bf16[128,512]{1,0:T(8,128)(2,1)S(1)} %bitcast.25, bf16[128,512]{1,0:T(8,128)(2,1)S(1)} %bitcast.27), custom_call_target="tpu_custom_call" | custom-call | tf_op jit(solution)/shard_map/pallas_call | solution.py:36
  90.5 0.0 copy-start.5
  90.5 3.1 %shard_map.150 = (f32[136,512]{1,0:T(8,128)S(1)}, bf16[512,4096]{1,0:T(8,128)(2,1)S(1)}) custom-call(s32[1]{0:T(128)} %bitcast.10.place, bf16[8,144,256]{2,1,0:T(8,128)(2,1)S(1)} %all_to_all.15.own, bf16[512,4096]{1,0:T(8,128)(2,1)} %proj.3), custom_call_target="tpu_custom_call" | custom-call | tf_op jit(solution)/shard_map/pallas_call | solution.py:36
  93.6 0.0 collective-permute-done.other
  93.7 0.0 copy-start.6
  93.7 2.0 %shard_map.152 = (bf16[128,768]{1,0:T(8,128)(2,1)}, f32[128,128]{1,0:T(8,128)S(1)}) custom-call(s32[1]{0:T(128)} %bitcast.10.place, bf16[8,144,256]{2,1,0:T(8,128)(2,1)S(1)} %all_to_all.15.own, bf16[8,144,256]{2,1,0:T(8,128)(2,1)S(1)} %collective-permute-done.other, f32[136,512]{1,0:T(8,128)S(1)} %get-tuple-element.21.half, ...), custom_call_target="tpu_custom_call" | custom-call | tf_op jit(solution)/shard_map/pallas_call | solution.py:36
  95.7 3.4 %all-to-all-start.2 = ((bf16[16,8,768]{2,1,0:T(8,128)(2,1)}), bf16[16,8,768]{2,1,0:T(8,128)(2,1)S(1)}, u32[]{:S(2)}, u32[]{:S(2)}) async-start(bf16[16,8,768]{2,1,0:T(8,128)(2,1)} %bitcast.15), calls=%async_computation.2 | async-start | bytes 393216 | tf_op jit(solution)/shard_map/all_to_all | solution.py:324
  99.1 0.6 shard_map.153
  99.8 9.5 %all-to-all-done.2.received = bf16[16,8,768]{2,1,0:T(8,128)(2,1)S(1)} async-done(((bf16[16,8,768]{2,1,0:T(8,128)(2,1)}), bf16[16,8,768]{2,1,0:T(8,128)(2,1)S(1)}, u32[]{:S(2)}, u32[]{:S(2)}) %all-to-all-start.2) | async-done | bytes 196640 | tf_op jit(solution)/shard_map/all_to_all | solution.py:324
  109.3 0.7 shard_map.154
  (9 shorter events, 0.0 us)
Async XLA Ops:
  2.7 24.9 %copy-start.1 = (bf16[1,128,256]{2,1,0:T(8,128)(2,1)S(1)}, bf16[1,128,256]{2,1,0:T(8,128)(2,1)}, u32[]{:S(2)}) copy-start(bf16[1,128,256]{2,1,0:T(8,128)(2,1)} %param.12) | copy-start | bytes 196612
  2.8 24.9 %copy-start.4 = (bf16[256,128]{1,0:T(8,128)(2,1)S(1)}, bf16[256,128]{1,0:T(8,128)(2,1)}, u32[]{:S(2)}) copy-start(bf16[256,128]{1,0:T(8,128)(2,1)} %router.3) | copy-start | bytes 196612
  2.8 24.9 %copy-start.8 = (s32[1,128,8]{1,2,0:T(8,128)S(1)}, s32[1,128,8]{1,2,0:T(8,128)}, u32[]{:S(2)}) copy-start(s32[1,128,8]{1,2,0:T(8,128)} %param.17) | copy-start | bytes 12292
  2.8 24.9 %copy-start.9 = (f32[256]{0:T(256)S(1)}, f32[256]{0:T(256)}, u32[]{:S(2)}) copy-start(f32[256]{0:T(256)} %param.13) | copy-start | bytes 3076
  4.4 50.8 %copy-start.7 = (bf16[1,128,256]{2,1,0:T(8,128)(2,1)S(1)}, bf16[1,128,256]{2,1,0:T(8,128)(2,1)}, u32[]{:S(2)}) copy-start(bf16[1,128,256]{2,1,0:T(8,128)(2,1)} %param.15) | copy-start | bytes 196612
  4.4 50.8 %copy-start.10 = (f32[1,128]{1,0:T(1,128)S(1)}, f32[1,128]{1,0:T(1,128)}, u32[]{:S(2)}) copy-start(f32[1,128]{1,0:T(1,128)} %scale.3) | copy-start | bytes 1540
  4.4 50.8 %all-to-all-start = ((bf16[64,32,256]{2,1,0:T(8,128)(2,1)}), bf16[64,32,256]{2,1,0:T(8,128)(2,1)S(1)}, u32[]{:S(2)}, u32[]{:S(2)}) async-start(bf16[64,32,256]{2,1,0:T(8,128)(2,1)} %copy.19), calls=%async_computation | async-start | bytes 2097152 | tf_op jit(solution)/shard_map/all_to_all | solution.py:288
  50.0 36.6 %copy-start.2 = (bf16[1,128,512]{2,1,0:T(8,128)(2,1)S(1)}, bf16[1,128,512]{2,1,0:T(8,128)(2,1)}, u32[]{:S(2)}) copy-start(bf16[1,128,512]{2,1,0:T(8,128)(2,1)} %param.21) | copy-start | bytes 393220
  50.0 36.6 %copy-start.3 = (bf16[1,128,512]{2,1,0:T(8,128)(2,1)S(1)}, bf16[1,128,512]{2,1,0:T(8,128)(2,1)}, u32[]{:S(2)}) copy-start(bf16[1,128,512]{2,1,0:T(8,128)(2,1)} %param.22) | copy-start | bytes 393220
  79.2 14.4 %collective-permute-start = (bf16[8,144,256]{2,1,0:T(8,128)(2,1)S(1)}, bf16[8,144,256]{2,1,0:T(8,128)(2,1)S(1)}, u32[]{:S(2)}, u32[]{:S(2)}) collective-permute-start(bf16[8,144,256]{2,1,0:T(8,128)(2,1)S(1)} %all_to_all.15.own), channel_id=1, source_target_pairs={{0,1},{1,0},{2,3},{3,2},{4,5},{5,4},{6,7},{7,6},{8,9},{9,8},{10,11... | collective-permute-start | bytes 1769480 | tf_op jit(solution)/shard_map/ppermute | solution.py:311
  86.7 2.2 %copy-start = (bf16[512,4096]{1,0:T(8,128)(2,1)S(1)}, bf16[512,4096]{1,0:T(8,128)(2,1)}, u32[]{:S(2)}) copy-start(bf16[512,4096]{1,0:T(8,128)(2,1)} %proj.3) | copy-start | bytes 12582916
  90.5 3.1 %copy-start.5 = (bf16[1,128,512]{2,1,0:T(8,128)(2,1)S(1)}, bf16[1,128,512]{2,1,0:T(8,128)(2,1)}, u32[]{:S(2)}) copy-start(bf16[1,128,512]{2,1,0:T(8,128)(2,1)} %param.23) | copy-start | bytes 393220
  93.7 5.4 %copy-start.6 = (f32[128,256]{1,0:T(8,128)S(1)}, f32[128,256]{1,0:T(8,128)}, u32[]{:S(2)}) copy-start(f32[128,256]{1,0:T(8,128)} %get-tuple-element.19.full) | copy-start | bytes 393220
  95.7 13.6 %all-to-all-start.2 = ((bf16[16,8,768]{2,1,0:T(8,128)(2,1)}), bf16[16,8,768]{2,1,0:T(8,128)(2,1)S(1)}, u32[]{:S(2)}, u32[]{:S(2)}) async-start(bf16[16,8,768]{2,1,0:T(8,128)(2,1)} %bitcast.15), calls=%async_computation.2 | async-start | bytes 393216 | tf_op jit(solution)/shard_map/all_to_all | solution.py:324

commit v6 on v5

--- a/solution.py
+++ b/solution.py
@@ -20,6 +20,7 @@
 ROWS = MAIN + TOPK - 1
 TAIL = 144
 STACK = TOKENS + LEFT
+KEPT = 256
 GRANT = 24 * 2**20
 
 
@@ -96,7 +97,7 @@
     return weight, nn(member.astype(BF16), earlier)
 
 
-def weights_kernel(gathered, ids, mix, gates_out):
+def weights_kernel(gathered, ids, mix):
     total = jnp.zeros((TOPK - 1, 128), F32)
     for i in range(gathered.shape[0]):
         both = gathered[i, MAIN:ROWS, :].astype(F32)
@@ -105,7 +106,6 @@
     top = jnp.max(total, axis=0, keepdims=True)
     e = jnp.exp(total - top)
     gates = e / jnp.sum(e, axis=0, keepdims=True)
-    gates_out[...] = gates
     weight, before = spread(gates, ids)
     step = 8
     for g in range(weight.shape[0] // step):
@@ -114,18 +114,27 @@
         slot = lax.broadcasted_iota(jnp.int32, (step, SLOTS, TOKENS), 1).astype(F32)
         block = jnp.where(jnp.broadcast_to(b3, slot.shape) == slot, jnp.broadcast_to(w3, slot.shape), 0.0)
         block = block.reshape(step * SLOTS, TOKENS).T
-        mix[:, g * step * SLOTS : (g + 1) * step * SLOTS] = block.astype(BF16)
-
-
-def rows_kernel(received, mix, gates, ids, router, x, gain, scale, out_grad, sent_out, full_out, sent, full, done):
-    weight, ranks = spread(gates[...], ids)
+        mix[0:TOKENS, g * step * SLOTS : (g + 1) * step * SLOTS] = block.astype(BF16)
     n = weight.shape[0]
-    rows = received[...]
-    both = nn(mix[...], rows)
     e_of = lax.broadcasted_iota(jnp.int32, (n, n * SLOTS), 0)
     j_of = lax.broadcasted_iota(jnp.int32, (n, n * SLOTS), 1)
-    pick = jnp.where(j_of == e_of * SLOTS + (SLOTS - 1), 1.0, 0.0).astype(BF16)
-    table = nn(pick, received[:, 0:128])
+    mix[TOKENS : TOKENS + n, 0 : n * SLOTS] = jnp.where(j_of == e_of * SLOTS + (SLOTS - 1), 1.0, 0.0).astype(BF16)
+    high, low = high_low(weight)
+    at = n * SLOTS
+    mix[0:n, at : at + 128] = before.astype(BF16)
+    mix[0:n, at + 128 : at + 256] = high
+    mix[n : 2 * n, at : at + 128] = low
+    mix[n : 2 * n, at + 128 : at + 256] = jnp.zeros_like(low)
+
+
+def rows_kernel(received, mix, router, x, gain, scale, out_grad, sent_out, full_out, sent, full, done):
+    n = mix.shape[0] - TOKENS
+    at = n * SLOTS
+    product = nn(mix[:, 0:at], received[...])
+    both = product[0:TOKENS]
+    table = product[TOKENS:, 0:128]
+    ranks = mix[0:n, at : at + 128].astype(F32)
+    weight = mix[0:n, at + 128 : at + 256].astype(F32) + mix[n : 2 * n, at : at + 128].astype(F32)
     slot_grads = jnp.zeros((n, TOKENS), F32)
     for c in range(SLOTS - 1):
         slot_grads = jnp.where(ranks == float(c), table[:, c : c + 1], slot_grads)
@@ -176,19 +185,27 @@
     return contract(lambda i: part[i, 0:STACK, :], blocks, proj)
 
 
-def half_kernel(place, own, proj, out, held, done):
-    pieces, bands = done.shape[0], 2
-    size, wide = held.shape[0] // pieces, held.shape[0] // bands
+def keep_kernel(proj, kept, done):
+    copy = pltpu.make_async_copy(proj.at[0:KEPT], kept, done)
+    copy.start()
+    copy.wait()
+
+
+def half_kernel(place, own, kept, proj, out, held, done):
+    size = held.shape[0] // 2
     copies = [
-        pltpu.make_async_copy(proj.at[b * size : (b + 1) * size], held.at[b * size : (b + 1) * size], done.at[b])
-        for b in range(pieces)
+        pltpu.make_async_copy(
+            proj.at[KEPT + b * size : KEPT + (b + 1) * size], held.at[b * size : (b + 1) * size], done.at[b]
+        )
+        for b in range(2)
     ]
     for copy in copies:
         copy.start()
-    for b in range(bands):
-        for copy in copies[b * pieces // bands : (b + 1) * pieces // bands]:
-            copy.wait()
-        out[:, b * wide : (b + 1) * wide] = stacked(own, held.at[b * wide : (b + 1) * wide], place[0] % 2)
+    core = place[0] % 2
+    out[:, 0:KEPT] = stacked(own, kept, core)
+    for b in range(2):
+        copies[b].wait()
+        out[:, KEPT + b * size : KEPT + (b + 1) * size] = stacked(own, held.at[b * size : (b + 1) * size], core)
 
 
 def early_kernel(place, gathered, proj, queries, keys, hidden_ctx, probs):
@@ -206,7 +223,7 @@
         probs[:, h * TOKENS : (h + 1) * TOKENS] = e / jnp.sum(e, axis=0, keepdims=True)
 
 
-def attention_kernel(place, own, other, half, proj, queries, keys, values, hidden_ctx, probs, scale, width, sent, shift):
+def attention_kernel(place, own, other, half, kept, held, queries, keys, values, hidden_ctx, probs, scale, width, sent_out, shift_out, sent, shift, done):
     core = place[0] % 2
     row = jnp.zeros((1, 128), F32)
     for part in (own, other):
@@ -215,11 +232,14 @@
             row = row + ((tail[0:1, 0:128] + tail[0:1, 128:256]) + tail[1:2, 0:128])
     column = jnp.broadcast_to(row * scale[...] / width[0].astype(F32), (TOKENS, TOKENS)).T
     shift[...] = column
+    copies = [pltpu.make_async_copy(shift, shift_out, done.at[0])]
+    copies[0].start()
     inv_sqrt = 1.0 / math.sqrt(HEAD_WIDTH)
     kv = pl.multiple_of(place[0] // KEY_VALUE_HEADS * HEAD_WIDTH, HEAD_WIDTH)
     key = keys[:, pl.ds(kv, HEAD_WIDTH)]
     value = values[:, pl.ds(kv, HEAD_WIDTH)]
-    both = half[...] + stacked(other, proj, 1 - core)
+    rest = [stacked(other, part, 1 - core) for part in (kept, held)]
+    both = half[...] + jnp.concatenate(rest, axis=1)
     ctx = both[0:TOKENS]
     hidden = jnp.concatenate([hidden_ctx[...], both[TOKENS:]], axis=0)
     n = hidden_ctx.shape[1] // HEAD_WIDTH
@@ -233,8 +253,15 @@
     query_grads = nn(score_grads.T.astype(BF16), key).astype(BF16)
     for h in range(n):
         sent[:, h * 128 : (h + 1) * 128] = query_grads[h * 128 : (h + 1) * 128]
-    sent[:, n * 128 : n * 128 + 128] = nn(score_grads.astype(BF16), stack(queries[...])).astype(BF16)
-    sent[:, n * 128 + 128 : n * 128 + 256] = nn(p.astype(BF16), grads).astype(BF16)
+    edge = n * 128
+    copies.append(pltpu.make_async_copy(sent.at[:, 0:edge], sent_out.at[:, 0:edge], done.at[1]))
+    copies[1].start()
+    sent[:, edge : edge + 128] = nn(score_grads.astype(BF16), stack(queries[...])).astype(BF16)
+    sent[:, edge + 128 : edge + 256] = nn(p.astype(BF16), grads).astype(BF16)
+    copies.append(pltpu.make_async_copy(sent.at[:, edge : edge + 256], sent_out.at[:, edge : edge + 256], done.at[2]))
+    copies[2].start()
+    for copy in copies:
+        copy.wait()
 
 
 def hidden_kernel(full, x, shift, out):
@@ -289,9 +316,7 @@
     received = received.reshape(n_experts * SLOTS, columns)
     early = call(logits_kernel, shape((1, ROWS, columns), BF16), x, gain, router_weight, ids)
     early = lax.all_gather(early, "head", tiled=True)
-    mix, gate_weights = call(
-        weights_kernel, (shape((TOKENS, n_experts * SLOTS), BF16), shape((TOPK, TOKENS))), early, ids,
-    )
+    mix = call(weights_kernel, shape((TOKENS + n_experts, n_experts * SLOTS + 256), BF16), early, ids)
     hidden_ctx, probs = call(
         early_kernel,
         (shape((MAIN, local)), shape((TOKENS, local // HEAD_WIDTH * TOKENS))),
@@ -300,7 +325,7 @@
     late, full = call(
         rows_kernel,
         (pltpu.HBM((n_head // 2, TAIL, columns), BF16), pltpu.HBM((TOKENS, columns), F32)),
-        received, mix, gate_weights, ids, router_weight, x, gain, norm_scale, out_grad[0],
+        received, mix, router_weight, x, gain, norm_scale, out_grad[0],
         far_out=(0, 1),
         scratch=(
             pltpu.VMEM((TAIL, columns), BF16), pltpu.VMEM((TOKENS, columns), F32),
@@ -308,16 +333,26 @@
         ),
     )
     late_own = lax.all_to_all(late, "head", split_axis=0, concat_axis=0, tiled=True, axis_index_groups=cores)
+    kept = call(
+        keep_kernel, shape((KEPT, out_proj.shape[1]), BF16), out_proj,
+        far=(0,), scratch=(pltpu.SemaphoreType.DMA(()),),
+    )
     late_other = lax.ppermute(late_own, "head", swap)
     half, held = call(
-        half_kernel, (shape((STACK, local)), shape(out_proj.shape, BF16)), place, late_own, out_proj,
-        far=(2,), scratch=(pltpu.SemaphoreType.DMA((16,)),),
+        half_kernel, (shape((STACK, local)), shape((local - KEPT, out_proj.shape[1]), BF16)),
+        place, late_own, kept, out_proj,
+        far=(3,), scratch=(pltpu.SemaphoreType.DMA((2,)),),
     )
     grads, shift = call(
         attention_kernel,
-        (shape((TOKENS, local + 256), BF16), shape((TOKENS, TOKENS))),
-        place, late_own, late_other, half, held, query_states[0], rotated_keys[0], value_tensor[0],
+        (pltpu.HBM((TOKENS, local + 256), BF16), pltpu.HBM((TOKENS, TOKENS), F32)),
+        place, late_own, late_other, half, kept, held, query_states[0], rotated_keys[0], value_tensor[0],
         hidden_ctx, probs, norm_scale, width,
+        far_out=(0, 1),
+        scratch=(
+            pltpu.VMEM((TOKENS, local + 256), BF16), pltpu.VMEM((TOKENS, TOKENS), F32),
+            pltpu.SemaphoreType.DMA((3,)),
+        ),
     )
     grad_hidden = call(hidden_kernel, shape((TOKENS, columns), BF16), full, x, shift)
     tokens = TOKENS // n_head

time: 110 us -> 110 us (level)
    pallas_call x8 -> x9, Pallas kernels: 11.2 us -> 11.9 us  [call(): pl.pallas_call(kernel, out_shape=outs, in_specs=specs, out_specs=vm if on...]
    unnamed x23 -> x25, local copies, waits for them, and re-layouts: 3.05 us -> 2.75 us
where the time goes in v6:
time: 110 us; the launch traced here: 109 us
  blocking collectives  43.7 us (40%)
  starting transfers between devices  34 us (31%)
  waiting for transfers between devices  13.2 us (12%)
  Pallas kernels  11.9 us (11%)
  local copies, waits for them, and re-layouts  4.32 us (4%)
  other arithmetic  1.29 us (1%)
    all_to_all x1, starting transfers between devices, per_device(): lax.all_to_all(packed, 'exp', split_axis=0, concat_axis=0, tiled=True)  23.1 us
    all_gather x1, blocking collectives, per_device(): early = lax.all_gather(early, 'head', tiled=True)  22.1 us
    all_to_all x1, blocking collectives, per_device(): lax.all_to_all(late, 'head', split_axis=0, concat_axis=0, tiled=True, axi...  21.6 us
    pallas_call x9, Pallas kernels, call(): pl.pallas_call(kernel, out_shape=outs, in_specs=specs, out_specs=vm if on...  11.9 us
    all_to_all x1, waiting for transfers between devices, per_device(): lax.all_to_all(grads.reshape(n_head, tokens, local + 256), 'head', split_...  8.67 us
    ppermute x1, starting transfers between devices, per_device(): late_other = lax.ppermute(late_own, 'head', swap)  7.42 us
    all_to_all x1, waiting for transfers between devices, per_device(): lax.all_to_all(packed, 'exp', split_axis=0, concat_axis=0, tiled=True)  4.49 us
    all_to_all x1, starting transfers between devices, per_device(): lax.all_to_all(grads.reshape(n_head, tokens, local + 256), 'head', split_...  3.43 us
  transfers between devices with their start and end apart: 3, of which 2 were waited for; matrix products, arithmetic and copies ran while one was open for 0% of the time, Pallas kernels for 6%

profile of v6, /device:TPU:1, one launch (start us, length us, event | category | flops | bytes accessed | tf_op | source)
XLA Modules:
  0.0 109.2 jit_solution(12061447853333050183)
XLA Ops:
  0.6 0.8 copy.20
  1.4 1.3 %fusion.1 = bf16[64,2,16,256]{3,0,2,1:T(8,128)(2,1)S(1)} fusion(bf16[64,2,1,15]{3,0,2,1:T(8,128)(2,1)S(1)} %copy.20, bf16[64,2,15,256]{3,0,2,1:T(8,128)(2,1)} %bitcast.36), kind=kLoop, calls=%fused_computation.2 | loop fusion | flops 3145728 | bytes 2035456 | tf_op jit(solution)/shard_map/concatenate | solution.py:313
  2.7 0.0 copy-start.1
  2.8 0.0 copy-start.4
  2.8 0.0 copy-start.9
  2.8 0.0 copy-start.10
  2.8 1.6 %copy.19 = bf16[64,32,256]{2,1,0:T(8,128)(2,1)} copy(bf16[64,32,256]{2,0,1:T(8,128)(2,1)S(1)} %bitcast.35) | data formatting | bytes 2097152 | tf_op jit(solution)/shard_map/reshape | solution.py:314
  4.4 23.1 %all-to-all-start = ((bf16[64,32,256]{2,1,0:T(8,128)(2,1)}), bf16[64,32,256]{2,1,0:T(8,128)(2,1)S(1)}, u32[]{:S(2)}, u32[]{:S(2)}) async-start(bf16[64,32,256]{2,1,0:T(8,128)(2,1)} %copy.19), calls=%async_computation | async-start | bytes 2097152 | tf_op jit(solution)/shard_map/all_to_all | solution.py:315
  27.5 0.0 copy-start.7
  27.5 0.0 copy-start.11
  27.6 0.3 shard_map.147
  27.9 22.1 %all_gather.3.gathered = bf16[16,127,256]{2,1,0:T(8,128)(2,1)S(1)} all-gather(bf16[1,127,256]{2,1,0:T(8,128)(2,1)S(1)} %shard_map.147), channel_id=1, replica_groups=mesh['exp'=64,'head'=16] {'head'}, dimensions={0}, use_global_device_ids=true | all-gather | bytes 1105408 | tf_op jit(solution)/shard_map/all_gather | solution.py:318
  49.9 0.6 shard_map.148.mix
  50.5 4.5 %all-to-all-done = bf16[64,32,256]{2,1,0:T(8,128)(2,1)S(1)} async-done(((bf16[64,32,256]{2,1,0:T(8,128)(2,1)}), bf16[64,32,256]{2,1,0:T(8,128)(2,1)S(1)}, u32[]{:S(2)}, u32[]{:S(2)}) %all-to-all-start) | async-done | bytes 1048608 | tf_op jit(solution)/shard_map/all_to_all | solution.py:315
  55.0 2.2 %shard_map.149 = (bf16[8,144,256]{2,1,0:T(8,128)(2,1)}, f32[128,256]{1,0:T(8,128)}) custom-call(bf16[2048,256]{1,0:T(8,128)(2,1)S(1)} %bitcast.21, bf16[256,2304]{1,0:T(8,128)(2,1)S(1)} %shard_map.148.mix, bf16[256,128]{1,0:T(8,128)(2,1)S(1)} %copy-done.4, bf16[128,256]{1,0:T(8,128)(2,1)S(1)} %bitcast.23, f32[1,256]{1,0:T(1,128)S(1)} %bitcast.34, ...), custom_call_target="tpu_custom_call" | custom-call | tf_op jit(solution)/shard_map/pallas_call | solution.py:37
  57.2 21.6 %all_to_all.15.own = bf16[8,144,256]{2,1,0:T(8,128)(2,1)S(1)} all-to-all(bf16[8,144,256]{2,1,0:T(8,128)(2,1)} %get-tuple-element.16), channel_id=1, replica_groups={{0,2,4,6,8,10,12,14},{1,3,5,7,9,11,13,15},{16,18,20,22,24,26,28,30},{17..., dimensions={0} | all-to-all | bytes 1179648 | tf_op jit(solution)/shard_map/all_to_all | solution.py:335
  78.8 7.4 %collective-permute-start = (bf16[8,144,256]{2,1,0:T(8,128)(2,1)S(1)}, bf16[8,144,256]{2,1,0:T(8,128)(2,1)S(1)}, u32[]{:S(2)}, u32[]{:S(2)}) collective-permute-start(bf16[8,144,256]{2,1,0:T(8,128)(2,1)S(1)} %all_to_all.15.own), channel_id=1, source_target_pairs={{0,1},{1,0},{2,3},{3,2},{4,5},{5,4},{6,7},{7,6},{8,9},{9,8},{10,11... | collective-permute-start | bytes 1769480 | tf_op jit(solution)/shard_map/ppermute | solution.py:340
  86.2 0.0 copy-start
  86.2 0.0 copy-start.2
  86.3 0.0 copy-start.3
  86.3 1.8 %shard_map.150.kept = bf16[256,4096]{1,0:T(8,128)(2,1)S(1)} custom-call(bf16[512,4096]{1,0:T(8,128)(2,1)} %proj.5), custom_call_target="tpu_custom_call" | custom-call | tf_op jit(solution)/shard_map/pallas_call | solution.py:37
  88.0 1.0 copy-done
  89.1 0.0 copy-done.3
  89.1 1.6 %shard_map.152 = (f32[120,512]{1,0:T(8,128)S(1)}, f32[128,512]{1,0:T(8,128)S(1)}) custom-call(s32[1]{0:T(128)} %bitcast.10.place, bf16[16,127,256]{2,1,0:T(8,128)(2,1)S(1)} %all_gather.3.gathered, bf16[512,4096]{1,0:T(8,128)(2,1)S(1)} %copy-done, bf16[128,512]{1,0:T(8,128)(2,1)S(1)} %bitcast.25, bf16[128,512]{1,0:T(8,128)(2,1)S(1)} %bitcast.27), custom_call_target="tpu_custom_call" | custom-call | tf_op jit(solution)/shard_map/pallas_call | solution.py:37
  90.7 2.2 %shard_map.151 = (f32[136,512]{1,0:T(8,128)S(1)}, bf16[256,4096]{1,0:T(8,128)(2,1)S(1)}) custom-call(s32[1]{0:T(128)} %bitcast.10.place, bf16[8,144,256]{2,1,0:T(8,128)(2,1)S(1)} %all_to_all.15.own, bf16[256,4096]{1,0:T(8,128)(2,1)S(1)} %shard_map.150.kept, bf16[512,4096]{1,0:T(8,128)(2,1)} %proj.5), custom_call_target="tpu_custom_call" | custom-call | tf_op jit(solution)/shard_map/pallas_call | solution.py:37
  92.9 0.0 copy-start.6
  92.9 2.0 %shard_map.153 = (bf16[128,768]{1,0:T(8,128)(2,1)}, f32[128,128]{1,0:T(8,128)}) custom-call(s32[1]{0:T(128)} %bitcast.10.place, bf16[8,144,256]{2,1,0:T(8,128)(2,1)S(1)} %all_to_all.15.own, bf16[8,144,256]{2,1,0:T(8,128)(2,1)S(1)} %collective-permute-done.other, f32[136,512]{1,0:T(8,128)S(1)} %get-tuple-element.17.half, ...), custom_call_target="tpu_custom_call" | custom-call | tf_op jit(solution)/shard_map/pallas_call | solution.py:37
  94.9 3.4 %all-to-all-start.2 = ((bf16[16,8,768]{2,1,0:T(8,128)(2,1)}), bf16[16,8,768]{2,1,0:T(8,128)(2,1)S(1)}, u32[]{:S(2)}, u32[]{:S(2)}) async-start(bf16[16,8,768]{2,1,0:T(8,128)(2,1)} %bitcast.37), calls=%async_computation.2 | async-start | bytes 393216 | tf_op jit(solution)/shard_map/all_to_all | solution.py:359
  98.4 0.8 copy-done.8
  99.2 0.6 shard_map.154
  99.9 8.7 %all-to-all-done.2.received = bf16[16,8,768]{2,1,0:T(8,128)(2,1)S(1)} async-done(((bf16[16,8,768]{2,1,0:T(8,128)(2,1)}), bf16[16,8,768]{2,1,0:T(8,128)(2,1)S(1)}, u32[]{:S(2)}, u32[]{:S(2)}) %all-to-all-start.2) | async-done | bytes 196640 | tf_op jit(solution)/shard_map/all_to_all | solution.py:359
  108.6 0.7 shard_map.155
  (12 shorter events, 0.0 us)
Async XLA Ops:
  2.7 24.8 %copy-start.1 = (bf16[1,128,256]{2,1,0:T(8,128)(2,1)S(1)}, bf16[1,128,256]{2,1,0:T(8,128)(2,1)}, u32[]{:S(2)}) copy-start(bf16[1,128,256]{2,1,0:T(8,128)(2,1)} %param.12) | copy-start | bytes 196612
  2.8 24.8 %copy-start.4 = (bf16[256,128]{1,0:T(8,128)(2,1)S(1)}, bf16[256,128]{1,0:T(8,128)(2,1)}, u32[]{:S(2)}) copy-start(bf16[256,128]{1,0:T(8,128)(2,1)} %router.3) | copy-start | bytes 196612
  2.8 24.8 %copy-start.9 = (s32[1,128,8]{1,2,0:T(8,128)S(1)}, s32[1,128,8]{1,2,0:T(8,128)}, u32[]{:S(2)}) copy-start(s32[1,128,8]{1,2,0:T(8,128)} %param.17) | copy-start | bytes 12292
  2.8 24.8 %copy-start.10 = (f32[256]{0:T(256)S(1)}, f32[256]{0:T(256)}, u32[]{:S(2)}) copy-start(f32[256]{0:T(256)} %param.13) | copy-start | bytes 3076
  4.4 50.6 %all-to-all-start = ((bf16[64,32,256]{2,1,0:T(8,128)(2,1)}), bf16[64,32,256]{2,1,0:T(8,128)(2,1)S(1)}, u32[]{:S(2)}, u32[]{:S(2)}) async-start(bf16[64,32,256]{2,1,0:T(8,128)(2,1)} %copy.19), calls=%async_computation | async-start | bytes 2097152 | tf_op jit(solution)/shard_map/all_to_all | solution.py:315
  27.5 27.5 %copy-start.7 = (bf16[1,128,256]{2,1,0:T(8,128)(2,1)S(1)}, bf16[1,128,256]{2,1,0:T(8,128)(2,1)}, u32[]{:S(2)}) copy-start(bf16[1,128,256]{2,1,0:T(8,128)(2,1)} %param.15) | copy-start | bytes 196612
  27.5 27.5 %copy-start.11 = (f32[1,128]{1,0:T(1,128)S(1)}, f32[1,128]{1,0:T(1,128)}, u32[]{:S(2)}) copy-start(f32[1,128]{1,0:T(1,128)} %scale.3) | copy-start | bytes 1540
  78.8 14.1 %collective-permute-start = (bf16[8,144,256]{2,1,0:T(8,128)(2,1)S(1)}, bf16[8,144,256]{2,1,0:T(8,128)(2,1)S(1)}, u32[]{:S(2)}, u32[]{:S(2)}) collective-permute-start(bf16[8,144,256]{2,1,0:T(8,128)(2,1)S(1)} %all_to_all.15.own), channel_id=1, source_target_pairs={{0,1},{1,0},{2,3},{3,2},{4,5},{5,4},{6,7},{7,6},{8,9},{9,8},{10,11... | collective-permute-start | bytes 1769480 | tf_op jit(solution)/shard_map/ppermute | solution.py:340
  86.2 2.8 %copy-start = (bf16[512,4096]{1,0:T(8,128)(2,1)S(1)}, bf16[512,4096]{1,0:T(8,128)(2,1)}, u32[]{:S(2)}) copy-start(bf16[512,4096]{1,0:T(8,128)(2,1)} %proj.5) | copy-start | bytes 12582916
  86.2 2.8 %copy-start.2 = (bf16[1,128,512]{2,1,0:T(8,128)(2,1)S(1)}, bf16[1,128,512]{2,1,0:T(8,128)(2,1)}, u32[]{:S(2)}) copy-start(bf16[1,128,512]{2,1,0:T(8,128)(2,1)} %param.21) | copy-start | bytes 393220
  86.3 2.8 %copy-start.3 = (bf16[1,128,512]{2,1,0:T(8,128)(2,1)S(1)}, bf16[1,128,512]{2,1,0:T(8,128)(2,1)}, u32[]{:S(2)}) copy-start(bf16[1,128,512]{2,1,0:T(8,128)(2,1)} %param.22) | copy-start | bytes 393220
  90.7 2.2 %copy-start.5 = (bf16[1,128,512]{2,1,0:T(8,128)(2,1)S(1)}, bf16[1,128,512]{2,1,0:T(8,128)(2,1)}, u32[]{:S(2)}) copy-start(bf16[1,128,512]{2,1,0:T(8,128)(2,1)} %param.23) | copy-start | bytes 393220
  92.9 5.5 %copy-start.6 = (f32[128,256]{1,0:T(8,128)S(1)}, f32[128,256]{1,0:T(8,128)}, u32[]{:S(2)}) copy-start(f32[128,256]{1,0:T(8,128)} %get-tuple-element.15.full) | copy-start | bytes 393220
  94.9 13.6 %all-to-all-start.2 = ((bf16[16,8,768]{2,1,0:T(8,128)(2,1)}), bf16[16,8,768]{2,1,0:T(8,128)(2,1)S(1)}, u32[]{:S(2)}, u32[]{:S(2)}) async-start(bf16[16,8,768]{2,1,0:T(8,128)(2,1)} %bitcast.37), calls=%async_computation.2 | async-start | bytes 393216 | tf_op jit(solution)/shard_map/all_to_all | solution.py:359
  98.4 0.8 copy-start.8

commit v7 on v6

--- a/solution.py
+++ b/solution.py
@@ -66,6 +66,25 @@
     rest = v - a.astype(F32)
     b = rest.astype(BF16)
     return a, b, (rest - b.astype(F32)).astype(BF16)
+
+
+def slots_kernel(rows, gates_far, out, gates, done):
+    held, slots, n, columns = out.shape
+    capacity = slots - 1
+    fetch = pltpu.make_async_copy(gates_far, gates, done.at[held])
+    fetch.start()
+    copies = [pltpu.make_async_copy(rows.at[e], out.at[e, 0:capacity], done.at[e]) for e in range(held)]
+    for copy in copies:
+        copy.start()
+    fetch.wait()
+    flat = gates[...].astype(F32)
+    for e in range(held):
+        wide = jnp.concatenate([flat[:, e, :], jnp.zeros((capacity, 128 - n), F32)], axis=1)
+        table = jnp.concatenate([wide, jnp.zeros((128 - capacity, 128), F32)], axis=0).T[0:n]
+        out[e, capacity, :, 0:128] = table.astype(BF16)
+        out[e, capacity, :, 128:columns] = jnp.zeros((n, columns - 128), BF16)
+    for copy in copies:
+        copy.wait()
 
 
 def logits_kernel(x, gain, router, ids, sent):
@@ -309,9 +328,13 @@
     width = jnp.full((1,), out_proj.shape[1], jnp.int32)
 
     local = out_proj.shape[0]
-    gates = jnp.pad(gate_grad.transpose(1, 0, 2)[:, :, None, :], ((0, 0), (0, 0), (0, 0), (0, columns - capacity)))
-    packed = jnp.concatenate([expert_grad.transpose(1, 0, 2, 3), gates], axis=2)
-    packed = packed.reshape(sequences, held * SLOTS, columns)
+    packed = call(
+        slots_kernel, shape((held, SLOTS, sequences, columns), BF16),
+        expert_grad.transpose(0, 2, 1, 3), gate_grad.transpose(2, 0, 1),
+        far=(0, 1),
+        scratch=(pltpu.VMEM((capacity, held, sequences), BF16), pltpu.SemaphoreType.DMA((held + 1,))),
+    )
+    packed = packed.transpose(2, 0, 1, 3).reshape(sequences, held * SLOTS, columns)
     received = lax.all_to_all(packed, "exp", split_axis=0, concat_axis=0, tiled=True)
     received = received.reshape(n_experts * SLOTS, columns)
     early = call(logits_kernel, shape((1, ROWS, columns), BF16), x, gain, router_weight, ids)

time: 110 us -> 109 us (level)
  other arithmetic: 1.29 us -> 0 us
  Pallas kernels: 11.9 us -> 13.1 us
    concatenate x1 -> x0, other arithmetic: 1.29 us -> none  [per_device(): packed = jnp.concatenate([expert_grad.transpose(1, 0, 2, 3), gates], axis=2)]
    pallas_call x9 -> x10, Pallas kernels: 11.9 us -> 13.1 us  [call(): pl.pallas_call(kernel, out_shape=outs, in_specs=specs, out_specs=vm if on...]
    unnamed x25 -> x24, local copies, waits for them, and re-layouts: 2.75 us -> 1.94 us
  transfers between devices with their start and end apart: 3 -> 3, of which waited for: 2 -> 2; matrix products, arithmetic and copies ran while one was open for 0% -> 0% of each run, Pallas kernels for 6% -> 7%
where the time goes in v7:
time: 109 us; the launch traced here: 108 us
  blocking collectives  43.7 us (40%)
  starting transfers between devices  34 us (31%)
  waiting for transfers between devices  13.2 us (12%)
  Pallas kernels  13.1 us (12%)
  local copies, waits for them, and re-layouts  3.51 us (3%)
    all_to_all x1, starting transfers between devices, per_device(): lax.all_to_all(packed, 'exp', split_axis=0, concat_axis=0, tiled=True)  23.1 us
    all_gather x1, blocking collectives, per_device(): early = lax.all_gather(early, 'head', tiled=True)  22.1 us
    all_to_all x1, blocking collectives, per_device(): lax.all_to_all(late, 'head', split_axis=0, concat_axis=0, tiled=True, axi...  21.6 us
    pallas_call x10, Pallas kernels, call(): pl.pallas_call(kernel, out_shape=outs, in_specs=specs, out_specs=vm if on...  13.1 us
    all_to_all x1, waiting for transfers between devices, per_device(): lax.all_to_all(grads.reshape(n_head, tokens, local + 256), 'head', split_...  8.67 us
    ppermute x1, starting transfers between devices, per_device(): late_other = lax.ppermute(late_own, 'head', swap)  7.42 us
    all_to_all x1, waiting for transfers between devices, per_device(): lax.all_to_all(packed, 'exp', split_axis=0, concat_axis=0, tiled=True)  4.49 us
    all_to_all x1, starting transfers between devices, per_device(): lax.all_to_all(grads.reshape(n_head, tokens, local + 256), 'head', split_...  3.43 us
  transfers between devices with their start and end apart: 3, of which 2 were waited for; matrix products, arithmetic and copies ran while one was open for 0% of the time, Pallas kernels for 7%

profile of v7, /device:TPU:1, one launch (start us, length us, event | category | flops | bytes accessed | tf_op | source)
XLA Modules:
  0.0 108.3 jit_solution(2314480702042157444)
XLA Ops:
  0.6 1.2 %shard_map.147 = bf16[2,16,64,256]{3,2,1,0:T(8,128)(2,1)S(1)} custom-call(bf16[2,15,64,256]{3,2,1,0:T(8,128)(2,1)} %bitcast.36, bf16[15,2,64]{2,1,0:T(2,128)(2,1)} %bitcast.39), custom_call_target="tpu_custom_call" | custom-call | tf_op jit(solution)/shard_map/pallas_call | solution.py:37
  1.9 0.0 copy-start.1
  1.9 0.0 copy-start.4
  1.9 0.0 copy-start.9
  1.9 0.0 copy-start.10
  1.9 1.6 %copy.17 = bf16[64,32,256]{2,1,0:T(8,128)(2,1)} copy(bf16[64,32,256]{2,0,1:T(8,128)(2,1)S(1)} %bitcast.22) | data formatting | bytes 2097152 | tf_op jit(solution)/shard_map/reshape | solution.py:337
  3.5 23.1 %all-to-all-start = ((bf16[64,32,256]{2,1,0:T(8,128)(2,1)}), bf16[64,32,256]{2,1,0:T(8,128)(2,1)S(1)}, u32[]{:S(2)}, u32[]{:S(2)}) async-start(bf16[64,32,256]{2,1,0:T(8,128)(2,1)} %copy.17), calls=%async_computation | async-start | bytes 2097152 | tf_op jit(solution)/shard_map/all_to_all | solution.py:338
  26.6 0.0 copy-start.7
  26.6 0.0 copy-start.11
  26.7 0.3 shard_map.148
  27.0 22.1 %all_gather.3.gathered = bf16[16,127,256]{2,1,0:T(8,128)(2,1)S(1)} all-gather(bf16[1,127,256]{2,1,0:T(8,128)(2,1)S(1)} %shard_map.148), channel_id=1, replica_groups=mesh['exp'=64,'head'=16] {'head'}, dimensions={0}, use_global_device_ids=true | all-gather | bytes 1105408 | tf_op jit(solution)/shard_map/all_gather | solution.py:341
  49.1 0.6 shard_map.149.mix
  49.6 4.5 %all-to-all-done = bf16[64,32,256]{2,1,0:T(8,128)(2,1)S(1)} async-done(((bf16[64,32,256]{2,1,0:T(8,128)(2,1)}), bf16[64,32,256]{2,1,0:T(8,128)(2,1)S(1)}, u32[]{:S(2)}, u32[]{:S(2)}) %all-to-all-start) | async-done | bytes 1048608 | tf_op jit(solution)/shard_map/all_to_all | solution.py:338
  54.1 2.2 %shard_map.150 = (bf16[8,144,256]{2,1,0:T(8,128)(2,1)}, f32[128,256]{1,0:T(8,128)}) custom-call(bf16[2048,256]{1,0:T(8,128)(2,1)S(1)} %bitcast.21, bf16[256,2304]{1,0:T(8,128)(2,1)S(1)} %shard_map.149.mix, bf16[256,128]{1,0:T(8,128)(2,1)S(1)} %copy-done.4, bf16[128,256]{1,0:T(8,128)(2,1)S(1)} %bitcast.24, f32[1,256]{1,0:T(1,128)S(1)} %bitcast.35, ...), custom_call_target="tpu_custom_call" | custom-call | tf_op jit(solution)/shard_map/pallas_call | solution.py:37
  56.3 21.6 %all_to_all.15.own = bf16[8,144,256]{2,1,0:T(8,128)(2,1)S(1)} all-to-all(bf16[8,144,256]{2,1,0:T(8,128)(2,1)} %get-tuple-element.16), channel_id=1, replica_groups={{0,2,4,6,8,10,12,14},{1,3,5,7,9,11,13,15},{16,18,20,22,24,26,28,30},{17..., dimensions={0} | all-to-all | bytes 1179648 | tf_op jit(solution)/shard_map/all_to_all | solution.py:358
  77.9 7.4 %collective-permute-start = (bf16[8,144,256]{2,1,0:T(8,128)(2,1)S(1)}, bf16[8,144,256]{2,1,0:T(8,128)(2,1)S(1)}, u32[]{:S(2)}, u32[]{:S(2)}) collective-permute-start(bf16[8,144,256]{2,1,0:T(8,128)(2,1)S(1)} %all_to_all.15.own), channel_id=1, source_target_pairs={{0,1},{1,0},{2,3},{3,2},{4,5},{5,4},{6,7},{7,6},{8,9},{9,8},{10,11... | collective-permute-start | bytes 1769480 | tf_op jit(solution)/shard_map/ppermute | solution.py:363
  85.3 0.0 copy-start
  85.4 0.0 copy-start.2
  85.4 0.0 copy-start.3
  85.4 1.8 %shard_map.151.kept = bf16[256,4096]{1,0:T(8,128)(2,1)S(1)} custom-call(bf16[512,4096]{1,0:T(8,128)(2,1)} %proj.5), custom_call_target="tpu_custom_call" | custom-call | tf_op jit(solution)/shard_map/pallas_call | solution.py:37
  87.1 1.0 copy-done
  88.2 0.0 copy-done.3
  88.2 1.6 %shard_map.153 = (f32[120,512]{1,0:T(8,128)S(1)}, f32[128,512]{1,0:T(8,128)S(1)}) custom-call(s32[1]{0:T(128)} %bitcast.10.place, bf16[16,127,256]{2,1,0:T(8,128)(2,1)S(1)} %all_gather.3.gathered, bf16[512,4096]{1,0:T(8,128)(2,1)S(1)} %copy-done, bf16[128,512]{1,0:T(8,128)(2,1)S(1)} %bitcast.26, bf16[128,512]{1,0:T(8,128)(2,1)S(1)} %bitcast.28), custom_call_target="tpu_custom_call" | custom-call | tf_op jit(solution)/shard_map/pallas_call | solution.py:37
  89.8 0.0 copy-start.5
  89.8 2.2 %shard_map.152 = (f32[136,512]{1,0:T(8,128)S(1)}, bf16[256,4096]{1,0:T(8,128)(2,1)S(1)}) custom-call(s32[1]{0:T(128)} %bitcast.10.place, bf16[8,144,256]{2,1,0:T(8,128)(2,1)S(1)} %all_to_all.15.own, bf16[256,4096]{1,0:T(8,128)(2,1)S(1)} %shard_map.151.kept, bf16[512,4096]{1,0:T(8,128)(2,1)} %proj.5), custom_call_target="tpu_custom_call" | custom-call | tf_op jit(solution)/shard_map/pallas_call | solution.py:37
  92.0 2.0 %shard_map.154 = (bf16[128,768]{1,0:T(8,128)(2,1)}, f32[128,128]{1,0:T(8,128)}) custom-call(s32[1]{0:T(128)} %bitcast.10.place, bf16[8,144,256]{2,1,0:T(8,128)(2,1)S(1)} %all_to_all.15.own, bf16[8,144,256]{2,1,0:T(8,128)(2,1)S(1)} %collective-permute-done.other, f32[136,512]{1,0:T(8,128)S(1)} %get-tuple-element.17.half, ...), custom_call_target="tpu_custom_call" | custom-call | tf_op jit(solution)/shard_map/pallas_call | solution.py:37
  94.1 3.4 %all-to-all-start.2 = ((bf16[16,8,768]{2,1,0:T(8,128)(2,1)}), bf16[16,8,768]{2,1,0:T(8,128)(2,1)S(1)}, u32[]{:S(2)}, u32[]{:S(2)}) async-start(bf16[16,8,768]{2,1,0:T(8,128)(2,1)} %bitcast.37), calls=%async_computation.2 | async-start | bytes 393216 | tf_op jit(solution)/shard_map/all_to_all | solution.py:382
  97.5 0.0 copy-start.8
  97.5 0.8 copy-done.8
  98.3 0.6 shard_map.155
  99.0 8.7 %all-to-all-done.2.received = bf16[16,8,768]{2,1,0:T(8,128)(2,1)S(1)} async-done(((bf16[16,8,768]{2,1,0:T(8,128)(2,1)}), bf16[16,8,768]{2,1,0:T(8,128)(2,1)S(1)}, u32[]{:S(2)}, u32[]{:S(2)}) %all-to-all-start.2) | async-done | bytes 196640 | tf_op jit(solution)/shard_map/all_to_all | solution.py:382
  107.7 0.7 shard_map.156
  (11 shorter events, 0.0 us)
Async XLA Ops:
  1.9 24.8 %copy-start.1 = (bf16[1,128,256]{2,1,0:T(8,128)(2,1)S(1)}, bf16[1,128,256]{2,1,0:T(8,128)(2,1)}, u32[]{:S(2)}) copy-start(bf16[1,128,256]{2,1,0:T(8,128)(2,1)} %param.12) | copy-start | bytes 196612
  1.9 24.8 %copy-start.4 = (bf16[256,128]{1,0:T(8,128)(2,1)S(1)}, bf16[256,128]{1,0:T(8,128)(2,1)}, u32[]{:S(2)}) copy-start(bf16[256,128]{1,0:T(8,128)(2,1)} %router.3) | copy-start | bytes 196612
  1.9 24.8 %copy-start.9 = (s32[1,128,8]{1,2,0:T(8,128)S(1)}, s32[1,128,8]{1,2,0:T(8,128)}, u32[]{:S(2)}) copy-start(s32[1,128,8]{1,2,0:T(8,128)} %param.17) | copy-start | bytes 12292
  1.9 24.8 %copy-start.10 = (f32[256]{0:T(256)S(1)}, f32[256]{0:T(256)}, u32[]{:S(2)}) copy-start(f32[256]{0:T(256)} %param.13) | copy-start | bytes 3076
  3.5 50.6 %all-to-all-start = ((bf16[64,32,256]{2,1,0:T(8,128)(2,1)}), bf16[64,32,256]{2,1,0:T(8,128)(2,1)S(1)}, u32[]{:S(2)}, u32[]{:S(2)}) async-start(bf16[64,32,256]{2,1,0:T(8,128)(2,1)} %copy.17), calls=%async_computation | async-start | bytes 2097152 | tf_op jit(solution)/shard_map/all_to_all | solution.py:338
  26.6 27.5 %copy-start.7 = (bf16[1,128,256]{2,1,0:T(8,128)(2,1)S(1)}, bf16[1,128,256]{2,1,0:T(8,128)(2,1)}, u32[]{:S(2)}) copy-start(bf16[1,128,256]{2,1,0:T(8,128)(2,1)} %param.15) | copy-start | bytes 196612
  26.6 27.5 %copy-start.11 = (f32[1,128]{1,0:T(1,128)S(1)}, f32[1,128]{1,0:T(1,128)}, u32[]{:S(2)}) copy-start(f32[1,128]{1,0:T(1,128)} %scale.3) | copy-start | bytes 1540
  77.9 14.1 %collective-permute-start = (bf16[8,144,256]{2,1,0:T(8,128)(2,1)S(1)}, bf16[8,144,256]{2,1,0:T(8,128)(2,1)S(1)}, u32[]{:S(2)}, u32[]{:S(2)}) collective-permute-start(bf16[8,144,256]{2,1,0:T(8,128)(2,1)S(1)} %all_to_all.15.own), channel_id=1, source_target_pairs={{0,1},{1,0},{2,3},{3,2},{4,5},{5,4},{6,7},{7,6},{8,9},{9,8},{10,11... | collective-permute-start | bytes 1769480 | tf_op jit(solution)/shard_map/ppermute | solution.py:363
  85.3 2.8 %copy-start = (bf16[512,4096]{1,0:T(8,128)(2,1)S(1)}, bf16[512,4096]{1,0:T(8,128)(2,1)}, u32[]{:S(2)}) copy-start(bf16[512,4096]{1,0:T(8,128)(2,1)} %proj.5) | copy-start | bytes 12582916
  85.4 2.8 %copy-start.2 = (bf16[1,128,512]{2,1,0:T(8,128)(2,1)S(1)}, bf16[1,128,512]{2,1,0:T(8,128)(2,1)}, u32[]{:S(2)}) copy-start(bf16[1,128,512]{2,1,0:T(8,128)(2,1)} %param.21) | copy-start | bytes 393220
  85.4 2.8 %copy-start.3 = (bf16[1,128,512]{2,1,0:T(8,128)(2,1)S(1)}, bf16[1,128,512]{2,1,0:T(8,128)(2,1)}, u32[]{:S(2)}) copy-start(bf16[1,128,512]{2,1,0:T(8,128)(2,1)} %param.22) | copy-start | bytes 393220
  89.8 2.2 %copy-start.5 = (bf16[1,128,512]{2,1,0:T(8,128)(2,1)S(1)}, bf16[1,128,512]{2,1,0:T(8,128)(2,1)}, u32[]{:S(2)}) copy-start(bf16[1,128,512]{2,1,0:T(8,128)(2,1)} %param.23) | copy-start | bytes 393220
  92.0 5.5 %copy-start.6 = (f32[128,256]{1,0:T(8,128)S(1)}, f32[128,256]{1,0:T(8,128)}, u32[]{:S(2)}) copy-start(f32[128,256]{1,0:T(8,128)} %get-tuple-element.15.full) | copy-start | bytes 393220
  94.1 13.6 %all-to-all-start.2 = ((bf16[16,8,768]{2,1,0:T(8,128)(2,1)}), bf16[16,8,768]{2,1,0:T(8,128)(2,1)S(1)}, u32[]{:S(2)}, u32[]{:S(2)}) async-start(bf16[16,8,768]{2,1,0:T(8,128)(2,1)} %bitcast.37), calls=%async_computation.2 | async-start | bytes 393216 | tf_op jit(solution)/shard_map/all_to_all | solution.py:382
  97.5 0.8 copy-start.8
